TPU v7x, 16 devices: a whole 2x2x2 slice. The times are simulated.
16 devices in a mesh: fsdp: 16 (over z, y, x, core).
Axes of the slice: x: 2, y: 2, z: 2, core: 2. Of those that a mesh axis runs over, the one named last changes fastest.
Arguments:
- token_ids: int32 [2, 64, 64], P(None, 'fsdp')
- labels: int32 [2, 64, 64], P(None, 'fsdp')
- emb_table: bfloat16 [32128, 768], P('fsdp')
- w_gate: bfloat16 [768, 2048], P('fsdp')
- w_up: bfloat16 [768, 2048], P('fsdp')
- w_down: bfloat16 [2048, 768], P('fsdp')
- gain_in: float32 [768], replicated
- gain_out: float32 [768], replicated
Outputs:
- output 1: float32 [], replicated
- output 2: float32 [32128, 768], P('fsdp')
- output 3: float32 [768, 2048], P('fsdp')
- output 4: float32 [768, 2048], P('fsdp')
- output 5: float32 [2048, 768], P('fsdp')
All inputs are finite; a program needn't handle non-finite values.
Results may differ from a plain program's by a relative error of at most 0.0126113.
Values are sent between devices in bfloat16 or wider.
A program may use at most 1 GiB of HBM per device.

v0:
```python
import jax
import jax.numpy as jnp
from jax import lax
from jax.sharding import PartitionSpec as P

NORM_EPS = 1e-6


def rms_scale(values, gain_vec):
    vals32 = values.astype(jnp.float32)
    inv_rms = lax.rsqrt(jnp.mean(vals32 * vals32, axis=-1, keepdims=True) + NORM_EPS)
    return (vals32 * inv_rms * gain_vec).astype(jnp.bfloat16), inv_rms


def rms_back(values, inv_rms, gain_vec, grad_out):
    vals32 = values.astype(jnp.float32)
    scaled = grad_out * gain_vec
    proj_mean = jnp.mean(scaled * vals32, axis=-1, keepdims=True)
    return inv_rms * scaled - vals32 * (inv_rms * inv_rms * inv_rms) * proj_mean


def mlp_forward(emb_rows, gain_in, gain_out, w_gate, w_up, w_down):
    normed_in, inv_in = rms_scale(emb_rows, gain_in)
    gate_pre = jnp.dot(normed_in, w_gate, preferred_element_type=jnp.float32).astype(jnp.bfloat16)
    up_proj = jnp.dot(normed_in, w_up, preferred_element_type=jnp.float32).astype(jnp.bfloat16)
    acts = (jax.nn.silu(gate_pre.astype(jnp.float32)) * up_proj.astype(jnp.float32)).astype(jnp.bfloat16)
    mlp_out = jnp.dot(acts, w_down, preferred_element_type=jnp.float32).astype(jnp.bfloat16)
    hidden = (emb_rows.astype(jnp.float32) + mlp_out.astype(jnp.float32)).astype(jnp.bfloat16)
    normed_out, inv_out = rms_scale(hidden, gain_out)
    return normed_out, (emb_rows, normed_in, inv_in, gate_pre, up_proj, acts, hidden, inv_out)


def mlp_backward(saved, grad_normed, gain_in, gain_out, w_gate, w_up, w_down):
    emb_rows, normed_in, inv_in, gate_pre, up_proj, acts, hidden, inv_out = saved
    rows_dims = (((0,), (0,)), ((), ()))
    cols_dims = (((1,), (1,)), ((), ()))
    grad_hidden = rms_back(hidden, inv_out, gain_out, grad_normed)
    grad_mid = grad_hidden.astype(jnp.bfloat16)
    grad_down = lax.dot_general(acts, grad_mid, rows_dims, preferred_element_type=jnp.float32)
    grad_acts = lax.dot_general(grad_mid, w_down, cols_dims, preferred_element_type=jnp.float32)
    gate32 = gate_pre.astype(jnp.float32)
    gate_sig = jax.nn.sigmoid(gate32)
    grad_gate_pre = (grad_acts * up_proj.astype(jnp.float32) * gate_sig * (1.0 + gate32 * (1.0 - gate_sig))).astype(jnp.bfloat16)
    grad_up_proj = (grad_acts * gate32 * gate_sig).astype(jnp.bfloat16)
    grad_gate = lax.dot_general(normed_in, grad_gate_pre, rows_dims, preferred_element_type=jnp.float32)
    grad_up = lax.dot_general(normed_in, grad_up_proj, rows_dims, preferred_element_type=jnp.float32)
    grad_normed_in = (lax.dot_general(grad_gate_pre, w_gate, cols_dims, preferred_element_type=jnp.float32)
                      + lax.dot_general(grad_up_proj, w_up, cols_dims, preferred_element_type=jnp.float32))
    grad_rows = grad_hidden + rms_back(emb_rows, inv_in, gain_in, grad_normed_in)
    return grad_rows, grad_gate, grad_up, grad_down


def head_block(full_table, normed_blk, lab_blk):
    logits = lax.dot_general(normed_blk, full_table, (((1,), (1,)), ((), ())), preferred_element_type=jnp.float32)
    row_max = jnp.max(logits, axis=-1, keepdims=True)
    exp_shift = jnp.exp(logits - row_max)
    exp_total = jnp.sum(exp_shift, axis=-1, keepdims=True)
    is_label = jnp.arange(full_table.shape[0], dtype=jnp.int32)[None, :] == lab_blk[:, None]
    lab_logit = jnp.sum(jnp.where(is_label, logits, 0.0), axis=-1)
    loss_part = jnp.sum(row_max[:, 0] + jnp.log(exp_total[:, 0]) - lab_logit)
    grad_logits = (exp_shift / exp_total - is_label.astype(jnp.float32)).astype(jnp.bfloat16)
    grad_normed = jnp.dot(grad_logits, full_table, preferred_element_type=jnp.float32)
    grad_table = lax.dot_general(grad_logits, normed_blk, (((0,), (0,)), ((), ())), preferred_element_type=jnp.float32)
    return loss_part, grad_normed, grad_table


def head_pass(full_table, normed_out, lab_flat, block_len):
    block_count = normed_out.shape[0] // block_len

    def head_step(acc_pair, block_pair):
        loss_acc, table_acc = acc_pair
        loss_part, grad_normed, grad_table = head_block(full_table, block_pair[0], block_pair[1])
        return (loss_acc + loss_part, table_acc + grad_table), grad_normed

    start_acc = (jnp.zeros((), jnp.float32), jnp.zeros(full_table.shape, jnp.float32))
    blocks = (normed_out.reshape(block_count, block_len, normed_out.shape[1]), lab_flat.reshape(block_count, block_len))
    (loss_sum, grad_table), grad_normed = lax.scan(head_step, start_acc, blocks)
    return loss_sum, grad_table, grad_normed.reshape(normed_out.shape)


def solution(mesh):
    groups = mesh.shape['fsdp']

    def device_step(token_ids, labels, table_shard, gate_shard, up_shard, down_shard, gain_in, gain_out):
        micro_count = token_ids.shape[0]
        tok_dev = token_ids.shape[1] * token_ids.shape[2]
        total_tokens = micro_count * tok_dev * groups
        block_len = min(256, tok_dev)
        loss_total = jnp.zeros((), jnp.float32)
        shard_accs = [jnp.zeros(param_shard.shape, jnp.float32) for param_shard in (table_shard, gate_shard, up_shard, down_shard)]
        for micro_idx in range(micro_count):
            full_table = lax.all_gather(table_shard, 'fsdp', axis=0, tiled=True)
            w_gate = lax.all_gather(gate_shard, 'fsdp', axis=0, tiled=True)
            w_up = lax.all_gather(up_shard, 'fsdp', axis=0, tiled=True)
            w_down = lax.all_gather(down_shard, 'fsdp', axis=0, tiled=True)
            ids_flat = token_ids[micro_idx].reshape(tok_dev)
            lab_flat = labels[micro_idx].reshape(tok_dev)
            emb_rows = jnp.take(full_table, ids_flat, axis=0)
            normed_out, saved = mlp_forward(emb_rows, gain_in, gain_out, w_gate, w_up, w_down)
            loss_sum, grad_table, grad_normed = head_pass(full_table, normed_out, lab_flat, block_len)
            grad_rows, grad_gate, grad_up, grad_down = mlp_backward(saved, grad_normed, gain_in, gain_out, w_gate, w_up, w_down)
            grad_table = grad_table.at[ids_flat].add(grad_rows)
            full_grads = (grad_table, grad_gate, grad_up, grad_down)
            shard_accs = [acc_shard + lax.psum_scatter(full_grad, 'fsdp', scatter_dimension=0, tiled=True) for acc_shard, full_grad in zip(shard_accs, full_grads)]
            loss_total = loss_total + lax.psum(loss_sum, 'fsdp')
        return (loss_total / total_tokens, shard_accs[0], shard_accs[1], shard_accs[2], shard_accs[3])

    row_spec = P('fsdp', None)
    tok_spec = P(None, 'fsdp', None)
    return jax.shard_map(device_step, mesh=mesh,
                         in_specs=(tok_spec, tok_spec, row_spec, row_spec, row_spec, row_spec, P(), P()),
                         out_specs=(P(), row_spec, row_spec, row_spec, row_spec), check_vma=False)
```

profile of v0, /device:TPU:0, one launch (start us, length us, event | category | flops | bytes accessed | tf_op | source)
XLA Modules:
  0.0 1242.8 jit_solution(9701342367514945259)
XLA Ops:
  10.5 185.5 %all-gather.5.cloned.1.call-done = bf16[32128,768]{1,0:T(8,128)(2,1)} async-done(((bf16[2008,768]{1,0:T(8,128)(2,1)}), bf16[32128,768]{1,0:T(8,128)(2,1)}) %all-gather.5.cloned.1.call-update) | async-done | bytes 49348624 | tf_op jit(solution)/shard_map/all_gather | solution.py:92
  203.5 26.3 %all-gather.7.cloned.1.call-done = bf16[768,2048]{1,0:T(8,128)(2,1)} async-done(((bf16[48,2048]{1,0:T(8,128)(2,1)}), bf16[768,2048]{1,0:T(8,128)(2,1)}) %all-gather.7.cloned.1.call-update) | async-done | bytes 3145744 | tf_op jit(solution)/shard_map/all_gather | solution.py:93
  232.8 30.8 %all-gather.9.cloned.1.call-done = bf16[768,2048]{1,0:T(8,128)(2,1)} async-done(((bf16[48,2048]{1,0:T(8,128)(2,1)}), bf16[768,2048]{1,0:T(8,128)(2,1)}) %all-gather.9.cloned.1.call-update) | async-done | bytes 3145744 | tf_op jit(solution)/shard_map/all_gather | solution.py:94
  263.6 3.9 convolution_convert_fusion.2
  267.5 29.7 %all-gather.11.cloned.1.call-done = bf16[2048,768]{1,0:T(8,128)(2,1)} async-done(((bf16[128,768]{1,0:T(8,128)(2,1)}), bf16[2048,768]{1,0:T(8,128)(2,1)}) %all-gather.11.cloned.1.call-update) | async-done | bytes 3145744 | tf_op jit(solution)/shard_map/all_gather | solution.py:95
  307.3 32.7 %fusion.86 = (f32[256]{0:T(256)S(1)}, f32[256,32128]{1,0:T(8,128)}) fusion(bf16[32128,768]{1,0:T(8,128)(2,1)} %all-gather.5.cloned.1.call-done, bf16[256,768]{1,0:T(8,128)(2,1)S(1)} %get-tuple-element.69, f32[256]{0:T(256)S(1)} %get-tuple-element.59, f32[768]{0:T(1024)S(1)} %copy-done.10), kind=kOutput, calls=%fused_computation.145 | convolution fusion | flops 12642254848 | bytes 82646016 | tf_op jit(solution)/shard_map/while/body/eval_jaxpr/dot_general | solution.py:54
  340.0 17.8 %fusion.1 = (f32[256]{0:T(256)S(1)}, f32[256]{0:T(256)}) fusion(f32[256,32128]{1,0:T(8,128)} %get-tuple-element.71, f32[256]{0:T(256)S(1)} %get-tuple-element.70, s32[256]{0:T(256)S(1)} %eq.49), kind=kLoop, calls=%fused_computation.13 | loop fusion | flops 41123328 | bytes 32903168 | tf_op jit(solution)/shard_map/while/body/eval_jaxpr/reduce_sum | solution.py:57
  360.0 10.9 subtract_convert_fusion
  370.8 25.9 %fusion.39 = (f32[256]{0:T(256)S(1)}, f32[256,768]{1,0:T(8,128)S(1)}) fusion(bf16[256,768]{1,0:T(8,128)(2,1)S(1)} %get-tuple-element.69, f32[768]{0:T(1024)S(1)} %copy-done.10, bf16[256,32128]{1,0:T(8,128)(2,1)} %subtract_convert_fusion, bf16[32128,768]{1,0:T(8,128)(2,1)} %all-gather.5.cloned.1.call-done), kind=kOutput, calls=%fused_computation.94 | convolution fusion | flops 12634030080 | bytes 66981888 | tf_op jit(solution)/shard_map/while/body/eval_jaxpr/dot_general | solution.py:62
  396.8 32.5 %fusion.85 = (f32[256]{0:T(256)S(1)}, f32[256,32128]{1,0:T(8,128)}) fusion(bf16[32128,768]{1,0:T(8,128)(2,1)} %all-gather.5.cloned.1.call-done, bf16[256,768]{1,0:T(8,128)(2,1)S(1)} %get-tuple-element.65, f32[768]{0:T(1024)S(1)} %copy-done.10, f32[256]{0:T(256)S(1)} %get-tuple-element.63), kind=kOutput, calls=%fused_computation.144 | convolution fusion | flops 12642254848 | bytes 82646016 | tf_op jit(solution)/shard_map/while/body/eval_jaxpr/dot_general | solution.py:54
  429.3 17.8 %fusion = (f32[256]{0:T(256)S(1)}, f32[256]{0:T(256)}) fusion(f32[256,32128]{1,0:T(8,128)} %get-tuple-element.67, f32[256]{0:T(256)S(1)} %get-tuple-element.66, s32[256]{0:T(256)S(1)} %eq.45), kind=kLoop, calls=%fused_computation.12 | loop fusion | flops 41123328 | bytes 32903168 | tf_op jit(solution)/shard_map/while/body/eval_jaxpr/reduce_sum | solution.py:57
  449.2 21.2 %subtract_convert_fusion.1 = bf16[256,32128]{1,0:T(8,128)(2,1)} fusion(f32[256,32128]{1,0:T(8,128)S(1)} %copy-done.1, f32[256]{0:T(256)S(1)} %get-tuple-element.43, s32[256]{0:T(256)S(1)} %eq.45, f32[256]{0:T(256)S(1)} %get-tuple-element.66), kind=kLoop, calls=%fused_computation.5 | loop fusion | flops 49348608 | bytes 49351680 | tf_op jit(solution)/shard_map/while/body/eval_jaxpr/convert_element_type | solution.py:61
  470.4 25.9 %fusion.33 = (f32[256]{0:T(256)S(1)}, f32[256,768]{1,0:T(8,128)S(1)}) fusion(bf16[256,768]{1,0:T(8,128)(2,1)S(1)} %get-tuple-element.65, f32[768]{0:T(1024)S(1)} %copy-done.10, bf16[256,32128]{1,0:T(8,128)(2,1)} %subtract_convert_fusion.1, bf16[32128,768]{1,0:T(8,128)(2,1)} %all-gather.5.cloned.1.call-done), kind=kOutput, calls=%fused_computation.88 | convolution fusion | flops 12634030080 | bytes 66981888 | tf_op jit(solution)/shard_map/while/body/eval_jaxpr/dot_general | solution.py:62
  496.5 5.2 fusion.5
  508.7 3.9 convolution_add_fusion.1
  516.3 4.3 convolution_add_fusion
  524.0 3.8 convolution_add_fusion.2
  528.0 42.6 %fusion.56 = f32[32128,768]{1,0:T(8,128)} fusion(bf16[256,32128]{1,0:T(8,128)(2,1)} %subtract_convert_fusion, bf16[256,768]{1,0:T(8,128)(2,1)S(1)} %get-tuple-element.69, f32[256]{0:T(256)S(1)} %get-tuple-element.59, f32[768]{0:T(1024)S(1)} %copy-done.10), kind=kOutput, calls=%fused_computation.113 | convolution fusion | flops 12634030080 | bytes 115544064 | tf_op jit(solution)/shard_map/while/body/eval_jaxpr/dot_general | solution.py:63
  576.3 33.0 %scatter_fusion.1 = f32[32128,768]{1,0:T(8,128)} fusion(f32[32128,768]{1,0:T(8,128)} %fusion.56, s32[256]{0:T(256)S(1)} %bitcast.27, f32[256,768]{1,0:T(8,128)S(1)} %fusion.52), kind=kCustom, calls=%fused_computation.3 | custom fusion | flops 196608 | bytes 2360320 | tf_op jit(solution)/shard_map/scatter-add | solution.py:102
  615.9 42.6 %fusion.60 = f32[32128,768]{1,0:T(8,128)} fusion(bf16[256,32128]{1,0:T(8,128)(2,1)} %subtract_convert_fusion.1, bf16[256,768]{1,0:T(8,128)(2,1)S(1)} %get-tuple-element.65, f32[768]{0:T(1024)S(1)} %copy-done.10, f32[256]{0:T(256)S(1)} %get-tuple-element.63), kind=kOutput, calls=%fused_computation.115 | convolution fusion | flops 12634030080 | bytes 115544064 | tf_op jit(solution)/shard_map/while/body/eval_jaxpr/dot_general | solution.py:63
  658.5 33.0 %scatter_fusion = f32[32128,768]{1,0:T(8,128)} fusion(f32[32128,768]{1,0:T(8,128)} %fusion.60, s32[256]{0:T(256)S(1)} %bitcast.26, f32[256,768]{1,0:T(8,128)S(1)} %fusion.45), kind=kCustom, calls=%fused_computation.2 | custom fusion | flops 196608 | bytes 2360320 | tf_op jit(solution)/shard_map/scatter-add | solution.py:102
  691.5 94.9 %add.187 = f32[32128,768]{1,0:T(8,128)} add(f32[32128,768]{1,0:T(8,128)} %scatter_fusion, f32[32128,768]{1,0:T(8,128)} %scatter_fusion.1) | non-fusion elementwise | flops 24674304 | bytes 296091648 | tf_op jit(solution)/shard_map/add | solution.py:104
  789.1 31.9 %psum.16 = f32[]{:T(128)} all-reduce(f32[]{:T(128)S(6)} %add.172), channel_id=1, replica_groups=mesh['fsdp'=16] {'fsdp'}, use_global_device_ids=true, to_apply=%region_6.8 | all-reduce | flops 1 | bytes 8 | tf_op jit(solution)/shard_map/psum | solution.py:105
  821.7 412.7 %reduce-scatter.13.cloned.1.call-done = f32[2008,768]{1,0:T(8,128)} async-done(((f32[32128,768]{1,0:T(8,128)}), f32[2008,768]{1,0:T(8,128)}) %reduce-scatter.13.cloned.1.call-update) | async-done | bytes 6168592
  (179 shorter events, 55.4 us)
Async XLA Ops:
  7.2 188.8 %all-gather.5.cloned.1.call-start = ((), (), s32[]{:S(2)}) async-start(), calls=%async_computation.4 | async-start | bytes 52432896 | tf_op jit(solution)/shard_map/all_gather | solution.py:92
  7.9 221.9 %all-gather.7.cloned.1.call-start = ((), (), s32[]{:S(2)}) async-start(), calls=%async_computation.5 | async-start | bytes 3342336 | tf_op jit(solution)/shard_map/all_gather | solution.py:93
  8.7 254.9 %all-gather.9.cloned.1.call-start = ((), (), s32[]{:S(2)}) async-start(), calls=%async_computation.6 | async-start | bytes 3342336 | tf_op jit(solution)/shard_map/all_gather | solution.py:94
  9.4 287.8 %all-gather.11.cloned.1.call-start = ((), (), s32[]{:S(2)}) async-start(), calls=%async_computation.7 | async-start | bytes 3342336 | tf_op jit(solution)/shard_map/all_gather | solution.py:95
  10.0 811.7 %reduce-scatter.9.cloned.1.call-start = ((), (), s32[]{:S(2)}) async-start(), calls=%async_computation.9 | async-start | bytes 6684672 | tf_op jit(solution)/shard_map/reduce_scatter | solution.py:104
  10.0 186.0 %copy-start.20 = (s32[1,4,64]{2,1,0:T(4,128)}, s32[1,4,64]{2,1,0:T(4,128)S(1)}, u32[]{:S(2)}) copy-start(s32[1,4,64]{2,1,0:T(4,128)S(1)} %get-tuple-element.48) | copy-start | bytes 3076
  10.1 185.9 %copy-start.22 = (s32[1,4,64]{2,1,0:T(4,128)}, s32[1,4,64]{2,1,0:T(4,128)S(1)}, u32[]{:S(2)}) copy-start(s32[1,4,64]{2,1,0:T(4,128)S(1)} %get-tuple-element.47) | copy-start | bytes 3076
  10.5 293.6 %copy-start.39 = (pred[256]{0:T(512)(128)(4,1)}, pred[256]{0:T(512)(128)(4,1)S(1)}, u32[]{:S(2)}) copy-start(pred[256]{0:T(512)(128)(4,1)S(1)} %compare_and_fusion) | copy-start | bytes 772
  10.5 286.8 %copy-start.37 = (pred[256]{0:T(512)(128)(4,1)}, pred[256]{0:T(512)(128)(4,1)S(1)}, u32[]{:S(2)}) copy-start(pred[256]{0:T(512)(128)(4,1)S(1)} %compare_and_fusion.1) | copy-start | bytes 772
  10.5 219.3 %copy-start.18 = (f32[768]{0:T(1024)S(1)}, f32[768]{0:T(1024)}, u32[]{:S(2)}) copy-start(f32[768]{0:T(1024)} %param.16) | copy-start | bytes 9220
  198.9 105.2 %copy-start.2 = (bf16[256,768]{1,0:T(8,128)(2,1)}, bf16[256,768]{1,0:T(8,128)(2,1)S(1)}, u32[]{:S(2)}) copy-start(bf16[256,768]{1,0:T(8,128)(2,1)S(1)} %gather_fusion.1) | copy-start | bytes 1179652
  201.8 95.5 %copy-start.4 = (bf16[256,768]{1,0:T(8,128)(2,1)}, bf16[256,768]{1,0:T(8,128)(2,1)S(1)}, u32[]{:S(2)}) copy-start(bf16[256,768]{1,0:T(8,128)(2,1)S(1)} %gather_fusion) | copy-start | bytes 1179652
  202.9 99.8 %copy-start.30 = (f32[256]{0:T(256)}, f32[256]{0:T(256)S(1)}, u32[]{:S(2)}) copy-start(f32[256]{0:T(256)S(1)} %get-tuple-element.57) | copy-start | bytes 3076
  203.5 64.0 %copy-start.28 = (f32[256]{0:T(256)}, f32[256]{0:T(256)S(1)}, u32[]{:S(2)}) copy-start(f32[256]{0:T(256)S(1)} %get-tuple-element.61) | copy-start | bytes 3076
  232.8 68.3 %copy-start.54 = (bf16[256,2048]{1,0:T(8,128)(2,1)}, bf16[256,2048]{1,0:T(8,128)(2,1)S(1)}, u32[]{:S(2)}) copy-start(bf16[256,2048]{1,0:T(8,128)(2,1)S(1)} %convolution_convert_fusion.3) | copy-start | bytes 3145732
  340.0 17.8 %copy-start.24 = (f32[256]{0:T(256)}, f32[256]{0:T(256)S(1)}, u32[]{:S(2)}) copy-start(f32[256]{0:T(256)S(1)} %get-tuple-element.70) | copy-start | bytes 3076
  340.0 19.9 %copy-start = (f32[256,32128]{1,0:T(8,128)S(1)}, f32[256,32128]{1,0:T(8,128)}, u32[]{:S(2)}) copy-start(f32[256,32128]{1,0:T(8,128)} %get-tuple-element.71) | copy-start | bytes 98697216
  429.3 19.9 %copy-start.1 = (f32[256,32128]{1,0:T(8,128)S(1)}, f32[256,32128]{1,0:T(8,128)}, u32[]{:S(2)}) copy-start(f32[256,32128]{1,0:T(8,128)} %get-tuple-element.67) | copy-start | bytes 98697216
  447.1 23.3 %copy-start.34 = (f32[256]{0:T(256)}, f32[256]{0:T(256)S(1)}, u32[]{:S(2)}) copy-start(f32[256]{0:T(256)S(1)} %get-tuple-element.43) | copy-start | bytes 3076
  470.4 26.0 %copy-start.43 = (f32[256]{0:T(256)S(1)}, f32[256]{0:T(256)}, u32[]{:S(2)}) copy-start(f32[256]{0:T(256)} %get-tuple-element.62) | copy-start | bytes 3076
  512.7 309.0 %reduce-scatter.11.cloned.1.call-start = ((), (), s32[]{:S(2)}) async-start(), calls=%async_computation.10 | async-start | bytes 6684672 | tf_op jit(solution)/shard_map/reduce_scatter | solution.py:104
  520.7 301.0 %reduce-scatter.7.cloned.1.call-start = ((), (), s32[]{:S(2)}) async-start(), calls=%async_computation.8 | async-start | bytes 6684672 | tf_op jit(solution)/shard_map/reduce_scatter | solution.py:104
  527.8 706.6 %reduce-scatter.13.cloned.1.call-start = ((), (), s32[]{:S(2)}) async-start(), calls=%async_computation.11 | async-start | bytes 104865792
  576.3 33.1 %copy-start.11 = (bf16[256,2048]{1,0:T(8,128)(2,1)S(1)}, bf16[256,2048]{1,0:T(8,128)(2,1)}, u32[]{:S(2)}) copy-start(bf16[256,2048]{1,0:T(8,128)(2,1)} %get-tuple-element.74) | copy-start | bytes 3145732
  (42 other events, 140.1 us)
Sparse Core Ops, SparseCore 0:
  10.2 185.7 all-gather.4
  198.2 31.5 all-gather.6
  232.1 31.5 all-gather.8
  265.7 31.5 all-gather.10
  512.8 67.3 reduce-scatter.8
  585.0 67.3 reduce-scatter.10
  657.3 67.3 reduce-scatter.6
  786.6 447.7 reduce-scatter.12
where the time goes:
time: 1250 us; the launch traced here: 1240 us
  waiting for transfers between devices  688 us (55%)
  matrix products  254 us (20%)
  other arithmetic  233 us (19%)
  blocking collectives  31.9 us (3%)
  between operations  18.2 us (1%)
  local copies, waits for them, and re-layouts  16.9 us (1%)
    unnamed x9, waiting for transfers between devices  415 us
    all_gather x1, waiting for transfers between devices, device_step(): full_table = lax.all_gather(table_shard, 'fsdp', axis=0, tiled=True)  185 us
    add x1, other arithmetic, device_step(): acc_shard + lax.psum_scatter(full_grad, 'fsdp', scatter_dimension=0, tile...  94.9 us
    dot_general x2, matrix products, head_block(): lax.dot_general(grad_logits, normed_blk, (((0,), (0,)), ((), ())), prefer...  85.2 us
    scatter-add x2, other arithmetic, device_step(): grad_table = grad_table.at[ids_flat].add(grad_rows)  66.1 us
    dot_general x2, matrix products, head_block(): lax.dot_general(normed_blk, full_table, (((1,), (1,)), ((), ())), preferr...  65.3 us
    dot_general x2, matrix products, head_block(): jnp.dot(grad_logits, full_table, preferred_element_type=jnp.float32)  51.9 us
    reduce_sum x2, other arithmetic, head_block(): exp_total = jnp.sum(exp_shift, axis=-1, keepdims=True)  35.7 us
  transfers between devices with their start and end apart: 8, of which 5 were waited for; matrix products, arithmetic and copies ran while one was open for 23% of the time, Pallas kernels for 0%

commit v1 on v0

v1 whole, which is shorter than its diff:
```python
import functools
import jax
import jax.numpy as jnp
from jax import lax
from jax.experimental import pallas as pl
from jax.experimental.pallas import tpu as pltpu
from jax.sharding import PartitionSpec as P

NORM_EPS = 1e-6
SLOTS = 64
TOK_BLOCK = 256
VMEM_LIMIT = 60 * 1024 * 1024


def rms_scale(values, gain_vec):
    vals32 = values.astype(jnp.float32)
    inv_rms = lax.rsqrt(jnp.mean(vals32 * vals32, axis=-1, keepdims=True) + NORM_EPS)
    return (vals32 * inv_rms * gain_vec).astype(jnp.bfloat16), inv_rms


def rms_back(values, inv_rms, gain_vec, grad_out):
    vals32 = values.astype(jnp.float32)
    scaled = grad_out * gain_vec
    proj_mean = jnp.mean(scaled * vals32, axis=-1, keepdims=True)
    return inv_rms * scaled - vals32 * (inv_rms * inv_rms * inv_rms) * proj_mean


def mlp_forward(emb_rows, gain_in, gain_out, w_gate, w_up, w_down):
    normed_in, inv_in = rms_scale(emb_rows, gain_in)
    gate_pre = jnp.dot(normed_in, w_gate, preferred_element_type=jnp.float32).astype(jnp.bfloat16)
    up_proj = jnp.dot(normed_in, w_up, preferred_element_type=jnp.float32).astype(jnp.bfloat16)
    acts = (jax.nn.silu(gate_pre.astype(jnp.float32)) * up_proj.astype(jnp.float32)).astype(jnp.bfloat16)
    mlp_out = jnp.dot(acts, w_down, preferred_element_type=jnp.float32).astype(jnp.bfloat16)
    hidden = (emb_rows.astype(jnp.float32) + mlp_out.astype(jnp.float32)).astype(jnp.bfloat16)
    normed_out, inv_out = rms_scale(hidden, gain_out)
    return normed_out, (emb_rows, normed_in, inv_in, gate_pre, up_proj, acts, hidden, inv_out)


COLS_DIMS = (((1,), (1,)), ((), ()))
ROWS_DIMS = (((0,), (0,)), ((), ()))


def mlp_backward(saved, grad_normed, gain_in, gain_out, w_gate, w_up, w_down):
    emb_rows, normed_in, inv_in, gate_pre, up_proj, acts, hidden, inv_out = saved
    grad_hidden = rms_back(hidden, inv_out, gain_out, grad_normed)
    grad_mid = grad_hidden.astype(jnp.bfloat16)
    grad_acts = lax.dot_general(grad_mid, w_down, COLS_DIMS, preferred_element_type=jnp.float32)
    gate32 = gate_pre.astype(jnp.float32)
    gate_sig = jax.nn.sigmoid(gate32)
    grad_gate_pre = (grad_acts * up_proj.astype(jnp.float32) * gate_sig * (1.0 + gate32 * (1.0 - gate_sig))).astype(jnp.bfloat16)
    grad_up_proj = (grad_acts * gate32 * gate_sig).astype(jnp.bfloat16)
    grad_normed_in = (lax.dot_general(grad_gate_pre, w_gate, COLS_DIMS, preferred_element_type=jnp.float32)
                      + lax.dot_general(grad_up_proj, w_up, COLS_DIMS, preferred_element_type=jnp.float32))
    grad_rows = grad_hidden + rms_back(emb_rows, inv_in, gain_in, grad_normed_in)
    return grad_rows, grad_mid, grad_gate_pre, grad_up_proj


def stats_kernel(base_ref, z_ref, table_ref, lab_ref, logits_ref, stats_ref):
    logits = lax.dot_general(table_ref[...], z_ref[...], COLS_DIMS, preferred_element_type=jnp.float32)
    logits_ref[0] = logits
    col_max = jnp.max(logits, axis=0, keepdims=True)
    exp_sum = jnp.sum(jnp.exp(logits - col_max), axis=0, keepdims=True)
    row_ids = lax.broadcasted_iota(jnp.int32, logits.shape, 0)
    is_label = row_ids == (lab_ref[...] - base_ref[0])
    lab_logit = jnp.sum(jnp.where(is_label, logits, 0.0), axis=0, keepdims=True)
    stats_ref[...] = jnp.concatenate([col_max, exp_sum, lab_logit], axis=0)


def head_stats(base, z_all, table_shard, lab_row):
    tokens, dim = z_all.shape
    rows = table_shard.shape[0]
    blocks = tokens // TOK_BLOCK
    return pl.pallas_call(
        stats_kernel,
        grid=(blocks,),
        in_specs=[pl.BlockSpec(memory_space=pltpu.SMEM),
                  pl.BlockSpec((TOK_BLOCK, dim), lambda i: (i, 0)),
                  pl.BlockSpec((rows, dim), lambda i: (0, 0)),
                  pl.BlockSpec((1, TOK_BLOCK), lambda i: (0, i))],
        out_specs=[pl.BlockSpec((1, rows, TOK_BLOCK), lambda i: (i, 0, 0)),
                   pl.BlockSpec((3, TOK_BLOCK), lambda i: (0, i))],
        out_shape=[jax.ShapeDtypeStruct((blocks, rows, TOK_BLOCK), jnp.float32),
                   jax.ShapeDtypeStruct((3, tokens), jnp.float32)],
        compiler_params=pltpu.CompilerParams(vmem_limit_bytes=VMEM_LIMIT, dimension_semantics=("arbitrary",)),
        cost_estimate=pl.CostEstimate(flops=2 * tokens * rows * dim, bytes_accessed=tokens * rows * 4, transcendentals=tokens * rows),
        name="head_stats",
    )(base, z_all, table_shard, lab_row)


def grad_kernel(base_ref, logits_ref, z_ref, table_ref, lab_ref, norm_ref, init_ref, dz_ref, dtable_ref):
    logits = logits_ref[0]
    norm = norm_ref[...]
    row_ids = lax.broadcasted_iota(jnp.int32, logits.shape, 0)
    is_label = row_ids == (lab_ref[...] - base_ref[0])
    probs = jnp.exp(logits - norm[0:1]) * norm[1:2]
    grad_logits = (probs - is_label.astype(jnp.float32)).astype(jnp.bfloat16)
    dz_ref[...] = lax.dot_general(grad_logits, table_ref[...], ROWS_DIMS, preferred_element_type=jnp.float32)
    step_grad = jnp.dot(grad_logits, z_ref[...], preferred_element_type=jnp.float32)

    @pl.when(pl.program_id(0) == 0)
    def _():
        dtable_ref[...] = init_ref[...] + step_grad

    @pl.when(pl.program_id(0) > 0)
    def _():
        dtable_ref[...] += step_grad


def head_grad(base, logits, z_all, table_shard, lab_row, norm, init):
    tokens, dim = z_all.shape
    rows = table_shard.shape[0]
    blocks = tokens // TOK_BLOCK
    return pl.pallas_call(
        grad_kernel,
        grid=(blocks,),
        in_specs=[pl.BlockSpec(memory_space=pltpu.SMEM),
                  pl.BlockSpec((1, rows, TOK_BLOCK), lambda i: (i, 0, 0)),
                  pl.BlockSpec((TOK_BLOCK, dim), lambda i: (i, 0)),
                  pl.BlockSpec((rows, dim), lambda i: (0, 0)),
                  pl.BlockSpec((1, TOK_BLOCK), lambda i: (0, i)),
                  pl.BlockSpec((2, TOK_BLOCK), lambda i: (0, i)),
                  pl.BlockSpec((rows, dim), lambda i: (0, 0))],
        out_specs=[pl.BlockSpec((TOK_BLOCK, dim), lambda i: (i, 0)),
                   pl.BlockSpec((rows, dim), lambda i: (0, 0))],
        out_shape=[jax.ShapeDtypeStruct((tokens, dim), jnp.float32),
                   jax.ShapeDtypeStruct((rows, dim), jnp.float32)],
        compiler_params=pltpu.CompilerParams(vmem_limit_bytes=VMEM_LIMIT, dimension_semantics=("arbitrary",)),
        cost_estimate=pl.CostEstimate(flops=4 * tokens * rows * dim, bytes_accessed=tokens * rows * 4, transcendentals=tokens * rows),
        name="head_grad",
    )(base, logits, z_all, table_shard, lab_row, norm, init)


def split3(values):
    high = lax.reduce_precision(values, 8, 7)
    rest = values - high
    mid = lax.reduce_precision(rest, 8, 7)
    low = rest - mid
    return [part.astype(jnp.bfloat16) for part in (high, mid, low)]


def pick_rows(select, values):
    total = None
    for part in split3(values):
        term = jnp.dot(select, part, preferred_element_type=jnp.float32)
        total = term if total is None else total + term
    return total


def solution(mesh):
    groups = mesh.shape['fsdp']

    def device_step(token_ids, labels, table_shard, gate_shard, up_shard, down_shard, gain_in, gain_out):
        micro_count = token_ids.shape[0]
        tok_micro = token_ids.shape[1] * token_ids.shape[2]
        tok_dev = micro_count * tok_micro
        total_tokens = tok_dev * groups
        rows, dim = table_shard.shape
        me = lax.axis_index('fsdp')
        base = (me * rows).astype(jnp.int32)
        base_arr = base.reshape(1)

        packed = jnp.stack([token_ids.reshape(tok_dev), labels.reshape(tok_dev)])
        packed_all = lax.all_gather(packed, 'fsdp', axis=0, tiled=False)
        ids_all = packed_all[:, 0]
        lab_all = packed_all[:, 1].reshape(groups, micro_count, tok_micro)

        gate_rows, ffn = gate_shard.shape
        down_rows = down_shard.shape[0]
        w_all = lax.all_gather(jnp.concatenate([gate_shard, up_shard, down_shard.reshape(gate_rows, ffn)], axis=0), 'fsdp', axis=0, tiled=False)
        w_gate = w_all[:, :gate_rows].reshape(groups * gate_rows, ffn)
        w_up = w_all[:, gate_rows:2 * gate_rows].reshape(groups * gate_rows, ffn)
        w_down = w_all[:, 2 * gate_rows:].reshape(groups, down_rows, dim).reshape(groups * down_rows, dim)

        owner = ids_all // rows
        local = ids_all - owner * rows
        owner_hot = owner[:, :, None] == jnp.arange(groups, dtype=jnp.int32)
        tri = jnp.tril(jnp.ones((tok_dev, tok_dev), jnp.bfloat16), -1)
        before = jnp.einsum('tu,suo->sto', tri, owner_hot.astype(jnp.bfloat16), preferred_element_type=jnp.float32)
        rank = jnp.sum(jnp.where(owner_hot, before, 0.0), axis=-1).astype(jnp.int32)
        rounds = jnp.max(rank) // SLOTS + 1
        my_owner = lax.dynamic_index_in_dim(owner, me, 0, keepdims=False)
        my_rank = lax.dynamic_index_in_dim(rank, me, 0, keepdims=False)
        owned = owner == me
        slot_ids = jnp.arange(SLOTS, dtype=jnp.int32)

        def owned_rows(round_idx):
            hit = owned[:, None, :] & (rank[:, None, :] == slot_ids[None, :, None] + round_idx * SLOTS)
            return (jnp.sum(jnp.where(hit, local[:, None, :] + 1, 0), axis=-1) - 1).reshape(groups * SLOTS)

        def my_slots(round_idx):
            off = my_rank - round_idx * SLOTS
            return jnp.where((off >= 0) & (off < SLOTS), my_owner * SLOTS + off, -1)

        def fetch_round(round_idx):
            row_idx = owned_rows(round_idx)
            select = (row_idx[:, None] == jnp.arange(rows, dtype=jnp.int32)[None, :]).astype(jnp.bfloat16)
            send = jnp.dot(select, table_shard, preferred_element_type=jnp.float32).astype(jnp.bfloat16)
            got = lax.all_to_all(send.reshape(groups, SLOTS, dim), 'fsdp', 0, 0).reshape(groups * SLOTS, dim)
            place = (my_slots(round_idx)[:, None] == jnp.arange(groups * SLOTS, dtype=jnp.int32)[None, :]).astype(jnp.bfloat16)
            return jnp.dot(place, got, preferred_element_type=jnp.float32).astype(jnp.bfloat16)

        def return_round(round_idx, grad_rows):
            place = (jnp.arange(groups * SLOTS, dtype=jnp.int32)[:, None] == my_slots(round_idx)[None, :]).astype(jnp.bfloat16)
            send = pick_rows(place, grad_rows)
            got = lax.all_to_all(send.reshape(groups, SLOTS, dim), 'fsdp', 0, 0).reshape(groups * SLOTS, dim)
            select = (jnp.arange(rows, dtype=jnp.int32)[:, None] == owned_rows(round_idx)[None, :]).astype(jnp.bfloat16)
            return pick_rows(select, got)

        emb_rows = fetch_round(jnp.int32(0))
        emb_rows = lax.fori_loop(1, rounds, lambda r, acc: acc + fetch_round(r), emb_rows)

        normed, saved = [], []
        for m in range(micro_count):
            out, kept = mlp_forward(emb_rows[m * tok_micro:(m + 1) * tok_micro], gain_in, gain_out, w_gate, w_up, w_down)
            normed.append(out)
            saved.append(kept)

        lab_rows = [lab_all[:, m].reshape(1, groups * tok_micro) for m in range(micro_count)]
        z_all = [lax.all_gather(normed[m], 'fsdp', axis=0, tiled=True) for m in range(micro_count)]
        dtable = jnp.zeros((rows, dim), jnp.float32)
        loss_total = jnp.zeros((), jnp.float32)
        firsts = [head_stats(base_arr, z_all[m], table_shard, lab_rows[m]) for m in range(micro_count)]
        grad_normed = []
        for m in range(micro_count):
            logits, stats = firsts[m]
            stats_all = lax.all_gather(stats, 'fsdp', axis=0, tiled=False)
            top = jnp.max(stats_all[:, 0], axis=0)
            exp_total = jnp.sum(stats_all[:, 1] * jnp.exp(stats_all[:, 0] - top[None]), axis=0)
            loss_total = loss_total + jnp.sum(top + jnp.log(exp_total) - jnp.sum(stats_all[:, 2], axis=0))
            norm = jnp.stack([top, 1.0 / exp_total])
            dz, dtable = head_grad(base_arr, logits, z_all[m], table_shard, lab_rows[m], norm, dtable)
            grad_normed.append(lax.psum_scatter(dz, 'fsdp', scatter_dimension=0, tiled=True))

        backs = [mlp_backward(saved[m], grad_normed[m], gain_in, gain_out, w_gate, w_up, w_down) for m in range(micro_count)]
        grad_rows, grad_mid, grad_gate_pre, grad_up_proj = [jnp.concatenate(parts, axis=0) for parts in zip(*backs)]
        normed_in = jnp.concatenate([kept[1] for kept in saved], axis=0)
        acts = jnp.concatenate([kept[5] for kept in saved], axis=0)
        grad_down = lax.dot_general(acts, grad_mid, ROWS_DIMS, preferred_element_type=jnp.float32)
        grad_gate = lax.dot_general(normed_in, grad_gate_pre, ROWS_DIMS, preferred_element_type=jnp.float32)
        grad_up = lax.dot_general(normed_in, grad_up_proj, ROWS_DIMS, preferred_element_type=jnp.float32)
        w_grads = jnp.concatenate([grad_gate.reshape(groups, gate_rows, ffn), grad_up.reshape(groups, gate_rows, ffn),
                                   grad_down.reshape(groups, down_rows, dim).reshape(groups, gate_rows, ffn)], axis=1)
        w_grad = lax.psum_scatter(w_grads, 'fsdp', scatter_dimension=0, tiled=False)

        dtable = dtable + return_round(jnp.int32(0), grad_rows)
        dtable = lax.fori_loop(1, rounds, lambda r, acc: acc + return_round(r, grad_rows), dtable)
        return (loss_total / total_tokens, dtable, w_grad[:gate_rows], w_grad[gate_rows:2 * gate_rows],
                w_grad[2 * gate_rows:].reshape(down_rows, dim))

    row_spec = P('fsdp', None)
    tok_spec = P(None, 'fsdp', None)
    return jax.shard_map(device_step, mesh=mesh,
                         in_specs=(tok_spec, tok_spec, row_spec, row_spec, row_spec, row_spec, P(), P()),
                         out_specs=(P(), row_spec, row_spec, row_spec, row_spec), check_vma=False)
```

time: 1250 us -> 622 us (0.50)
  waiting for transfers between devices: 688 us -> 261 us
  other arithmetic: 233 us -> 25.9 us
  matrix products: 254 us -> 62 us
  Pallas kernels: 0 us -> 151 us
  blocking collectives: 31.9 us -> 50.6 us
  local copies, waits for them, and re-layouts: 16.9 us -> 34.5 us
    unnamed x9 -> x6, waiting for transfers between devices: 415 us -> 0.77 us
    all_gather x4 -> x3, waiting for transfers between devices: 272 us -> 46.5 us  [the longest x2 37.4 us: device_step(): lax.all_gather(normed[m], 'fsdp', axis=0, tiled=True)]
    dot_general x18, matrix products: 240 us -> 51.3 us  [the longest x6 18.6 us: pick_rows(): term = jnp.dot(select, part, preferred_element_type=jnp.float32)]
    pallas_call x0 -> x4, Pallas kernels: none -> 151 us  [the longest x2 95 us: head_grad(): pl.pallas_call(grad_kernel, grid=(blocks,), in_specs=[pl.BlockSpec(memory...]
    reduce_scatter x3, waiting for transfers between devices: 0.06 us -> 134 us  [the longest x2 92.2 us: device_step(): lax.psum_scatter(dz, 'fsdp', scatter_dimension=0, tiled=True)]
    add x1, other arithmetic: 94.9 us -> 0.01 us  [device_step(): tri = jnp.tril(jnp.ones((tok_dev, tok_dev), jnp.bfloat16), -1)]
    all_to_all x0 -> x2, waiting for transfers between devices: none -> 79.6 us  [the longest x1 54.1 us: return_round(): lax.all_to_all(send.reshape(groups, SLOTS, dim), 'fsdp', 0, 0)]
    scatter-add x2 -> x0, other arithmetic: 66.1 us -> none  [device_step(): grad_table = grad_table.at[ids_flat].add(grad_rows)]
  transfers between devices with their start and end apart: 8 -> 8, of which waited for: 5 -> 6; matrix products, arithmetic and copies ran while one was open for 23% -> 9% of each run, Pallas kernels for 0% -> 25%
where the time goes in v1:
time: 622 us; the launch traced here: 614 us
  waiting for transfers between devices  261 us (42%)
  Pallas kernels  151 us (24%)
  matrix products  62 us (10%)
  blocking collectives  50.6 us (8%)
  local copies, waits for them, and re-layouts  34.5 us (6%)
  other arithmetic  25.9 us (4%)
  between operations  20.2 us (3%)
  starting transfers between devices  6.81 us (1%)
    pallas_call x2, Pallas kernels, head_grad(): pl.pallas_call(grad_kernel, grid=(blocks,), in_specs=[pl.BlockSpec(memory...  95 us
    reduce_scatter x2, waiting for transfers between devices, device_step(): lax.psum_scatter(dz, 'fsdp', scatter_dimension=0, tiled=True)  92.2 us
    pallas_call x2, Pallas kernels, head_stats(): pl.pallas_call(stats_kernel, grid=(blocks,), in_specs=[pl.BlockSpec(memor...  56.4 us
    all_to_all x1, waiting for transfers between devices, return_round(): lax.all_to_all(send.reshape(groups, SLOTS, dim), 'fsdp', 0, 0)  54.1 us
    reduce_scatter x1, waiting for transfers between devices, device_step(): w_grad = lax.psum_scatter(w_grads, 'fsdp', scatter_dimension=0, tiled=False)  42.1 us
    all_gather x2, waiting for transfers between devices, device_step(): lax.all_gather(normed[m], 'fsdp', axis=0, tiled=True)  37.4 us
    all_gather x2, blocking collectives, device_step(): stats_all = lax.all_gather(stats, 'fsdp', axis=0, tiled=False)  35.6 us
    all_to_all x1, waiting for transfers between devices, fetch_round(): lax.all_to_all(send.reshape(groups, SLOTS, dim), 'fsdp', 0, 0)  25.5 us
  transfers between devices with their start and end apart: 8, of which 6 were waited for; matrix products, arithmetic and copies ran while one was open for 9% of the time, Pallas kernels for 25%

profile of v1, /device:TPU:0, one launch (start us, length us, event | category | flops | bytes accessed | tf_op | source)
XLA Modules:
  0.0 613.9 jit_solution(368016076687923949)
XLA Ops:
  10.5 15.0 %all-gather.4 = s32[16,2,512]{2,1,0:T(2,128)S(1)} all-gather(s32[1,2,512]{2,1,0:T(2,128)S(1)} %add_bitcast_fusion.1), channel_id=2, replica_groups=mesh['fsdp'=16] {'fsdp'}, dimensions={0}, use_global_device_ids=true | all-gather | bytes 69632 | tf_op jit(solution)/shard_map/all_gather | solution.py:163
  27.5 6.8 %fusion.70 = bf16[1024,768]{1,0:T(8,128)(2,1)} fusion(bf16[2008,768]{1,0:T(8,128)(2,1)} %table_ref.7, s32[1024]{0:T(1024)S(1)} %sub.134), kind=kOutput, calls=%fused_computation.121 | convolution fusion | flops 3161153536 | bytes 4661248 | tf_op jit(solution)/shard_map/dot_general | solution.py:197
  40.8 25.5 %all-to-all-done.2 = bf16[16,64,768]{2,1,0:T(8,128)(2,1)S(1)} async-done(((bf16[16,64,768]{2,1,0:T(8,128)(2,1)}), bf16[16,64,768]{2,1,0:T(8,128)(2,1)S(1)}, u32[]{:S(2)}, u32[]{:S(2)}) %all-to-all-start.2) | async-done | bytes 1572896 | tf_op jit(solution)/shard_map/all_to_all | solution.py:198
  69.4 9.1 %all-gather.15.cloned.1.call-done = bf16[2304,2048]{1,0:T(8,128)(2,1)} async-done(((bf16[144,2048]{1,0:T(8,128)(2,1)}), bf16[2304,2048]{1,0:T(8,128)(2,1)}) %all-gather.15.cloned.1.call-update) | async-done | bytes 9437200 | tf_op jit(solution)/shard_map/all_gather | solution.py:169
  78.6 6.0 fusion.140
  84.6 6.6 %reshape_reshape.6 = bf16[2048,768]{1,0:T(8,128)(2,1)} reshape(bf16[16,48,2048]{2,1,0:T(8,128)(2,1)} %get-tuple-element.397) | data formatting | bytes 6291456 | tf_op jit(solution)/shard_map/reshape;reshape | solution.py:172
  108.2 37.4 %all-gather.11.cloned.1.call-done.z_ref = bf16[4096,768]{1,0:T(8,128)(2,1)} async-done(((bf16[256,768]{1,0:T(8,128)(2,1)}), bf16[4096,768]{1,0:T(8,128)(2,1)}) %all-gather.11.cloned.1.call-update) | async-done | bytes 6291472 | tf_op jit(solution)/shard_map/all_gather | solution.py:219
  145.6 28.2 %head_stats.2 = (f32[16,2008,256]{2,1,0:T(8,128)}, f32[3,4096]{1,0:T(4,128)}) custom-call(s32[1]{0:T(128)} %bitcast.base_ref, bf16[4096,768]{1,0:T(8,128)(2,1)} %all-gather.11.cloned.1.call-done.z_ref, bf16[2008,768]{1,0:T(8,128)(2,1)} %get-tuple-element.696, s32[1,4096]{1,0:T(1,128)} %bitcast.195), custom_call_target="tpu_custom_call" | custom-call | flops 12633243648 | bytes 32899072 | tf_op jit(solution)/shard_map/head_stats/pallas_call | solution.py:73
  173.8 18.6 %all-gather.5 = f32[16,3,4096]{2,1,0:T(4,128)S(1)} all-gather(f32[1,3,4096]{2,1,0:T(4,128)} %bitcast.189), channel_id=4, replica_groups=mesh['fsdp'=16] {'fsdp'}, dimensions={0}, use_global_device_ids=true | all-gather | bytes 835584 | tf_op jit(solution)/shard_map/all_gather | solution.py:226
  197.8 47.5 %head_grad.2 = (f32[4096,768]{1,0:T(8,128)}, f32[2008,768]{1,0:T(8,128)}) custom-call(s32[1]{0:T(128)} %bitcast.base_ref, f32[16,2008,256]{2,1,0:T(8,128)} %get-tuple-element.289.logits_ref, bf16[4096,768]{1,0:T(8,128)(2,1)} %all-gather.11.cloned.1.call-done.z_ref, bf16[2008,768]{1,0:T(8,128)(2,1)} %get-tuple-element.696, s32[1,4096]{1,0:T(1,128)} %bitcast.196, ...), custom_call_target="tpu_custom_call" | custom-call | flops 25266487296 | bytes 32899072 | tf_op jit(solution)/shard_map/head_grad/pallas_call | solution.py:113
  245.4 28.2 %head_stats.3 = (f32[16,2008,256]{2,1,0:T(8,128)}, f32[3,4096]{1,0:T(4,128)}) custom-call(s32[1]{0:T(128)} %bitcast.base_ref, bf16[4096,768]{1,0:T(8,128)(2,1)} %all-gather.13.cloned.1.call-done.z_ref, bf16[2008,768]{1,0:T(8,128)(2,1)} %get-tuple-element.696, s32[1,4096]{1,0:T(1,128)} %bitcast.193), custom_call_target="tpu_custom_call" | custom-call | flops 12633243648 | bytes 32899072 | tf_op jit(solution)/shard_map/head_stats/pallas_call | solution.py:73
  273.6 17.0 %all-gather.6 = f32[16,3,4096]{2,1,0:T(4,128)S(1)} all-gather(f32[1,3,4096]{2,1,0:T(4,128)} %bitcast.190), channel_id=5, replica_groups=mesh['fsdp'=16] {'fsdp'}, dimensions={0}, use_global_device_ids=true | all-gather | bytes 835584 | tf_op jit(solution)/shard_map/all_gather | solution.py:226
  292.9 47.6 %head_grad.3 = (f32[4096,768]{1,0:T(8,128)}, f32[2008,768]{1,0:T(8,128)}) custom-call(s32[1]{0:T(128)} %bitcast.base_ref, f32[16,2008,256]{2,1,0:T(8,128)} %get-tuple-element.288.logits_ref, bf16[4096,768]{1,0:T(8,128)(2,1)} %all-gather.13.cloned.1.call-done.z_ref, bf16[2008,768]{1,0:T(8,128)(2,1)} %get-tuple-element.696, s32[1,4096]{1,0:T(1,128)} %bitcast.194, ...), custom_call_target="tpu_custom_call" | custom-call | flops 25266487296 | bytes 32899072 | tf_op jit(solution)/shard_map/head_grad/pallas_call | solution.py:113
  341.0 92.1 %reduce-scatter.6.cloned.1.call-done = f32[256,768]{1,0:T(8,128)} async-done(((f32[4096,768]{1,0:T(8,128)}), f32[256,768]{1,0:T(8,128)}) %reduce-scatter.6.cloned.1.call-update) | async-done | bytes 786448 | tf_op jit(solution)/shard_map/reduce_scatter | solution.py:232
  437.0 4.5 fusion.46
  441.6 4.5 fusion.61
  448.9 7.8 %reshape_reshape.7 = f32[16,48,2048]{2,1,0:T(8,128)} reshape(f32[2048,768]{1,0:T(8,128)} %fusion.61) | data formatting | bytes 12582912 | tf_op jit(solution)/shard_map/reshape;reshape | solution.py:242
  456.8 3.8 fusion.57
  462.5 6.9 %pad_maximum_fusion = f32[16,144,2048]{2,1,0:T(8,128)} fusion(f32[16,48,2048]{2,1,0:T(8,128)S(1)} %bitcast.168, f32[16,48,2048]{2,1,0:T(8,128)S(1)} %bitcast.169, f32[16,48,2048]{2,1,0:T(8,128)S(1)} %bitcast.170), kind=kLoop, calls=%fused_computation.42 | loop fusion | flops 9437184 | bytes 37748736 | tf_op jit(solution)/shard_map/concatenate | solution.py:241
  488.9 54.1 %all-to-all-done.3 = f32[16,64,768]{2,1,0:T(8,128)} async-done(((f32[16,64,768]{2,1,0:T(8,128)}), f32[16,64,768]{2,1,0:T(8,128)}, u32[]{:S(2)}, u32[]{:S(2)}) %all-to-all-start.3) | async-done | bytes 3145760 | tf_op jit(solution)/shard_map/all_to_all | solution.py:205
  545.7 3.9 fusion.25
  549.6 3.8 fusion.26
  553.4 6.0 add_add_fusion.2
  559.5 42.1 %reduce-scatter.8.cloned.1.call-done = f32[1,144,2048]{2,1,0:T(8,128)} async-done(((f32[16,144,2048]{2,1,0:T(8,128)}), f32[1,144,2048]{2,1,0:T(8,128)}) %reduce-scatter.8.cloned.1.call-update) | async-done | bytes 1179664 | tf_op jit(solution)/shard_map/reduce_scatter | solution.py:243
  (214 shorter events, 70.6 us)
Async XLA Ops:
  7.2 71.3 %all-gather.15.cloned.1.call-start = ((), (), s32[]{:S(2)}) async-start(), calls=%async_computation.12 | async-start | bytes 10027008 | tf_op jit(solution)/shard_map/all_gather | solution.py:169
  34.3 32.0 %all-to-all-start.2 = ((bf16[16,64,768]{2,1,0:T(8,128)(2,1)}), bf16[16,64,768]{2,1,0:T(8,128)(2,1)S(1)}, u32[]{:S(2)}, u32[]{:S(2)}) async-start(bf16[16,64,768]{2,1,0:T(8,128)(2,1)} %bitcast.182), calls=%async_computation.2 | async-start | bytes 3145728 | tf_op jit(solution)/shard_map/all_to_all | solution.py:198
  36.8 108.8 %all-gather.11.cloned.1.call-start = ((), (), s32[]{:S(2)}) async-start(), calls=%async_computation.7 | async-start | bytes 6684672 | tf_op jit(solution)/shard_map/all_gather | solution.py:219
  67.6 11.0 %copy-start.2 = (bf16[512,768]{1,0:T(8,128)(2,1)}, bf16[512,768]{1,0:T(8,128)(2,1)S(1)}, u32[]{:S(2)}) copy-start(bf16[512,768]{1,0:T(8,128)(2,1)S(1)} %get-tuple-element.285) | copy-start | bytes 2359300
  67.6 11.0 %copy-start.12 = (s32[16,512]{1,0:T(8,128)}, s32[16,512]{1,0:T(8,128)S(1)}, u32[]{:S(2)}) copy-start(s32[16,512]{1,0:T(8,128)S(1)} %get-tuple-element.679) | copy-start | bytes 98308
  67.6 10.9 %copy-start.15 = (s32[16,512]{1,0:T(8,128)}, s32[16,512]{1,0:T(8,128)S(1)}, u32[]{:S(2)}) copy-start(s32[16,512]{1,0:T(8,128)S(1)} %get-tuple-element.680) | copy-start | bytes 98308
  67.6 10.9 %copy-start.30 = (pred[16,512]{1,0:T(8,128)(4,1)}, pred[16,512]{1,0:T(8,128)(4,1)S(1)}, u32[]{:S(2)}) copy-start(pred[16,512]{1,0:T(8,128)(4,1)S(1)} %get-tuple-element.691) | copy-start | bytes 24580
  67.6 10.9 %copy-start.36 = (s32[512]{0:T(512)}, s32[512]{0:T(512)S(1)}, u32[]{:S(2)}) copy-start(s32[512]{0:T(512)S(1)} %get-tuple-element.692) | copy-start | bytes 6148
  67.6 10.9 %copy-start.38 = (s32[512]{0:T(512)}, s32[512]{0:T(512)S(1)}, u32[]{:S(2)}) copy-start(s32[512]{0:T(512)S(1)} %get-tuple-element.693) | copy-start | bytes 6148
  68.4 10.1 %copy-start.48 = (f32[256]{0:T(256)}, f32[256]{0:T(256)S(1)}, u32[]{:S(2)}) copy-start(f32[256]{0:T(256)S(1)} %get-tuple-element.454) | copy-start | bytes 3076
  68.5 10.1 %copy-start.50 = (f32[256]{0:T(256)}, f32[256]{0:T(256)S(1)}, u32[]{:S(2)}) copy-start(f32[256]{0:T(256)S(1)} %get-tuple-element.440) | copy-start | bytes 3076
  69.4 21.8 %copy-start.17 = (bf16[256,768]{1,0:T(8,128)(2,1)}, bf16[256,768]{1,0:T(8,128)(2,1)S(1)}, u32[]{:S(2)}) copy-start(bf16[256,768]{1,0:T(8,128)(2,1)S(1)} %get-tuple-element.421) | copy-start | bytes 1179652
  104.6 140.8 %all-gather.13.cloned.1.call-start = ((), (), s32[]{:S(2)}) async-start(), calls=%async_computation.8 | async-start | bytes 6684672 | tf_op jit(solution)/shard_map/all_gather | solution.py:219
  105.3 235.7 %reduce-scatter.4.cloned.1.call-start = ((), (), s32[]{:S(2)}) async-start(), calls=%async_computation.9 | async-start | bytes 13369344 | tf_op jit(solution)/shard_map/reduce_scatter | solution.py:232
  245.3 187.8 %reduce-scatter.6.cloned.1.call-start = ((), (), s32[]{:S(2)}) async-start(), calls=%async_computation.10 | async-start | bytes 13369344 | tf_op jit(solution)/shard_map/reduce_scatter | solution.py:232
  340.5 261.0 %reduce-scatter.8.cloned.1.call-start = ((), (), s32[]{:S(2)}) async-start(), calls=%async_computation.11 | async-start | bytes 20054016 | tf_op jit(solution)/shard_map/reduce_scatter | solution.py:243
  484.0 59.0 %all-to-all-start.3 = ((f32[16,64,768]{2,1,0:T(8,128)}), f32[16,64,768]{2,1,0:T(8,128)}, u32[]{:S(2)}, u32[]{:S(2)}) async-start(f32[16,64,768]{2,1,0:T(8,128)} %bitcast.175), calls=%async_computation.5 | async-start | bytes 6291456 | tf_op jit(solution)/shard_map/all_to_all | solution.py:205
  488.9 56.7 %copy-start.56 = (s32[1024]{0:T(1024)S(1)}, s32[1024]{0:T(1024)}, u32[]{:S(2)}) copy-start(s32[1024]{0:T(1024)} %copy-done.55) | copy-start | bytes 12292
  545.6 7.7 %slice-start.4 = ((s8[6168576]{0:T(1024)(128)(4,1)}), s8[4194304]{0:T(1024)(128)(4,1)S(1)}, s32[]{:S(2)}) async-start(s8[6168576]{0:T(1024)(128)(4,1)} %bitcast.202), calls=%async_computation.17 | async-start | bytes 8388608
  559.4 45.1 %copy-start.13 = (s32[16,512]{1,0:T(8,128)S(1)}, s32[16,512]{1,0:T(8,128)}, u32[]{:S(2)}) copy-start(s32[16,512]{1,0:T(8,128)} %copy-done.12) | copy-start | bytes 98308
  559.4 45.1 %copy-start.16 = (s32[16,512]{1,0:T(8,128)S(1)}, s32[16,512]{1,0:T(8,128)}, u32[]{:S(2)}) copy-start(s32[16,512]{1,0:T(8,128)} %copy-done.15) | copy-start | bytes 98308
  559.4 45.1 %copy-start.31 = (pred[16,512]{1,0:T(8,128)(4,1)S(1)}, pred[16,512]{1,0:T(8,128)(4,1)}, u32[]{:S(2)}) copy-start(pred[16,512]{1,0:T(8,128)(4,1)} %copy-done.30) | copy-start | bytes 24580
  559.4 45.1 %copy-start.37 = (s32[512]{0:T(512)S(1)}, s32[512]{0:T(512)}, u32[]{:S(2)}) copy-start(s32[512]{0:T(512)} %copy-done.36) | copy-start | bytes 6148
  559.5 45.1 %copy-start.39 = (s32[512]{0:T(512)S(1)}, s32[512]{0:T(512)}, u32[]{:S(2)}) copy-start(s32[512]{0:T(512)} %copy-done.38) | copy-start | bytes 6148
  (49 other events, 120.4 us)
Sparse Core Ops, SparseCore 0:
  10.4 68.0 all-gather.14
  104.7 40.8 all-gather.10
  148.4 45.2 all-gather.12
  245.4 92.7 reduce-scatter.3
  342.7 90.4 reduce-scatter.5
  469.5 131.9 reduce-scatter.7

commit v2 on v1

--- a/solution.py
+++ b/solution.py
@@ -8,8 +8,6 @@
 
 NORM_EPS = 1e-6
 SLOTS = 64
-TOK_BLOCK = 256
-VMEM_LIMIT = 60 * 1024 * 1024
 
 
 def rms_scale(values, gain_vec):
@@ -55,79 +53,285 @@
     return grad_rows, grad_mid, grad_gate_pre, grad_up_proj
 
 
-def stats_kernel(base_ref, z_ref, table_ref, lab_ref, logits_ref, stats_ref):
-    logits = lax.dot_general(table_ref[...], z_ref[...], COLS_DIMS, preferred_element_type=jnp.float32)
-    logits_ref[0] = logits
-    col_max = jnp.max(logits, axis=0, keepdims=True)
-    exp_sum = jnp.sum(jnp.exp(logits - col_max), axis=0, keepdims=True)
-    row_ids = lax.broadcasted_iota(jnp.int32, logits.shape, 0)
-    is_label = row_ids == (lab_ref[...] - base_ref[0])
-    lab_logit = jnp.sum(jnp.where(is_label, logits, 0.0), axis=0, keepdims=True)
-    stats_ref[...] = jnp.concatenate([col_max, exp_sum, lab_logit], axis=0)
-
-
-def head_stats(base, z_all, table_shard, lab_row):
-    tokens, dim = z_all.shape
-    rows = table_shard.shape[0]
-    blocks = tokens // TOK_BLOCK
+UNIT = 64
+CUBE_BITS = 3
+PARTS = 3
+VOCAB_TILE = 256
+STAT_ROWS = 8
+MESH_ID = pl.DeviceIdType.MESH
+PAD_LOGIT = -1e30
+
+
+def head_kernel(vocab_rows, chunks, z_hbm, table_ref, lab_ref, dz_ref, dtable_ref, loss_ref,
+                zbuf, lbuf, gbuf, dzbuf, got_core, got_one, got_two, got_three, stats, norm,
+                local_sem, ag_send, ag_recv, rs_send, rs_recv, st_send, st_recv):
+    me = lax.axis_index('fsdp')
+    total = 16
+    core = lax.rem(me, 2)
+    pos = [lax.rem(me // 2, 2), lax.rem(me // 4, 2), me // 8]
+    base = me * vocab_rows
+    padded, dim = table_ref.shape
+    part_cols = dim // PARTS
+    half = 8 * UNIT
+    tiles = padded // VOCAB_TILE
+
+    def peer(axis):
+        return me + (1 - 2 * pos[axis]) * (2 << axis)
+
+    core_peer = me + 1 - 2 * core
+
+    barrier = pltpu.get_barrier_semaphore()
+    for step in range(1, total):
+        pl.semaphore_signal(barrier, inc=1, device_id=(lax.rem(me + step, total),), device_id_type=MESH_ID)
+    own = pltpu.make_async_copy(z_hbm, zbuf.at[:, pos[2], pos[1], pos[0], core], local_sem)
+    own.start()
+    dtable_ref[...] = jnp.zeros_like(dtable_ref)
+    loss_ref[...] = jnp.zeros_like(loss_ref)
+    own.wait()
+    pl.semaphore_wait(barrier, total - 1)
+
+    def where(choice):
+        return choice.get(2, slice(None)), choice.get(1, slice(None)), choice.get(0, slice(None))
+
+    def axes(part):
+        return part % 3, (part + 1) % 3, (part + 2) % 3
+
+    def cols(part):
+        return pl.ds(part * part_cols, part_cols)
+
+    def gather_copies(chunk, phase):
+        if phase == 4:
+            here = zbuf.at[chunk, :, :, :, core]
+            return [pltpu.make_async_remote_copy(here, here, ag_send.at[chunk, 9], ag_recv.at[chunk, 9],
+                                                 device_id=(core_peer,), device_id_type=MESH_ID)]
+        copies = []
+        for part in range(PARTS):
+            order = axes(part)
+            fixed = {axis: pos[axis] for axis in order[phase - 1:]}
+            iz, iy, ix = where(fixed)
+            here = zbuf.at[chunk, iz, iy, ix, core, :, cols(part)]
+            sem = (phase - 1) * PARTS + part
+            copies.append(pltpu.make_async_remote_copy(here, here, ag_send.at[chunk, sem], ag_recv.at[chunk, sem],
+                                                       device_id=(peer(order[phase - 1]),), device_id_type=MESH_ID))
+        return copies
+
+    def reduce_copies(chunk, phase):
+        slot = lax.rem(chunk, 2)
+        if phase == 0:
+            return [pltpu.make_async_remote_copy(dzbuf.at[slot, :, :, :, 1 - core], got_core.at[slot], rs_send.at[chunk, 9], rs_recv.at[chunk, 9],
+                                                 device_id=(core_peer,), device_id_type=MESH_ID)]
+        copies = []
+        for part in range(PARTS):
+            order = axes(part)
+            fixed = {axis: pos[axis] for axis in order[:phase - 1]}
+            fixed[order[phase - 1]] = 1 - pos[order[phase - 1]]
+            iz, iy, ix = where(fixed)
+            got = (got_one, got_two, got_three)[phase - 1]
+            sem = (phase - 1) * PARTS + part
+            copies.append(pltpu.make_async_remote_copy(dzbuf.at[slot, iz, iy, ix, core, :, cols(part)], got.at[slot, part],
+                                                       rs_send.at[chunk, sem], rs_recv.at[chunk, sem],
+                                                       device_id=(peer(order[phase - 1]),), device_id_type=MESH_ID))
+        return copies
+
+    def start(copies):
+        for copy in copies:
+            copy.start()
+
+    def finish(copies):
+        for copy in copies:
+            copy.wait()
+
+    def reduce_add(chunk, phase):
+        slot = lax.rem(chunk, 2)
+        if phase == 0:
+            dzbuf[slot, :, :, :, core] += got_core[slot]
+            return
+        for part in range(PARTS):
+            order = axes(part)
+            iz, iy, ix = where({axis: pos[axis] for axis in order[:phase]})
+            got = (got_one, got_two, got_three)[phase - 1]
+            lanes = slice(part * part_cols, (part + 1) * part_cols)
+            if phase == 3:
+                rows = pl.ds(pl.multiple_of(chunk * UNIT, UNIT), UNIT)
+                dz_ref[rows, lanes] = dzbuf[slot, iz, iy, ix, core, :, lanes] + got[slot, part]
+            else:
+                dzbuf[slot, iz, iy, ix, core, :, lanes] += got[slot, part]
+
+    def stat_copies(chunk):
+        copies = []
+        for step in range(1, total):
+            to = lax.rem(me + step, total)
+            copies.append(pltpu.make_async_remote_copy(stats.at[chunk, me], stats.at[chunk, me], st_send.at[chunk, step], st_recv.at[chunk, step],
+                                                       device_id=(to,), device_id_type=MESH_ID))
+        return copies
+
+    def label_row(chunk, part):
+        lab = lab_ref[pl.ds(chunk * 2 + part, 1), :] - base
+        return jnp.where(lab < vocab_rows, lab, -1)
+
+    row_ids = lax.broadcasted_iota(jnp.int32, (VOCAB_TILE, half), 0)
+
+    def forward_half(chunk, part):
+        slot = lax.rem(chunk, 2)
+        zb = zbuf[chunk, part].reshape(half, dim)
+        lab = label_row(chunk, part)
+        tops, sums, labs = [], [], []
+        for tile in range(tiles):
+            rows = slice(tile * VOCAB_TILE, (tile + 1) * VOCAB_TILE)
+            logits = lax.dot_general(table_ref[rows, :], zb, COLS_DIMS, preferred_element_type=jnp.float32)
+            if (tile + 1) * VOCAB_TILE > vocab_rows:
+                logits = jnp.where(row_ids < vocab_rows - tile * VOCAB_TILE, logits, PAD_LOGIT)
+            lbuf[slot, rows, part * half:(part + 1) * half] = logits
+            top = jnp.max(logits, axis=0, keepdims=True)
+            tops.append(top)
+            sums.append(jnp.sum(jnp.exp(logits - top), axis=0, keepdims=True))
+            labs.append(jnp.sum(jnp.where(row_ids == lab - tile * VOCAB_TILE, logits, 0.0), axis=0, keepdims=True))
+        top = functools.reduce(jnp.maximum, tops)
+        exp_sum = sum(s * jnp.exp(t - top) for s, t in zip(sums, tops))
+        stats[chunk, me, part:part + 1, :] = top
+        stats[chunk, me, 2 + part:3 + part, :] = exp_sum
+        stats[chunk, me, 4 + part:5 + part, :] = sum(labs)
+
+    def combine(chunk):
+        for part in range(2):
+            tops = stats[chunk, :, part, :]
+            top = jnp.max(tops, axis=0, keepdims=True)
+            exp_sum = jnp.sum(stats[chunk, :, 2 + part, :] * jnp.exp(tops - top), axis=0, keepdims=True)
+            lab = jnp.sum(stats[chunk, :, 4 + part, :], axis=0, keepdims=True)
+            norm[part:part + 1, :] = top
+            norm[2 + part:3 + part, :] = 1.0 / exp_sum
+            loss_ref[part:part + 1, :] += top + jnp.log(exp_sum) - lab
+
+    def table_half(chunk, which):
+        slot = lax.rem(chunk, 2)
+        zc = zbuf[chunk].reshape(2 * half, dim)
+        for tile in range(which * tiles // 2, (which + 1) * tiles // 2):
+            rows = slice(tile * VOCAB_TILE, (tile + 1) * VOCAB_TILE)
+            for part in range(2):
+                lanes = slice(part * half, (part + 1) * half)
+                probs = jnp.exp(lbuf[slot, rows, lanes] - norm[part:part + 1, :]) * norm[2 + part:3 + part, :]
+                hot = row_ids == label_row(chunk, part) - tile * VOCAB_TILE
+                gbuf[rows, lanes] = jnp.where(hot, probs - 1.0, probs).astype(jnp.bfloat16)
+            dtable_ref[rows, :] += jnp.dot(gbuf[rows, :], zc, preferred_element_type=jnp.float32)
+
+    def token_half(chunk, part):
+        slot = lax.rem(chunk, 2)
+        dz = lax.dot_general(gbuf[:, part * half:(part + 1) * half], table_ref[...], ROWS_DIMS, preferred_element_type=jnp.float32)
+        dzbuf[slot, part] = dz.reshape(2, 2, 2, UNIT, dim)
+
+    for phase in range(1, 5):
+        first = gather_copies(0, phase)
+        start(first)
+        finish(first)
+
+    def body(i, carry):
+        fwd = i < chunks
+        more = i < chunks - 1
+        bwd = (i >= 1) & (i <= chunks)
+        red = (i >= 2) & (i <= chunks + 1)
+        last = i >= 3
+        nxt = jnp.minimum(i + 1, chunks - 1)
+        prev = jnp.maximum(i - 1, 0)
+        old = jnp.maximum(i - 2, 0)
+        older = jnp.maximum(i - 3, 0)
+
+        pl.when(red)(lambda: start(reduce_copies(old, 0)))
+        pl.when(more)(lambda: start(gather_copies(nxt, 1)))
+        pl.when(fwd)(lambda: forward_half(i, 0))
+
+        @pl.when(last)
+        def _():
+            finish(reduce_copies(older, 3))
+            reduce_add(older, 3)
+
+        @pl.when(red)
+        def _():
+            finish(reduce_copies(old, 0))
+            reduce_add(old, 0)
+            start(reduce_copies(old, 1))
+
+        @pl.when(more)
+        def _():
+            finish(gather_copies(nxt, 1))
+            start(gather_copies(nxt, 2))
+        pl.when(fwd)(lambda: forward_half(i, 1))
+
+        @pl.when(more)
+        def _():
+            finish(gather_copies(nxt, 2))
+            start(gather_copies(nxt, 3))
+
+        @pl.when(bwd)
+        def _():
+            finish(stat_copies(prev))
+            combine(prev)
+            table_half(prev, 0)
+
+        pl.when(fwd)(lambda: start(stat_copies(i)))
+
+        @pl.when(more)
+        def _():
+            finish(gather_copies(nxt, 3))
+            start(gather_copies(nxt, 4))
+        pl.when(bwd)(lambda: table_half(prev, 1))
+
+        @pl.when(red)
+        def _():
+            finish(reduce_copies(old, 1))
+            reduce_add(old, 1)
+            start(reduce_copies(old, 2))
+
+        @pl.when(bwd)
+        def _():
+            token_half(prev, 0)
+            token_half(prev, 1)
+
+        @pl.when(red)
+        def _():
+            finish(reduce_copies(old, 2))
+            reduce_add(old, 2)
+            start(reduce_copies(old, 3))
+        pl.when(more)(lambda: finish(gather_copies(nxt, 4)))
+        return carry
+
+    lax.fori_loop(0, chunks + 3, body, 0)
+
+
+def head(z_local, table_padded, lab_rows, vocab_rows):
+    tokens, dim = z_local.shape
+    chunks = tokens // UNIT
+    padded = table_padded.shape[0]
+    chunk_tokens = 16 * UNIT
+    part_cols = dim // PARTS
+    f32, bf16 = jnp.float32, jnp.bfloat16
+    sems = pltpu.SemaphoreType.DMA
+    vmem = pl.BlockSpec(memory_space=pltpu.VMEM)
+    cost = 6 * tokens * 16 * padded * dim
     return pl.pallas_call(
-        stats_kernel,
-        grid=(blocks,),
-        in_specs=[pl.BlockSpec(memory_space=pltpu.SMEM),
-                  pl.BlockSpec((TOK_BLOCK, dim), lambda i: (i, 0)),
-                  pl.BlockSpec((rows, dim), lambda i: (0, 0)),
-                  pl.BlockSpec((1, TOK_BLOCK), lambda i: (0, i))],
-        out_specs=[pl.BlockSpec((1, rows, TOK_BLOCK), lambda i: (i, 0, 0)),
-                   pl.BlockSpec((3, TOK_BLOCK), lambda i: (0, i))],
-        out_shape=[jax.ShapeDtypeStruct((blocks, rows, TOK_BLOCK), jnp.float32),
-                   jax.ShapeDtypeStruct((3, tokens), jnp.float32)],
-        compiler_params=pltpu.CompilerParams(vmem_limit_bytes=VMEM_LIMIT, dimension_semantics=("arbitrary",)),
-        cost_estimate=pl.CostEstimate(flops=2 * tokens * rows * dim, bytes_accessed=tokens * rows * 4, transcendentals=tokens * rows),
-        name="head_stats",
-    )(base, z_all, table_shard, lab_row)
-
-
-def grad_kernel(base_ref, logits_ref, z_ref, table_ref, lab_ref, norm_ref, init_ref, dz_ref, dtable_ref):
-    logits = logits_ref[0]
-    norm = norm_ref[...]
-    row_ids = lax.broadcasted_iota(jnp.int32, logits.shape, 0)
-    is_label = row_ids == (lab_ref[...] - base_ref[0])
-    probs = jnp.exp(logits - norm[0:1]) * norm[1:2]
-    grad_logits = (probs - is_label.astype(jnp.float32)).astype(jnp.bfloat16)
-    dz_ref[...] = lax.dot_general(grad_logits, table_ref[...], ROWS_DIMS, preferred_element_type=jnp.float32)
-    step_grad = jnp.dot(grad_logits, z_ref[...], preferred_element_type=jnp.float32)
-
-    @pl.when(pl.program_id(0) == 0)
-    def _():
-        dtable_ref[...] = init_ref[...] + step_grad
-
-    @pl.when(pl.program_id(0) > 0)
-    def _():
-        dtable_ref[...] += step_grad
-
-
-def head_grad(base, logits, z_all, table_shard, lab_row, norm, init):
-    tokens, dim = z_all.shape
-    rows = table_shard.shape[0]
-    blocks = tokens // TOK_BLOCK
-    return pl.pallas_call(
-        grad_kernel,
-        grid=(blocks,),
-        in_specs=[pl.BlockSpec(memory_space=pltpu.SMEM),
-                  pl.BlockSpec((1, rows, TOK_BLOCK), lambda i: (i, 0, 0)),
-                  pl.BlockSpec((TOK_BLOCK, dim), lambda i: (i, 0)),
-                  pl.BlockSpec((rows, dim), lambda i: (0, 0)),
-                  pl.BlockSpec((1, TOK_BLOCK), lambda i: (0, i)),
-                  pl.BlockSpec((2, TOK_BLOCK), lambda i: (0, i)),
-                  pl.BlockSpec((rows, dim), lambda i: (0, 0))],
-        out_specs=[pl.BlockSpec((TOK_BLOCK, dim), lambda i: (i, 0)),
-                   pl.BlockSpec((rows, dim), lambda i: (0, 0))],
-        out_shape=[jax.ShapeDtypeStruct((tokens, dim), jnp.float32),
-                   jax.ShapeDtypeStruct((rows, dim), jnp.float32)],
-        compiler_params=pltpu.CompilerParams(vmem_limit_bytes=VMEM_LIMIT, dimension_semantics=("arbitrary",)),
-        cost_estimate=pl.CostEstimate(flops=4 * tokens * rows * dim, bytes_accessed=tokens * rows * 4, transcendentals=tokens * rows),
-        name="head_grad",
-    )(base, logits, z_all, table_shard, lab_row, norm, init)
+        functools.partial(head_kernel, vocab_rows, chunks),
+        in_specs=[pl.BlockSpec(memory_space=pl.ANY), vmem, vmem],
+        out_specs=[vmem, vmem, vmem],
+        out_shape=[jax.ShapeDtypeStruct((tokens, dim), f32),
+                   jax.ShapeDtypeStruct((padded, dim), f32),
+                   jax.ShapeDtypeStruct((2, 8 * UNIT), f32)],
+        scratch_shapes=[pltpu.VMEM((chunks, 2, 2, 2, 2, UNIT, dim), bf16),
+                        pltpu.VMEM((2, padded, chunk_tokens), f32),
+                        pltpu.VMEM((padded, chunk_tokens), bf16),
+                        pltpu.VMEM((2, 2, 2, 2, 2, UNIT, dim), f32),
+                        pltpu.VMEM((2, 2, 2, 2, UNIT, dim), f32),
+                        pltpu.VMEM((2, PARTS, 2, 2, UNIT, part_cols), f32),
+                        pltpu.VMEM((2, PARTS, 2, UNIT, part_cols), f32),
+                        pltpu.VMEM((2, PARTS, UNIT, part_cols), f32),
+                        pltpu.VMEM((chunks, 16, STAT_ROWS, 8 * UNIT), f32),
+                        pltpu.VMEM((8, 8 * UNIT), f32),
+                        sems(()),
+                        sems((chunks, 10)), sems((chunks, 10)),
+                        sems((chunks, 10)), sems((chunks, 10)),
+                        sems((chunks, 16)), sems((chunks, 16))],
+        compiler_params=pltpu.CompilerParams(vmem_limit_bytes=67043328, collective_id=1, has_side_effects=True),
+        cost_estimate=pl.CostEstimate(flops=cost, bytes_accessed=4 * padded * dim, transcendentals=2 * tokens * 16 * padded),
+        name="head_all",
+    )(z_local.reshape(chunks, UNIT, dim), table_padded, lab_rows)
 
 
 def split3(values):
@@ -156,13 +360,10 @@
         total_tokens = tok_dev * groups
         rows, dim = table_shard.shape
         me = lax.axis_index('fsdp')
-        base = (me * rows).astype(jnp.int32)
-        base_arr = base.reshape(1)
 
         packed = jnp.stack([token_ids.reshape(tok_dev), labels.reshape(tok_dev)])
         packed_all = lax.all_gather(packed, 'fsdp', axis=0, tiled=False)
         ids_all = packed_all[:, 0]
-        lab_all = packed_all[:, 1].reshape(groups, micro_count, tok_micro)
 
         gate_rows, ffn = gate_shard.shape
         down_rows = down_shard.shape[0]
@@ -215,21 +416,14 @@
             normed.append(out)
             saved.append(kept)
 
-        lab_rows = [lab_all[:, m].reshape(1, groups * tok_micro) for m in range(micro_count)]
-        z_all = [lax.all_gather(normed[m], 'fsdp', axis=0, tiled=True) for m in range(micro_count)]
-        dtable = jnp.zeros((rows, dim), jnp.float32)
-        loss_total = jnp.zeros((), jnp.float32)
-        firsts = [head_stats(base_arr, z_all[m], table_shard, lab_rows[m]) for m in range(micro_count)]
-        grad_normed = []
-        for m in range(micro_count):
-            logits, stats = firsts[m]
-            stats_all = lax.all_gather(stats, 'fsdp', axis=0, tiled=False)
-            top = jnp.max(stats_all[:, 0], axis=0)
-            exp_total = jnp.sum(stats_all[:, 1] * jnp.exp(stats_all[:, 0] - top[None]), axis=0)
-            loss_total = loss_total + jnp.sum(top + jnp.log(exp_total) - jnp.sum(stats_all[:, 2], axis=0))
-            norm = jnp.stack([top, 1.0 / exp_total])
-            dz, dtable = head_grad(base_arr, logits, z_all[m], table_shard, lab_rows[m], norm, dtable)
-            grad_normed.append(lax.psum_scatter(dz, 'fsdp', scatter_dimension=0, tiled=True))
+        chunks = tok_dev // UNIT
+        lab_rows = jnp.transpose(packed_all[:, 1].reshape(groups, chunks, UNIT), (1, 0, 2)).reshape(2 * chunks, groups * UNIT // 2)
+        padded = -(-rows // VOCAB_TILE) * VOCAB_TILE
+        table_padded = jnp.pad(table_shard, ((0, padded - rows), (0, 0)))
+        dz, dtable, loss_rows = head(jnp.concatenate(normed, axis=0), table_padded, lab_rows, rows)
+        dtable = dtable[:rows]
+        loss_total = jnp.sum(loss_rows)
+        grad_normed = [dz[m * tok_micro:(m + 1) * tok_micro] for m in range(micro_count)]
 
         backs = [mlp_backward(saved[m], grad_normed[m], gain_in, gain_out, w_gate, w_up, w_down) for m in range(micro_count)]
         grad_rows, grad_mid, grad_gate_pre, grad_up_proj = [jnp.concatenate(parts, axis=0) for parts in zip(*backs)]

time: 622 us -> 533 us (0.86)
  waiting for transfers between devices: 261 us -> 127 us
  Pallas kernels: 151 us -> 239 us
  blocking collectives: 50.6 us -> 15 us
    reduce_scatter x2 -> x0, waiting for transfers between devices: 92.2 us -> none  [device_step(): lax.psum_scatter(dz, 'fsdp', scatter_dimension=0, tiled=True)]
    pallas_call x4 -> x1, Pallas kernels: 151 us -> 239 us  [head(): pl.pallas_call(functools.partial(head_kernel, vocab_rows, chunks), in_spe...]
    all_gather x2 -> x0, waiting for transfers between devices: 37.4 us -> none  [device_step(): lax.all_gather(normed[m], 'fsdp', axis=0, tiled=True)]
    all_gather x2 -> x0, blocking collectives: 35.6 us -> none  [device_step(): stats_all = lax.all_gather(stats, 'fsdp', axis=0, tiled=False)]
  transfers between devices with their start and end apart: 8 -> 4, of which waited for: 6 -> 4; matrix products, arithmetic and copies ran while one was open for 9% -> 9% of each run, Pallas kernels for 25% -> 0%
where the time goes in v2:
time: 533 us; the launch traced here: 525 us
  Pallas kernels  239 us (45%)
  waiting for transfers between devices  127 us (24%)
  matrix products  60.6 us (11%)
  local copies, waits for them, and re-layouts  34.4 us (6%)
  other arithmetic  21.7 us (4%)
  between operations  19.5 us (4%)
  blocking collectives  15 us (3%)
  starting transfers between devices  6.43 us (1%)
    pallas_call x1, Pallas kernels, head(): pl.pallas_call(functools.partial(head_kernel, vocab_rows, chunks), in_spe...  239 us
    all_to_all x1, waiting for transfers between devices, return_round(): lax.all_to_all(send.reshape(groups, SLOTS, dim), 'fsdp', 0, 0)  53.4 us
    reduce_scatter x1, waiting for transfers between devices, device_step(): w_grad = lax.psum_scatter(w_grads, 'fsdp', scatter_dimension=0, tiled=False)  42.9 us
    all_to_all x1, waiting for transfers between devices, fetch_round(): lax.all_to_all(send.reshape(groups, SLOTS, dim), 'fsdp', 0, 0)  21.4 us
    dot_general x6, matrix products, pick_rows(): term = jnp.dot(select, part, preferred_element_type=jnp.float32)  18.5 us
    all_gather x1, blocking collectives, device_step(): packed_all = lax.all_gather(packed, 'fsdp', axis=0, tiled=False)  15 us
  transfers between devices with their start and end apart: 4, of which 4 were waited for; matrix products, arithmetic and copies ran while one was open for 9% of the time, Pallas kernels for 0%

profile of v2, /device:TPU:0, one launch (start us, length us, event | category | flops | bytes accessed | tf_op | source)
XLA Modules:
  0.0 524.6 jit_solution(10663798254363946017)
XLA Ops:
  10.5 15.0 %all-gather.2 = s32[16,2,512]{2,1,0:T(2,128)S(1)} all-gather(s32[1,2,512]{2,1,0:T(2,128)S(1)} %add_bitcast_fusion.1), channel_id=2, replica_groups=mesh['fsdp'=16] {'fsdp'}, dimensions={0}, use_global_device_ids=true | all-gather | bytes 69632 | tf_op jit(solution)/shard_map/all_gather | solution.py:365
  26.9 6.8 %fusion.70 = bf16[1024,768]{1,0:T(8,128)(2,1)} fusion(bf16[2008,768]{1,0:T(8,128)(2,1)} %param.14, s32[1024]{0:T(1024)S(1)} %sub.112), kind=kOutput, calls=%fused_computation.121 | convolution fusion | flops 3161153536 | bytes 4661248 | tf_op jit(solution)/shard_map/dot_general | solution.py:398
  33.7 2.5 all-to-all-start.2
  39.5 3.8 pad.4.table_ref
  44.7 21.4 %all-to-all-done.2 = bf16[16,64,768]{2,1,0:T(8,128)(2,1)S(1)} async-done(((bf16[16,64,768]{2,1,0:T(8,128)(2,1)}), bf16[16,64,768]{2,1,0:T(8,128)(2,1)S(1)}, u32[]{:S(2)}, u32[]{:S(2)}) %all-to-all-start.2) | async-done | bytes 1572896 | tf_op jit(solution)/shard_map/all_to_all | solution.py:399
  69.3 8.9 %all-gather.5.cloned.1.call-done = bf16[2304,2048]{1,0:T(8,128)(2,1)} async-done(((bf16[144,2048]{1,0:T(8,128)(2,1)}), bf16[2304,2048]{1,0:T(8,128)(2,1)}) %all-gather.5.cloned.1.call-update) | async-done | bytes 9437200 | tf_op jit(solution)/shard_map/all_gather | solution.py:370
  78.2 6.1 %fusion.132 = (bf16[16,48,2048]{2,1,0:T(8,128)(2,1)}, bf16[16,48,2048]{2,1,0:T(8,128)(2,1)S(1)}, bf16[16,48,2048]{2,1,0:T(8,128)(2,1)}) fusion(bf16[16,144,2048]{2,1,0:T(8,128)(2,1)} %bitcast.147), kind=kLoop, calls=%fused_computation.248 | loop fusion | bytes 18874368 | tf_op jit(solution)/shard_map/slice | solution.py:373
  84.3 7.0 %reshape_reshape.6 = bf16[2048,768]{1,0:T(8,128)(2,1)} reshape(bf16[16,48,2048]{2,1,0:T(8,128)(2,1)} %get-tuple-element.383) | data formatting | bytes 6291456 | tf_op jit(solution)/shard_map/reshape;reshape | solution.py:373
  91.3 2.9 convolution_convert_fusion.3
  105.3 239.0 %head_all.1 = (f32[512,768]{1,0:T(8,128)}, f32[2048,768]{1,0:T(8,128)}, f32[2,512]{1,0:T(2,128)}) custom-call(bf16[8,64,768]{2,1,0:T(8,128)(2,1)} %bitcast.154, bf16[2048,768]{1,0:T(8,128)(2,1)} %pad.4.table_ref, s32[16,512]{1,0:T(8,128)} %reshape.280.lab_ref), custom_call_target="tpu_custom_call" | custom-call | flops 77309411328 | bytes 6291456 | tf_op jit(solution)/shard_map/head_all/pallas_call | solution.py:310
  348.3 4.5 fusion.52
  352.8 4.5 fusion.61
  359.7 7.9 %reshape_reshape.7 = f32[16,48,2048]{2,1,0:T(8,128)} reshape(f32[2048,768]{1,0:T(8,128)} %fusion.61) | data formatting | bytes 12582912 | tf_op jit(solution)/shard_map/reshape;reshape | solution.py:436
  367.6 3.5 fusion.57
  373.0 6.9 %pad_maximum_fusion = f32[16,144,2048]{2,1,0:T(8,128)} fusion(f32[16,48,2048]{2,1,0:T(8,128)S(1)} %bitcast.139, f32[16,48,2048]{2,1,0:T(8,128)S(1)} %bitcast.140, f32[16,48,2048]{2,1,0:T(8,128)S(1)} %bitcast.141), kind=kLoop, calls=%fused_computation.42 | loop fusion | flops 9437184 | bytes 37748736 | tf_op jit(solution)/shard_map/concatenate | solution.py:435
  379.9 3.4 fusion.135
  391.7 2.8 add_add_fusion.3
  394.5 3.8 all-to-all-start.3
  399.6 53.4 %all-to-all-done.3 = f32[16,64,768]{2,1,0:T(8,128)} async-done(((f32[16,64,768]{2,1,0:T(8,128)}), f32[16,64,768]{2,1,0:T(8,128)}, u32[]{:S(2)}, u32[]{:S(2)}) %all-to-all-start.3) | async-done | bytes 3145760 | tf_op jit(solution)/shard_map/all_to_all | solution.py:406
  453.0 2.6 reduce-precision_convert_fusion.3
  455.7 3.8 fusion.25
  459.5 3.9 fusion.26
  463.4 5.9 %add_add_fusion.2 = f32[2008,768]{1,0:T(8,128)} fusion(f32[2008,768]{1,0:T(8,128)S(1)} %fusion.25, f32[2008,768]{1,0:T(8,128)S(1)} %fusion.26, f32[2048,768]{1,0:T(8,128)S(1)} %bitcast.166, bf16[1024,768]{1,0:T(8,128)(2,1)S(1)} %get-tuple-element.386, s32[1024]{0:T(1024)S(1)} %copy-done.56), kind=kOutput, calls=%fused_computation.49 | convolution fusion | flops 3164993536 | bytes 26251264 | tf_op jit(solution)/shard_map/dot_general | solution.py:348
  469.3 42.9 %reduce-scatter.2.cloned.1.call-done = f32[1,144,2048]{2,1,0:T(8,128)} async-done(((f32[16,144,2048]{2,1,0:T(8,128)}), f32[1,144,2048]{2,1,0:T(8,128)}) %reduce-scatter.2.cloned.1.call-update) | async-done | bytes 1179664 | tf_op jit(solution)/shard_map/reduce_scatter | solution.py:437
  (194 shorter events, 41.9 us)
Async XLA Ops:
  7.2 71.0 %all-gather.5.cloned.1.call-start = ((), (), s32[]{:S(2)}) async-start(), calls=%async_computation.6 | async-start | bytes 10027008 | tf_op jit(solution)/shard_map/all_gather | solution.py:370
  26.9 6.8 %copy-start.55 = (s32[1024]{0:T(1024)}, s32[1024]{0:T(1024)S(1)}, u32[]{:S(2)}) copy-start(s32[1024]{0:T(1024)S(1)} %sub.112) | copy-start | bytes 12292
  33.7 32.5 %all-to-all-start.2 = ((bf16[16,64,768]{2,1,0:T(8,128)(2,1)}), bf16[16,64,768]{2,1,0:T(8,128)(2,1)S(1)}, u32[]{:S(2)}, u32[]{:S(2)}) async-start(bf16[16,64,768]{2,1,0:T(8,128)(2,1)} %bitcast.153), calls=%async_computation.2 | async-start | bytes 3145728 | tf_op jit(solution)/shard_map/all_to_all | solution.py:399
  36.2 476.0 %reduce-scatter.2.cloned.1.call-start = ((), (), s32[]{:S(2)}) async-start(), calls=%async_computation.5 | async-start | bytes 20054016 | tf_op jit(solution)/shard_map/reduce_scatter | solution.py:437
  67.5 10.7 %copy-start.5 = (bf16[512,768]{1,0:T(8,128)(2,1)}, bf16[512,768]{1,0:T(8,128)(2,1)S(1)}, u32[]{:S(2)}) copy-start(bf16[512,768]{1,0:T(8,128)(2,1)S(1)} %get-tuple-element.280) | copy-start | bytes 2359300
  67.5 10.7 %copy-start.12 = (s32[16,512]{1,0:T(8,128)}, s32[16,512]{1,0:T(8,128)S(1)}, u32[]{:S(2)}) copy-start(s32[16,512]{1,0:T(8,128)S(1)} %get-tuple-element.641) | copy-start | bytes 98308
  67.5 10.7 %copy-start.14 = (s32[16,512]{1,0:T(8,128)}, s32[16,512]{1,0:T(8,128)S(1)}, u32[]{:S(2)}) copy-start(s32[16,512]{1,0:T(8,128)S(1)} %get-tuple-element.642) | copy-start | bytes 98308
  67.5 10.7 %copy-start.28 = (pred[16,512]{1,0:T(8,128)(4,1)}, pred[16,512]{1,0:T(8,128)(4,1)S(1)}, u32[]{:S(2)}) copy-start(pred[16,512]{1,0:T(8,128)(4,1)S(1)} %get-tuple-element.649) | copy-start | bytes 24580
  67.5 10.7 %copy-start.34 = (s32[512]{0:T(512)}, s32[512]{0:T(512)S(1)}, u32[]{:S(2)}) copy-start(s32[512]{0:T(512)S(1)} %get-tuple-element.650) | copy-start | bytes 6148
  67.5 10.7 %copy-start.36 = (s32[512]{0:T(512)}, s32[512]{0:T(512)S(1)}, u32[]{:S(2)}) copy-start(s32[512]{0:T(512)S(1)} %get-tuple-element.651) | copy-start | bytes 6148
  68.3 9.9 %copy-start.48 = (f32[256]{0:T(256)}, f32[256]{0:T(256)S(1)}, u32[]{:S(2)}) copy-start(f32[256]{0:T(256)S(1)} %get-tuple-element.426) | copy-start | bytes 3076
  68.3 9.9 %copy-start.50 = (f32[256]{0:T(256)}, f32[256]{0:T(256)S(1)}, u32[]{:S(2)}) copy-start(f32[256]{0:T(256)S(1)} %get-tuple-element.412) | copy-start | bytes 3076
  69.3 24.9 %copy-start.16 = (bf16[256,768]{1,0:T(8,128)(2,1)}, bf16[256,768]{1,0:T(8,128)(2,1)S(1)}, u32[]{:S(2)}) copy-start(bf16[256,768]{1,0:T(8,128)(2,1)S(1)} %get-tuple-element.401) | copy-start | bytes 1179652
  84.3 15.8 %copy-start.3 = (bf16[16,48,2048]{2,1,0:T(8,128)(2,1)}, bf16[16,48,2048]{2,1,0:T(8,128)(2,1)S(1)}, u32[]{:S(2)}) copy-start(bf16[16,48,2048]{2,1,0:T(8,128)(2,1)S(1)} %get-tuple-element.384) | copy-start | bytes 9437188
  98.2 5.9 %copy-start.8 = (bf16[256,768]{1,0:T(8,128)(2,1)}, bf16[256,768]{1,0:T(8,128)(2,1)S(1)}, u32[]{:S(2)}) copy-start(bf16[256,768]{1,0:T(8,128)(2,1)S(1)} %get-tuple-element.420) | copy-start | bytes 1179652
  367.6 5.4 %slice-start = ((s8[6291456]{0:T(1024)(128)(4,1)}), s8[4194304]{0:T(1024)(128)(4,1)S(1)}, s32[]{:S(2)}) async-start(s8[6291456]{0:T(1024)(128)(4,1)} %bitcast.138), calls=%async_computation.7 | async-start | bytes 8388608
  394.5 58.5 %all-to-all-start.3 = ((f32[16,64,768]{2,1,0:T(8,128)}), f32[16,64,768]{2,1,0:T(8,128)}, u32[]{:S(2)}, u32[]{:S(2)}) async-start(f32[16,64,768]{2,1,0:T(8,128)} %bitcast.146), calls=%async_computation.3 | async-start | bytes 6291456 | tf_op jit(solution)/shard_map/all_to_all | solution.py:406
  399.6 56.1 %copy-start.56 = (s32[1024]{0:T(1024)S(1)}, s32[1024]{0:T(1024)}, u32[]{:S(2)}) copy-start(s32[1024]{0:T(1024)} %copy-done.55) | copy-start | bytes 12292
  455.7 7.7 %slice-start.4 = ((s8[6291456]{0:T(1024)(128)(4,1)}), s8[4194304]{0:T(1024)(128)(4,1)S(1)}, s32[]{:S(2)}) async-start(s8[6291456]{0:T(1024)(128)(4,1)} %bitcast.165), calls=%async_computation.11 | async-start | bytes 8388608
  469.3 46.0 %copy-start.13 = (s32[16,512]{1,0:T(8,128)S(1)}, s32[16,512]{1,0:T(8,128)}, u32[]{:S(2)}) copy-start(s32[16,512]{1,0:T(8,128)} %copy-done.12) | copy-start | bytes 98308
  469.3 46.0 %copy-start.15 = (s32[16,512]{1,0:T(8,128)S(1)}, s32[16,512]{1,0:T(8,128)}, u32[]{:S(2)}) copy-start(s32[16,512]{1,0:T(8,128)} %copy-done.14) | copy-start | bytes 98308
  469.3 46.0 %copy-start.29 = (pred[16,512]{1,0:T(8,128)(4,1)S(1)}, pred[16,512]{1,0:T(8,128)(4,1)}, u32[]{:S(2)}) copy-start(pred[16,512]{1,0:T(8,128)(4,1)} %copy-done.28) | copy-start | bytes 24580
  469.3 46.0 %copy-start.35 = (s32[512]{0:T(512)S(1)}, s32[512]{0:T(512)}, u32[]{:S(2)}) copy-start(s32[512]{0:T(512)} %copy-done.34) | copy-start | bytes 6148
  469.3 46.0 %copy-start.37 = (s32[512]{0:T(512)S(1)}, s32[512]{0:T(512)}, u32[]{:S(2)}) copy-start(s32[512]{0:T(512)} %copy-done.36) | copy-start | bytes 6148
  (46 other events, 112.6 us)
Sparse Core Ops, SparseCore 0:
  10.4 67.6 all-gather.4
  380.0 132.1 reduce-scatter.1

commit v3 on v2

--- a/solution.py
+++ b/solution.py
@@ -57,14 +57,14 @@
 CUBE_BITS = 3
 PARTS = 3
 VOCAB_TILE = 256
-STAT_ROWS = 8
+STAT_ROWS = 4
 MESH_ID = pl.DeviceIdType.MESH
 PAD_LOGIT = -1e30
 
 
 def head_kernel(vocab_rows, chunks, z_hbm, table_ref, lab_ref, dz_ref, dtable_ref, loss_ref,
-                zbuf, lbuf, gbuf, dzbuf, got_core, got_one, got_two, got_three, stats, norm,
-                local_sem, ag_send, ag_recv, rs_send, rs_recv, st_send, st_recv):
+                zbuf, lbuf, gbuf, dzbuf, got_core, got_one, got_two, got_three, stats, labs, norm,
+                local_sem, ag_send, ag_recv, rs_send, rs_recv, st_send, st_recv, lab_send, lab_recv):
     me = lax.axis_index('fsdp')
     total = 16
     core = lax.rem(me, 2)
@@ -87,6 +87,7 @@
     own.start()
     dtable_ref[...] = jnp.zeros_like(dtable_ref)
     loss_ref[...] = jnp.zeros_like(loss_ref)
+    labs[me] = jnp.zeros((1, half), jnp.float32)
     own.wait()
     pl.semaphore_wait(barrier, total - 1)
 
@@ -116,9 +117,9 @@
         return copies
 
     def reduce_copies(chunk, phase):
-        slot = lax.rem(chunk, 2)
+        slot, dzs = lax.rem(chunk, 2), lax.rem(chunk, 3)
         if phase == 0:
-            return [pltpu.make_async_remote_copy(dzbuf.at[slot, :, :, :, 1 - core], got_core.at[slot], rs_send.at[chunk, 9], rs_recv.at[chunk, 9],
+            return [pltpu.make_async_remote_copy(dzbuf.at[dzs, :, :, :, 1 - core], got_core.at[slot], rs_send.at[chunk, 9], rs_recv.at[chunk, 9],
                                                  device_id=(core_peer,), device_id_type=MESH_ID)]
         copies = []
         for part in range(PARTS):
@@ -128,7 +129,7 @@
             iz, iy, ix = where(fixed)
             got = (got_one, got_two, got_three)[phase - 1]
             sem = (phase - 1) * PARTS + part
-            copies.append(pltpu.make_async_remote_copy(dzbuf.at[slot, iz, iy, ix, core, :, cols(part)], got.at[slot, part],
+            copies.append(pltpu.make_async_remote_copy(dzbuf.at[dzs, iz, iy, ix, core, :, cols(part)], got.at[slot, part],
                                                        rs_send.at[chunk, sem], rs_recv.at[chunk, sem],
                                                        device_id=(peer(order[phase - 1]),), device_id_type=MESH_ID))
         return copies
@@ -142,9 +143,9 @@
             copy.wait()
 
     def reduce_add(chunk, phase):
-        slot = lax.rem(chunk, 2)
+        slot, dzs = lax.rem(chunk, 2), lax.rem(chunk, 3)
         if phase == 0:
-            dzbuf[slot, :, :, :, core] += got_core[slot]
+            dzbuf[dzs, :, :, :, core] += got_core[slot]
             return
         for part in range(PARTS):
             order = axes(part)
@@ -153,9 +154,9 @@
             lanes = slice(part * part_cols, (part + 1) * part_cols)
             if phase == 3:
                 rows = pl.ds(pl.multiple_of(chunk * UNIT, UNIT), UNIT)
-                dz_ref[rows, lanes] = dzbuf[slot, iz, iy, ix, core, :, lanes] + got[slot, part]
+                dz_ref[rows, lanes] = dzbuf[dzs, iz, iy, ix, core, :, lanes] + got[slot, part]
             else:
-                dzbuf[slot, iz, iy, ix, core, :, lanes] += got[slot, part]
+                dzbuf[dzs, iz, iy, ix, core, :, lanes] += got[slot, part]
 
     def stat_copies(chunk):
         copies = []
@@ -165,6 +166,10 @@
                                                        device_id=(to,), device_id_type=MESH_ID))
         return copies
 
+    def lab_copies():
+        return [pltpu.make_async_remote_copy(labs.at[me], labs.at[me], lab_send.at[step], lab_recv.at[step],
+                                             device_id=(lax.rem(me + step, total),), device_id_type=MESH_ID) for step in range(1, total)]
+
     def label_row(chunk, part):
         lab = lab_ref[pl.ds(chunk * 2 + part, 1), :] - base
         return jnp.where(lab < vocab_rows, lab, -1)
@@ -175,7 +180,7 @@
         slot = lax.rem(chunk, 2)
         zb = zbuf[chunk, part].reshape(half, dim)
         lab = label_row(chunk, part)
-        tops, sums, labs = [], [], []
+        tops, sums, hits = [], [], []
         for tile in range(tiles):
             rows = slice(tile * VOCAB_TILE, (tile + 1) * VOCAB_TILE)
             logits = lax.dot_general(table_ref[rows, :], zb, COLS_DIMS, preferred_element_type=jnp.float32)
@@ -185,22 +190,21 @@
             top = jnp.max(logits, axis=0, keepdims=True)
             tops.append(top)
             sums.append(jnp.sum(jnp.exp(logits - top), axis=0, keepdims=True))
-            labs.append(jnp.sum(jnp.where(row_ids == lab - tile * VOCAB_TILE, logits, 0.0), axis=0, keepdims=True))
+            hits.append(jnp.sum(jnp.where(row_ids == lab - tile * VOCAB_TILE, logits, 0.0), axis=0, keepdims=True))
         top = functools.reduce(jnp.maximum, tops)
         exp_sum = sum(s * jnp.exp(t - top) for s, t in zip(sums, tops))
         stats[chunk, me, part:part + 1, :] = top
         stats[chunk, me, 2 + part:3 + part, :] = exp_sum
-        stats[chunk, me, 4 + part:5 + part, :] = sum(labs)
+        labs[me] += sum(hits)
 
     def combine(chunk):
         for part in range(2):
             tops = stats[chunk, :, part, :]
             top = jnp.max(tops, axis=0, keepdims=True)
             exp_sum = jnp.sum(stats[chunk, :, 2 + part, :] * jnp.exp(tops - top), axis=0, keepdims=True)
-            lab = jnp.sum(stats[chunk, :, 4 + part, :], axis=0, keepdims=True)
             norm[part:part + 1, :] = top
             norm[2 + part:3 + part, :] = 1.0 / exp_sum
-            loss_ref[part:part + 1, :] += top + jnp.log(exp_sum) - lab
+            loss_ref[part:part + 1, :] += top + jnp.log(exp_sum)
 
     def table_half(chunk, which):
         slot = lax.rem(chunk, 2)
@@ -215,86 +219,78 @@
             dtable_ref[rows, :] += jnp.dot(gbuf[rows, :], zc, preferred_element_type=jnp.float32)
 
     def token_half(chunk, part):
-        slot = lax.rem(chunk, 2)
         dz = lax.dot_general(gbuf[:, part * half:(part + 1) * half], table_ref[...], ROWS_DIMS, preferred_element_type=jnp.float32)
-        dzbuf[slot, part] = dz.reshape(2, 2, 2, UNIT, dim)
-
-    for phase in range(1, 5):
-        first = gather_copies(0, phase)
-        start(first)
-        finish(first)
+        dzbuf[lax.rem(chunk, 3), part] = dz.reshape(2, 2, 2, UNIT, dim)
+
+    start(gather_copies(0, 1))
+    start(gather_copies(1, 1))
+    start(gather_copies(2, 1))
+    for chunk in range(3):
+        finish(gather_copies(chunk, 1))
+        start(gather_copies(chunk, 2))
+    for chunk in range(2):
+        finish(gather_copies(chunk, 2))
+        start(gather_copies(chunk, 3))
+    finish(gather_copies(0, 3))
+    start(gather_copies(0, 4))
+    finish(gather_copies(0, 4))
 
     def body(i, carry):
-        fwd = i < chunks
-        more = i < chunks - 1
-        bwd = (i >= 1) & (i <= chunks)
-        red = (i >= 2) & (i <= chunks + 1)
-        last = i >= 3
-        nxt = jnp.minimum(i + 1, chunks - 1)
-        prev = jnp.maximum(i - 1, 0)
-        old = jnp.maximum(i - 2, 0)
-        older = jnp.maximum(i - 3, 0)
-
-        pl.when(red)(lambda: start(reduce_copies(old, 0)))
-        pl.when(more)(lambda: start(gather_copies(nxt, 1)))
-        pl.when(fwd)(lambda: forward_half(i, 0))
-
-        @pl.when(last)
+        def inside(offset, action):
+            chunk = i + offset
+            pl.when((chunk >= 0) & (chunk < chunks))(lambda: action(jnp.clip(chunk, 0, chunks - 1)))
+
+        def step_reduce(phase, follow):
+            def action(chunk):
+                finish(reduce_copies(chunk, phase))
+                reduce_add(chunk, phase)
+                if follow:
+                    start(reduce_copies(chunk, phase + 1))
+            return action
+
+        def step_gather(phase):
+            def action(chunk):
+                finish(gather_copies(chunk, phase))
+                start(gather_copies(chunk, phase + 1))
+            return action
+
+        inside(-4, step_reduce(2, True))
+        inside(-2, lambda chunk: start(reduce_copies(chunk, 0)))
+        inside(1, step_gather(3))
+        inside(3, lambda chunk: start(gather_copies(chunk, 1)))
+        inside(2, step_gather(2))
+
+        @pl.when(i < chunks)
         def _():
-            finish(reduce_copies(older, 3))
-            reduce_add(older, 3)
-
-        @pl.when(red)
+            forward_half(i, 0)
+            forward_half(i, 1)
+
+        inside(-2, step_reduce(0, False))
+        inside(-3, step_reduce(1, True))
+        inside(-4, step_reduce(3, False))
+        inside(3, step_gather(1))
+        inside(1, lambda chunk: finish(gather_copies(chunk, 4)))
+        inside(-2, lambda chunk: start(reduce_copies(chunk, 1)))
+        inside(0, lambda chunk: start(stat_copies(chunk)))
+
+        @pl.when(i == chunks - 1)
         def _():
-            finish(reduce_copies(old, 0))
-            reduce_add(old, 0)
-            start(reduce_copies(old, 1))
-
-        @pl.when(more)
-        def _():
-            finish(gather_copies(nxt, 1))
-            start(gather_copies(nxt, 2))
-        pl.when(fwd)(lambda: forward_half(i, 1))
-
-        @pl.when(more)
-        def _():
-            finish(gather_copies(nxt, 2))
-            start(gather_copies(nxt, 3))
-
-        @pl.when(bwd)
-        def _():
-            finish(stat_copies(prev))
-            combine(prev)
-            table_half(prev, 0)
-
-        pl.when(fwd)(lambda: start(stat_copies(i)))
-
-        @pl.when(more)
-        def _():
-            finish(gather_copies(nxt, 3))
-            start(gather_copies(nxt, 4))
-        pl.when(bwd)(lambda: table_half(prev, 1))
-
-        @pl.when(red)
-        def _():
-            finish(reduce_copies(old, 1))
-            reduce_add(old, 1)
-            start(reduce_copies(old, 2))
-
-        @pl.when(bwd)
-        def _():
-            token_half(prev, 0)
-            token_half(prev, 1)
-
-        @pl.when(red)
-        def _():
-            finish(reduce_copies(old, 2))
-            reduce_add(old, 2)
-            start(reduce_copies(old, 3))
-        pl.when(more)(lambda: finish(gather_copies(nxt, 4)))
+            start(lab_copies())
+
+        def backward(chunk):
+            finish(stat_copies(chunk))
+            combine(chunk)
+            table_half(chunk, 0)
+            table_half(chunk, 1)
+            token_half(chunk, 0)
+            token_half(chunk, 1)
+
+        inside(-1, backward)
         return carry
 
-    lax.fori_loop(0, chunks + 3, body, 0)
+    lax.fori_loop(0, chunks + 4, body, 0)
+    finish(lab_copies())
+    loss_ref[2:3, :] = -jnp.sum(labs[...], axis=0)
 
 
 def head(z_local, table_padded, lab_rows, vocab_rows):
@@ -313,21 +309,23 @@
         out_specs=[vmem, vmem, vmem],
         out_shape=[jax.ShapeDtypeStruct((tokens, dim), f32),
                    jax.ShapeDtypeStruct((padded, dim), f32),
-                   jax.ShapeDtypeStruct((2, 8 * UNIT), f32)],
+                   jax.ShapeDtypeStruct((3, 8 * UNIT), f32)],
         scratch_shapes=[pltpu.VMEM((chunks, 2, 2, 2, 2, UNIT, dim), bf16),
                         pltpu.VMEM((2, padded, chunk_tokens), f32),
                         pltpu.VMEM((padded, chunk_tokens), bf16),
-                        pltpu.VMEM((2, 2, 2, 2, 2, UNIT, dim), f32),
+                        pltpu.VMEM((3, 2, 2, 2, 2, UNIT, dim), f32),
                         pltpu.VMEM((2, 2, 2, 2, UNIT, dim), f32),
                         pltpu.VMEM((2, PARTS, 2, 2, UNIT, part_cols), f32),
                         pltpu.VMEM((2, PARTS, 2, UNIT, part_cols), f32),
                         pltpu.VMEM((2, PARTS, UNIT, part_cols), f32),
                         pltpu.VMEM((chunks, 16, STAT_ROWS, 8 * UNIT), f32),
+                        pltpu.VMEM((16, 1, 8 * UNIT), f32),
                         pltpu.VMEM((8, 8 * UNIT), f32),
                         sems(()),
                         sems((chunks, 10)), sems((chunks, 10)),
                         sems((chunks, 10)), sems((chunks, 10)),
-                        sems((chunks, 16)), sems((chunks, 16))],
+                        sems((chunks, 16)), sems((chunks, 16)),
+                        sems((16,)), sems((16,))],
         compiler_params=pltpu.CompilerParams(vmem_limit_bytes=67043328, collective_id=1, has_side_effects=True),
         cost_estimate=pl.CostEstimate(flops=cost, bytes_accessed=4 * padded * dim, transcendentals=2 * tokens * 16 * padded),
         name="head_all",

time: 533 us -> 457 us (0.86)
  Pallas kernels: 239 us -> 164 us
    pallas_call x1, Pallas kernels: 239 us -> 164 us  [head(): pl.pallas_call(functools.partial(head_kernel, vocab_rows, chunks), in_spe...]
  transfers between devices with their start and end apart: 4 -> 4, of which waited for: 4 -> 4; matrix products, arithmetic and copies ran while one was open for 9% -> 10% of each run, Pallas kernels for 0% -> 0%
where the time goes in v3:
time: 457 us; the launch traced here: 449 us
  Pallas kernels  164 us (36%)
  waiting for transfers between devices  127 us (28%)
  matrix products  60.6 us (13%)
  local copies, waits for them, and re-layouts  34.4 us (8%)
  other arithmetic  21.7 us (5%)
  between operations  19.5 us (4%)
  blocking collectives  15 us (3%)
  starting transfers between devices  6.36 us (1%)
    pallas_call x1, Pallas kernels, head(): pl.pallas_call(functools.partial(head_kernel, vocab_rows, chunks), in_spe...  164 us
    all_to_all x1, waiting for transfers between devices, return_round(): lax.all_to_all(send.reshape(groups, SLOTS, dim), 'fsdp', 0, 0)  55 us
    reduce_scatter x1, waiting for transfers between devices, device_step(): w_grad = lax.psum_scatter(w_grads, 'fsdp', scatter_dimension=0, tiled=False)  41.3 us
    all_to_all x1, waiting for transfers between devices, fetch_round(): lax.all_to_all(send.reshape(groups, SLOTS, dim), 'fsdp', 0, 0)  21.4 us
    dot_general x6, matrix products, pick_rows(): term = jnp.dot(select, part, preferred_element_type=jnp.float32)  18.5 us
    all_gather x1, blocking collectives, device_step(): packed_all = lax.all_gather(packed, 'fsdp', axis=0, tiled=False)  15 us
  transfers between devices with their start and end apart: 4, of which 4 were waited for; matrix products, arithmetic and copies ran while one was open for 10% of the time, Pallas kernels for 0%

profile of v3, /device:TPU:0, one launch (start us, length us, event | category | flops | bytes accessed | tf_op | source)
XLA Modules:
  0.0 449.2 jit_solution(905253712020817308)
XLA Ops:
  10.5 15.0 %all-gather.2 = s32[16,2,512]{2,1,0:T(2,128)S(1)} all-gather(s32[1,2,512]{2,1,0:T(2,128)S(1)} %add_bitcast_fusion.1), channel_id=2, replica_groups=mesh['fsdp'=16] {'fsdp'}, dimensions={0}, use_global_device_ids=true | all-gather | bytes 69632 | tf_op jit(solution)/shard_map/all_gather | solution.py:363
  26.9 6.8 %fusion.70 = bf16[1024,768]{1,0:T(8,128)(2,1)} fusion(bf16[2008,768]{1,0:T(8,128)(2,1)} %param.14, s32[1024]{0:T(1024)S(1)} %sub.112), kind=kOutput, calls=%fused_computation.121 | convolution fusion | flops 3161153536 | bytes 4661248 | tf_op jit(solution)/shard_map/dot_general | solution.py:396
  33.7 2.5 all-to-all-start.2
  39.5 3.8 pad.4.table_ref
  44.7 21.4 %all-to-all-done.2 = bf16[16,64,768]{2,1,0:T(8,128)(2,1)S(1)} async-done(((bf16[16,64,768]{2,1,0:T(8,128)(2,1)}), bf16[16,64,768]{2,1,0:T(8,128)(2,1)S(1)}, u32[]{:S(2)}, u32[]{:S(2)}) %all-to-all-start.2) | async-done | bytes 1572896 | tf_op jit(solution)/shard_map/all_to_all | solution.py:397
  69.3 8.9 %all-gather.5.cloned.1.call-done = bf16[2304,2048]{1,0:T(8,128)(2,1)} async-done(((bf16[144,2048]{1,0:T(8,128)(2,1)}), bf16[2304,2048]{1,0:T(8,128)(2,1)}) %all-gather.5.cloned.1.call-update) | async-done | bytes 9437200 | tf_op jit(solution)/shard_map/all_gather | solution.py:368
  78.2 6.1 %fusion.132 = (bf16[16,48,2048]{2,1,0:T(8,128)(2,1)}, bf16[16,48,2048]{2,1,0:T(8,128)(2,1)S(1)}, bf16[16,48,2048]{2,1,0:T(8,128)(2,1)}) fusion(bf16[16,144,2048]{2,1,0:T(8,128)(2,1)} %bitcast.147), kind=kLoop, calls=%fused_computation.248 | loop fusion | bytes 18874368 | tf_op jit(solution)/shard_map/slice | solution.py:371
  84.3 7.0 %reshape_reshape.6 = bf16[2048,768]{1,0:T(8,128)(2,1)} reshape(bf16[16,48,2048]{2,1,0:T(8,128)(2,1)} %get-tuple-element.383) | data formatting | bytes 6291456 | tf_op jit(solution)/shard_map/reshape;reshape | solution.py:371
  91.3 2.9 convolution_convert_fusion.3
  105.3 163.7 %head_all.1 = (f32[512,768]{1,0:T(8,128)}, f32[2048,768]{1,0:T(8,128)}, f32[3,512]{1,0:T(4,128)}) custom-call(bf16[8,64,768]{2,1,0:T(8,128)(2,1)} %bitcast.154, bf16[2048,768]{1,0:T(8,128)(2,1)} %pad.4.table_ref, s32[16,512]{1,0:T(8,128)} %reshape.280.lab_ref), custom_call_target="tpu_custom_call" | custom-call | flops 77309411328 | bytes 6291456 | tf_op jit(solution)/shard_map/head_all/pallas_call | solution.py:306
  273.1 4.5 fusion.52
  277.6 4.5 fusion.61
  284.5 7.9 %reshape_reshape.7 = f32[16,48,2048]{2,1,0:T(8,128)} reshape(f32[2048,768]{1,0:T(8,128)} %fusion.61) | data formatting | bytes 12582912 | tf_op jit(solution)/shard_map/reshape;reshape | solution.py:434
  292.4 3.5 fusion.57
  297.7 6.9 %pad_maximum_fusion = f32[16,144,2048]{2,1,0:T(8,128)} fusion(f32[16,48,2048]{2,1,0:T(8,128)S(1)} %bitcast.139, f32[16,48,2048]{2,1,0:T(8,128)S(1)} %bitcast.140, f32[16,48,2048]{2,1,0:T(8,128)S(1)} %bitcast.141), kind=kLoop, calls=%fused_computation.42 | loop fusion | flops 9437184 | bytes 37748736 | tf_op jit(solution)/shard_map/concatenate | solution.py:433
  304.7 3.4 fusion.135
  316.4 2.8 add_add_fusion.3
  319.2 3.8 all-to-all-start.3
  324.3 55.0 %all-to-all-done.3 = f32[16,64,768]{2,1,0:T(8,128)} async-done(((f32[16,64,768]{2,1,0:T(8,128)}), f32[16,64,768]{2,1,0:T(8,128)}, u32[]{:S(2)}, u32[]{:S(2)}) %all-to-all-start.3) | async-done | bytes 3145760 | tf_op jit(solution)/shard_map/all_to_all | solution.py:404
  379.2 2.6 reduce-precision_convert_fusion.3
  381.9 3.8 fusion.25
  385.7 3.9 fusion.26
  389.6 5.9 %add_add_fusion.2 = f32[2008,768]{1,0:T(8,128)} fusion(f32[2008,768]{1,0:T(8,128)S(1)} %fusion.25, f32[2008,768]{1,0:T(8,128)S(1)} %fusion.26, f32[2048,768]{1,0:T(8,128)S(1)} %bitcast.166, bf16[1024,768]{1,0:T(8,128)(2,1)S(1)} %get-tuple-element.386, s32[1024]{0:T(1024)S(1)} %copy-done.57), kind=kOutput, calls=%fused_computation.49 | convolution fusion | flops 3164993536 | bytes 26251264 | tf_op jit(solution)/shard_map/dot_general | solution.py:346
  395.5 41.3 %reduce-scatter.2.cloned.1.call-done = f32[1,144,2048]{2,1,0:T(8,128)} async-done(((f32[16,144,2048]{2,1,0:T(8,128)}), f32[1,144,2048]{2,1,0:T(8,128)}) %reduce-scatter.2.cloned.1.call-update) | async-done | bytes 1179664 | tf_op jit(solution)/shard_map/reduce_scatter | solution.py:435
  (194 shorter events, 41.9 us)
Async XLA Ops:
  7.2 71.0 %all-gather.5.cloned.1.call-start = ((), (), s32[]{:S(2)}) async-start(), calls=%async_computation.6 | async-start | bytes 10027008 | tf_op jit(solution)/shard_map/all_gather | solution.py:368
  26.9 6.8 %copy-start.56 = (s32[1024]{0:T(1024)}, s32[1024]{0:T(1024)S(1)}, u32[]{:S(2)}) copy-start(s32[1024]{0:T(1024)S(1)} %sub.112) | copy-start | bytes 12292
  33.7 32.5 %all-to-all-start.2 = ((bf16[16,64,768]{2,1,0:T(8,128)(2,1)}), bf16[16,64,768]{2,1,0:T(8,128)(2,1)S(1)}, u32[]{:S(2)}, u32[]{:S(2)}) async-start(bf16[16,64,768]{2,1,0:T(8,128)(2,1)} %bitcast.153), calls=%async_computation.2 | async-start | bytes 3145728 | tf_op jit(solution)/shard_map/all_to_all | solution.py:397
  36.2 400.6 %reduce-scatter.2.cloned.1.call-start = ((), (), s32[]{:S(2)}) async-start(), calls=%async_computation.5 | async-start | bytes 20054016 | tf_op jit(solution)/shard_map/reduce_scatter | solution.py:435
  67.5 10.7 %copy-start.5 = (bf16[512,768]{1,0:T(8,128)(2,1)}, bf16[512,768]{1,0:T(8,128)(2,1)S(1)}, u32[]{:S(2)}) copy-start(bf16[512,768]{1,0:T(8,128)(2,1)S(1)} %get-tuple-element.280) | copy-start | bytes 2359300
  67.5 10.7 %copy-start.12 = (s32[16,512]{1,0:T(8,128)}, s32[16,512]{1,0:T(8,128)S(1)}, u32[]{:S(2)}) copy-start(s32[16,512]{1,0:T(8,128)S(1)} %get-tuple-element.641) | copy-start | bytes 98308
  67.5 10.7 %copy-start.14 = (s32[16,512]{1,0:T(8,128)}, s32[16,512]{1,0:T(8,128)S(1)}, u32[]{:S(2)}) copy-start(s32[16,512]{1,0:T(8,128)S(1)} %get-tuple-element.642) | copy-start | bytes 98308
  67.5 10.7 %copy-start.28 = (pred[16,512]{1,0:T(8,128)(4,1)}, pred[16,512]{1,0:T(8,128)(4,1)S(1)}, u32[]{:S(2)}) copy-start(pred[16,512]{1,0:T(8,128)(4,1)S(1)} %get-tuple-element.649) | copy-start | bytes 24580
  67.5 10.7 %copy-start.34 = (s32[512]{0:T(512)}, s32[512]{0:T(512)S(1)}, u32[]{:S(2)}) copy-start(s32[512]{0:T(512)S(1)} %get-tuple-element.650) | copy-start | bytes 6148
  67.5 10.7 %copy-start.36 = (s32[512]{0:T(512)}, s32[512]{0:T(512)S(1)}, u32[]{:S(2)}) copy-start(s32[512]{0:T(512)S(1)} %get-tuple-element.651) | copy-start | bytes 6148
  68.3 9.9 %copy-start.48 = (f32[256]{0:T(256)}, f32[256]{0:T(256)S(1)}, u32[]{:S(2)}) copy-start(f32[256]{0:T(256)S(1)} %get-tuple-element.426) | copy-start | bytes 3076
  68.3 9.9 %copy-start.50 = (f32[256]{0:T(256)}, f32[256]{0:T(256)S(1)}, u32[]{:S(2)}) copy-start(f32[256]{0:T(256)S(1)} %get-tuple-element.412) | copy-start | bytes 3076
  69.3 24.9 %copy-start.16 = (bf16[256,768]{1,0:T(8,128)(2,1)}, bf16[256,768]{1,0:T(8,128)(2,1)S(1)}, u32[]{:S(2)}) copy-start(bf16[256,768]{1,0:T(8,128)(2,1)S(1)} %get-tuple-element.401) | copy-start | bytes 1179652
  84.3 15.8 %copy-start.3 = (bf16[16,48,2048]{2,1,0:T(8,128)(2,1)}, bf16[16,48,2048]{2,1,0:T(8,128)(2,1)S(1)}, u32[]{:S(2)}) copy-start(bf16[16,48,2048]{2,1,0:T(8,128)(2,1)S(1)} %get-tuple-element.384) | copy-start | bytes 9437188
  98.2 5.9 %copy-start.8 = (bf16[256,768]{1,0:T(8,128)(2,1)}, bf16[256,768]{1,0:T(8,128)(2,1)S(1)}, u32[]{:S(2)}) copy-start(bf16[256,768]{1,0:T(8,128)(2,1)S(1)} %get-tuple-element.420) | copy-start | bytes 1179652
  292.4 5.4 %slice-start = ((s8[6291456]{0:T(1024)(128)(4,1)}), s8[4194304]{0:T(1024)(128)(4,1)S(1)}, s32[]{:S(2)}) async-start(s8[6291456]{0:T(1024)(128)(4,1)} %bitcast.138), calls=%async_computation.7 | async-start | bytes 8388608
  319.2 60.0 %all-to-all-start.3 = ((f32[16,64,768]{2,1,0:T(8,128)}), f32[16,64,768]{2,1,0:T(8,128)}, u32[]{:S(2)}, u32[]{:S(2)}) async-start(f32[16,64,768]{2,1,0:T(8,128)} %bitcast.146), calls=%async_computation.3 | async-start | bytes 6291456 | tf_op jit(solution)/shard_map/all_to_all | solution.py:404
  324.3 57.6 %copy-start.57 = (s32[1024]{0:T(1024)S(1)}, s32[1024]{0:T(1024)}, u32[]{:S(2)}) copy-start(s32[1024]{0:T(1024)} %copy-done.56) | copy-start | bytes 12292
  381.9 7.7 %slice-start.4 = ((s8[6291456]{0:T(1024)(128)(4,1)}), s8[4194304]{0:T(1024)(128)(4,1)S(1)}, s32[]{:S(2)}) async-start(s8[6291456]{0:T(1024)(128)(4,1)} %bitcast.165), calls=%async_computation.11 | async-start | bytes 8388608
  395.5 44.4 %copy-start.13 = (s32[16,512]{1,0:T(8,128)S(1)}, s32[16,512]{1,0:T(8,128)}, u32[]{:S(2)}) copy-start(s32[16,512]{1,0:T(8,128)} %copy-done.12) | copy-start | bytes 98308
  395.5 44.4 %copy-start.15 = (s32[16,512]{1,0:T(8,128)S(1)}, s32[16,512]{1,0:T(8,128)}, u32[]{:S(2)}) copy-start(s32[16,512]{1,0:T(8,128)} %copy-done.14) | copy-start | bytes 98308
  395.5 44.4 %copy-start.29 = (pred[16,512]{1,0:T(8,128)(4,1)S(1)}, pred[16,512]{1,0:T(8,128)(4,1)}, u32[]{:S(2)}) copy-start(pred[16,512]{1,0:T(8,128)(4,1)} %copy-done.28) | copy-start | bytes 24580
  395.5 44.4 %copy-start.35 = (s32[512]{0:T(512)S(1)}, s32[512]{0:T(512)}, u32[]{:S(2)}) copy-start(s32[512]{0:T(512)} %copy-done.34) | copy-start | bytes 6148
  395.5 44.4 %copy-start.37 = (s32[512]{0:T(512)S(1)}, s32[512]{0:T(512)}, u32[]{:S(2)}) copy-start(s32[512]{0:T(512)} %copy-done.36) | copy-start | bytes 6148
  (46 other events, 112.5 us)
Sparse Core Ops, SparseCore 0:
  10.4 67.6 all-gather.4
  304.8 131.9 reduce-scatter.1

commit v4 on v3

--- a/solution.py
+++ b/solution.py
@@ -332,6 +332,163 @@
     )(z_local.reshape(chunks, UNIT, dim), table_padded, lab_rows)
 
 
+PIECES = 4
+
+
+def axes(part):
+    return part % 3, (part + 1) % 3, (part + 2) % 3
+
+
+def cube_index(choice):
+    return choice.get(2, slice(None)), choice.get(1, slice(None)), choice.get(0, slice(None))
+
+
+def tail_kernel(table_rows, gate_hbm, up_hbm, down_hbm, send_hbm, row_ref, dtable_hbm, gate_out, up_out, down_out, dtable_out,
+                acc_g, acc_u, acc_d, core_g, core_u, core_d, one_g, one_u, one_d, two_g, two_u, two_d, three_g, three_u, three_d,
+                rows_got, split, local_sem, send_sem, recv_sem, row_send, row_recv):
+    me = lax.axis_index('fsdp')
+    total = 16
+    core = lax.rem(me, 2)
+    pos = [lax.rem(me // 2, 2), lax.rem(me // 4, 2), me // 8]
+    core_peer = me + 1 - 2 * core
+    whole = (gate_hbm, up_hbm, down_hbm)
+    accs = (acc_g, acc_u, acc_d)
+    gots = ((core_g, core_u, core_d), (one_g, one_u, one_d), (two_g, two_u, two_d), (three_g, three_u, three_d))
+    outs = (gate_out, up_out, down_out)
+
+    barrier = pltpu.get_barrier_semaphore()
+    for step in range(1, total):
+        pl.semaphore_signal(barrier, inc=1, device_id=(lax.rem(me + step, total),), device_id_type=MESH_ID)
+    loads = [pltpu.make_async_copy(whole[part].at[:, :, :, core], accs[part], local_sem.at[part]) for part in range(3)]
+    loads.append(pltpu.make_async_copy(dtable_hbm.at[pl.ds(0, table_rows)], dtable_out, local_sem.at[3]))
+    loads.append(pltpu.make_async_copy(send_hbm.at[me], rows_got.at[me], local_sem.at[4]))
+    for load in loads:
+        load.start()
+    pl.semaphore_wait(barrier, total - 1)
+
+    def piece(part, q):
+        if part == 2:
+            size = acc_d.shape[3] // PIECES
+            return pl.ds(q * size, size), slice(None)
+        size = acc_g.shape[4] // PIECES
+        return slice(None), pl.ds(q * size, size)
+
+    def copies(phase, q):
+        made = []
+        for part in range(3):
+            rows, lanes = piece(part, q)
+            order = axes(part)
+            if phase == 0:
+                src = whole[part].at[:, :, :, 1 - core, rows, lanes]
+                dst = gots[0][part].at[:, :, :, rows, lanes]
+                to = core_peer
+            else:
+                fixed = {axis: pos[axis] for axis in order[:phase - 1]}
+                fixed[order[phase - 1]] = 1 - pos[order[phase - 1]]
+                iz, iy, ix = cube_index(fixed)
+                src = accs[part].at[iz, iy, ix, rows, lanes]
+                lead = (slice(None),) * (3 - phase)
+                dst = gots[phase][part].at[lead + (rows, lanes)]
+                axis = order[phase - 1]
+                to = me + (1 - 2 * pos[axis]) * (2 << axis)
+            made.append(pltpu.make_async_remote_copy(src, dst, send_sem.at[phase, part, q], recv_sem.at[phase, part, q],
+                                                     device_id=(to,), device_id_type=MESH_ID))
+        return made
+
+    def start(made):
+        for copy in made:
+            copy.start()
+
+    def finish_add(phase, q):
+        for copy in copies(phase, q):
+            copy.wait()
+        for part in range(3):
+            rows, lanes = piece(part, q)
+            iz, iy, ix = cube_index({axis: pos[axis] for axis in axes(part)[:phase]})
+            got = gots[phase][part][(slice(None),) * (3 - phase) + (rows, lanes)]
+            if phase == 3:
+                outs[part][rows, lanes] = accs[part][iz, iy, ix, rows, lanes] + got
+            else:
+                accs[part][iz, iy, ix, rows, lanes] += got
+
+    row_copies = []
+    for step in range(1, total):
+        to = lax.rem(me + step, total)
+        row_copies.append(pltpu.make_async_remote_copy(send_hbm.at[to], rows_got.at[me], row_send.at[step], row_recv.at[step],
+                                                       device_id=(to,), device_id_type=MESH_ID))
+    for q in range(PIECES):
+        start(copies(0, q))
+    start(row_copies)
+    for load in loads:
+        load.wait()
+    for q in range(PIECES):
+        finish_add(0, q)
+        start(copies(1, q))
+    for copy in row_copies:
+        copy.wait()
+    slots, dim = rows_got.shape[0] * rows_got.shape[1], rows_got.shape[2]
+
+    def split_rows(s, carry):
+        vals = rows_got[s]
+        at = pl.multiple_of(s * SLOTS, SLOTS)
+        high = vals.astype(jnp.bfloat16)
+        rest = vals - high.astype(jnp.float32)
+        mid = rest.astype(jnp.bfloat16)
+        split[pl.ds(at, SLOTS), :] = high
+        split[pl.ds(slots + at, SLOTS), :] = mid
+        split[pl.ds(2 * slots + at, SLOTS), :] = (rest - mid.astype(jnp.float32)).astype(jnp.bfloat16)
+        return carry
+
+    lax.fori_loop(0, total, split_rows, 0)
+
+    def add_rows(first, count):
+        ids = lax.broadcasted_iota(jnp.int32, (count, slots), 0) + first
+        hot = jnp.where(ids == row_ref[...], 1.0, 0.0).astype(jnp.bfloat16)
+        dtable_out[pl.ds(first, count), :] += jnp.dot(jnp.concatenate([hot, hot, hot], axis=1), split[...], preferred_element_type=jnp.float32)
+
+    full = table_rows // VOCAB_TILE
+
+    def add_tile(tile, carry):
+        add_rows(pl.multiple_of(tile * VOCAB_TILE, VOCAB_TILE), VOCAB_TILE)
+        return carry
+
+    lax.fori_loop(0, full, add_tile, 0)
+    if table_rows % VOCAB_TILE:
+        add_rows(full * VOCAB_TILE, table_rows % VOCAB_TILE)
+
+    for q in range(PIECES + 2):
+        if q < PIECES:
+            finish_add(1, q)
+            start(copies(2, q))
+        if 1 <= q <= PIECES:
+            finish_add(2, q - 1)
+            start(copies(3, q - 1))
+        if q >= 2:
+            finish_add(3, q - 2)
+
+
+def tail(grad_gate, grad_up, grad_down, send, row_idx, dtable, table_rows):
+    f32 = jnp.float32
+    vmem = pl.BlockSpec(memory_space=pltpu.VMEM)
+    anywhere = pl.BlockSpec(memory_space=pl.ANY)
+    sems = pltpu.SemaphoreType.DMA
+    blocks = [tuple(array.shape[4:]) for array in (grad_gate, grad_up, grad_down)]
+    scratch = [pltpu.VMEM(lead + block, f32) for lead in ((2, 2, 2), (2, 2, 2), (2, 2), (2,), ()) for block in blocks]
+    slots = send.shape[0] * send.shape[1]
+    dim = send.shape[2]
+    return pl.pallas_call(
+        functools.partial(tail_kernel, table_rows),
+        in_specs=[anywhere, anywhere, anywhere, anywhere, vmem, anywhere],
+        out_specs=[vmem] * 4,
+        out_shape=[jax.ShapeDtypeStruct(block, f32) for block in blocks] + [jax.ShapeDtypeStruct((table_rows, dim), f32)],
+        scratch_shapes=scratch + [pltpu.VMEM(send.shape, f32), pltpu.VMEM((3 * slots, dim), jnp.bfloat16),
+                                  sems((5,)), sems((4, 3, PIECES)), sems((4, 3, PIECES)), sems((16,)), sems((16,))],
+        compiler_params=pltpu.CompilerParams(vmem_limit_bytes=60 * 1024 * 1024, collective_id=2, has_side_effects=True),
+        cost_estimate=pl.CostEstimate(flops=6 * slots * table_rows * dim, bytes_accessed=40 * 1024 * 1024, transcendentals=0),
+        name="tail_all",
+    )(grad_gate, grad_up, grad_down, send, row_idx, dtable)
+
+
 def split3(values):
     high = lax.reduce_precision(values, 8, 7)
     rest = values - high
@@ -398,9 +555,11 @@
             place = (my_slots(round_idx)[:, None] == jnp.arange(groups * SLOTS, dtype=jnp.int32)[None, :]).astype(jnp.bfloat16)
             return jnp.dot(place, got, preferred_element_type=jnp.float32).astype(jnp.bfloat16)
 
+        def slot_place(round_idx):
+            return (jnp.arange(groups * SLOTS, dtype=jnp.int32)[:, None] == my_slots(round_idx)[None, :]).astype(jnp.bfloat16)
+
         def return_round(round_idx, grad_rows):
-            place = (jnp.arange(groups * SLOTS, dtype=jnp.int32)[:, None] == my_slots(round_idx)[None, :]).astype(jnp.bfloat16)
-            send = pick_rows(place, grad_rows)
+            send = pick_rows(slot_place(round_idx), grad_rows)
             got = lax.all_to_all(send.reshape(groups, SLOTS, dim), 'fsdp', 0, 0).reshape(groups * SLOTS, dim)
             select = (jnp.arange(rows, dtype=jnp.int32)[:, None] == owned_rows(round_idx)[None, :]).astype(jnp.bfloat16)
             return pick_rows(select, got)
@@ -419,7 +578,6 @@
         padded = -(-rows // VOCAB_TILE) * VOCAB_TILE
         table_padded = jnp.pad(table_shard, ((0, padded - rows), (0, 0)))
         dz, dtable, loss_rows = head(jnp.concatenate(normed, axis=0), table_padded, lab_rows, rows)
-        dtable = dtable[:rows]
         loss_total = jnp.sum(loss_rows)
         grad_normed = [dz[m * tok_micro:(m + 1) * tok_micro] for m in range(micro_count)]
 
@@ -430,14 +588,12 @@
         grad_down = lax.dot_general(acts, grad_mid, ROWS_DIMS, preferred_element_type=jnp.float32)
         grad_gate = lax.dot_general(normed_in, grad_gate_pre, ROWS_DIMS, preferred_element_type=jnp.float32)
         grad_up = lax.dot_general(normed_in, grad_up_proj, ROWS_DIMS, preferred_element_type=jnp.float32)
-        w_grads = jnp.concatenate([grad_gate.reshape(groups, gate_rows, ffn), grad_up.reshape(groups, gate_rows, ffn),
-                                   grad_down.reshape(groups, down_rows, dim).reshape(groups, gate_rows, ffn)], axis=1)
-        w_grad = lax.psum_scatter(w_grads, 'fsdp', scatter_dimension=0, tiled=False)
-
-        dtable = dtable + return_round(jnp.int32(0), grad_rows)
+        cube = (2, 2, 2, 2)
+        send = pick_rows(slot_place(0), grad_rows).reshape(groups, SLOTS, dim)
+        out_gate, out_up, out_down, dtable = tail(grad_gate.reshape(cube + (gate_rows, ffn)), grad_up.reshape(cube + (gate_rows, ffn)),
+                                                  grad_down.reshape(cube + (down_rows, dim)), send, owned_rows(0).reshape(1, groups * SLOTS), dtable, rows)
         dtable = lax.fori_loop(1, rounds, lambda r, acc: acc + return_round(r, grad_rows), dtable)
-        return (loss_total / total_tokens, dtable, w_grad[:gate_rows], w_grad[gate_rows:2 * gate_rows],
-                w_grad[2 * gate_rows:].reshape(down_rows, dim))
+        return (loss_total / total_tokens, dtable, out_gate, out_up, out_down)
 
     row_spec = P('fsdp', None)
     tok_spec = P(None, 'fsdp', None)

time: 457 us -> 439 us (0.961)
  Pallas kernels: 164 us -> 273 us
  waiting for transfers between devices: 127 us -> 29.7 us
  matrix products: 60.6 us -> 46.2 us
  other arithmetic: 21.7 us -> 12.1 us
    pallas_call x0 -> x1, Pallas kernels: none -> 109 us  [tail(): pl.pallas_call(functools.partial(tail_kernel, table_rows), in_specs=[anyw...]
    all_to_all x1 -> x0, waiting for transfers between devices: 55 us -> none  [return_round(): lax.all_to_all(send.reshape(groups, SLOTS, dim), 'fsdp', 0, 0)]
    reduce_scatter x1 -> x0, waiting for transfers between devices: 41.3 us -> none  [device_step(): w_grad = lax.psum_scatter(w_grads, 'fsdp', scatter_dimension=0, tiled=False)]
    dot_general x6 -> x3, matrix products: 18.5 us -> 4.87 us  [pick_rows(): term = jnp.dot(select, part, preferred_element_type=jnp.float32)]
    another operation x1 -> x0, local copies, waits for them, and re-layouts: 7.85 us -> none  [device_step(): grad_down.reshape(groups, down_rows, dim).reshape(groups, gate_rows, ffn)]
    unnamed x132 -> x122, local copies, waits for them, and re-layouts: 4.31 us -> 11.6 us
    concatenate x1 -> x0, other arithmetic: 6.91 us -> none  [device_step(): jnp.concatenate([grad_gate.reshape(groups, gate_rows, ffn), grad_up.resha...]
  transfers between devices with their start and end apart: 4 -> 2, of which waited for: 4 -> 2; matrix products, arithmetic and copies ran while one was open for 10% -> 4% of each run, Pallas kernels for 0% -> 0%
where the time goes in v4:
time: 439 us; the launch traced here: 431 us
  Pallas kernels  273 us (62%)
  matrix products  46.2 us (11%)
  local copies, waits for them, and re-layouts  31.4 us (7%)
  waiting for transfers between devices  29.7 us (7%)
  between operations  19.6 us (4%)
  blocking collectives  15 us (3%)
  other arithmetic  12.1 us (3%)
    pallas_call x1, Pallas kernels, head(): pl.pallas_call(functools.partial(head_kernel, vocab_rows, chunks), in_spe...  164 us
    pallas_call x1, Pallas kernels, tail(): pl.pallas_call(functools.partial(tail_kernel, table_rows), in_specs=[anyw...  109 us
    all_to_all x1, waiting for transfers between devices, fetch_round(): lax.all_to_all(send.reshape(groups, SLOTS, dim), 'fsdp', 0, 0)  20.9 us
    all_gather x1, blocking collectives, device_step(): packed_all = lax.all_gather(packed, 'fsdp', axis=0, tiled=False)  15 us
    unnamed x122, local copies, waits for them, and re-layouts  11.6 us
  transfers between devices with their start and end apart: 2, of which 2 were waited for; matrix products, arithmetic and copies ran while one was open for 4% of the time, Pallas kernels for 0%

profile of v4, /device:TPU:0, one launch (start us, length us, event | category | flops | bytes accessed | tf_op | source)
XLA Modules:
  0.0 431.5 jit_solution(17336241878195595871)
XLA Ops:
  8.4 1.9 pad_maximum_fusion.3
  10.5 15.0 %all-gather.2 = s32[16,2,512]{2,1,0:T(2,128)S(1)} all-gather(s32[1,2,512]{2,1,0:T(2,128)S(1)} %add_bitcast_fusion.1), channel_id=2, replica_groups=mesh['fsdp'=16] {'fsdp'}, dimensions={0}, use_global_device_ids=true | all-gather | bytes 69632 | tf_op jit(solution)/shard_map/all_gather | solution.py:520
  26.8 6.8 %fusion.63 = bf16[1024,768]{1,0:T(8,128)(2,1)} fusion(bf16[2008,768]{1,0:T(8,128)(2,1)} %param.14, s32[1024]{0:T(1024)S(1)} %sub.108), kind=kOutput, calls=%fused_computation.107 | convolution fusion | flops 3161153536 | bytes 4661248 | tf_op jit(solution)/shard_map/dot_general | solution.py:553
  33.6 2.5 all-to-all-start.2
  40.9 3.8 pad.4.table_ref
  45.2 20.9 %all-to-all-done.2 = bf16[16,64,768]{2,1,0:T(8,128)(2,1)S(1)} async-done(((bf16[16,64,768]{2,1,0:T(8,128)(2,1)}), bf16[16,64,768]{2,1,0:T(8,128)(2,1)S(1)}, u32[]{:S(2)}, u32[]{:S(2)}) %all-to-all-start.2) | async-done | bytes 1572896 | tf_op jit(solution)/shard_map/all_to_all | solution.py:554
  69.4 8.7 %all-gather.5.cloned.1.call-done = bf16[2304,2048]{1,0:T(8,128)(2,1)} async-done(((bf16[144,2048]{1,0:T(8,128)(2,1)}), bf16[2304,2048]{1,0:T(8,128)(2,1)}) %all-gather.5.cloned.1.call-update) | async-done | bytes 9437200 | tf_op jit(solution)/shard_map/all_gather | solution.py:525
  78.2 6.1 %fusion.125 = (bf16[16,48,2048]{2,1,0:T(8,128)(2,1)}, bf16[16,48,2048]{2,1,0:T(8,128)(2,1)S(1)}, bf16[16,48,2048]{2,1,0:T(8,128)(2,1)}) fusion(bf16[16,144,2048]{2,1,0:T(8,128)(2,1)} %bitcast.129), kind=kLoop, calls=%fused_computation.232 | loop fusion | bytes 18874368 | tf_op jit(solution)/shard_map/slice | solution.py:528
  84.3 7.0 %reshape_reshape.4 = bf16[2048,768]{1,0:T(8,128)(2,1)} reshape(bf16[16,48,2048]{2,1,0:T(8,128)(2,1)} %get-tuple-element.391) | data formatting | bytes 6291456 | tf_op jit(solution)/shard_map/reshape;reshape | solution.py:528
  91.3 3.0 convolution_convert_fusion.3
  95.4 2.2 fusion.30
  99.9 2.1 fusion.26
  105.1 163.8 %head_all.1 = (f32[512,768]{1,0:T(8,128)}, f32[2048,768]{1,0:T(8,128)}, f32[3,512]{1,0:T(4,128)}) custom-call(bf16[8,64,768]{2,1,0:T(8,128)(2,1)} %bitcast.141, bf16[2048,768]{1,0:T(8,128)(2,1)} %pad.4.table_ref, s32[16,512]{1,0:T(8,128)} %reshape.280.lab_ref), custom_call_target="tpu_custom_call" | custom-call | flops 77309411328 | bytes 6291456 | tf_op jit(solution)/shard_map/head_all/pallas_call | solution.py:306
  269.0 2.0 fusion.84
  271.7 1.3 copy-done.24
  273.0 3.2 fusion.39
  276.2 4.5 %fusion.54 = f32[2048,768]{1,0:T(8,128)} fusion(bf16[256,2048]{1,0:T(8,128)(2,1)S(1)} %copy-done.62, bf16[256,2048]{1,0:T(8,128)(2,1)S(1)} %copy-done.64, bf16[256,768]{1,0:T(8,128)(2,1)S(1)} %get-tuple-element.399, bf16[256,768]{1,0:T(8,128)(2,1)S(1)} %get-tuple-element.398), kind=kOutput, calls=%fused_computation.94 | convolution fusion | flops 1616379904 | bytes 9175040 | tf_op jit(solution)/shard_map/dot_general | solution.py:588
  280.7 1.5 fusion.45
  284.8 4.4 %fusion.46 = f32[768,2048]{1,0:T(8,128)} fusion(bf16[256,2048]{1,0:T(8,128)(2,1)S(1)} %get-tuple-element.397, bf16[256,2048]{1,0:T(8,128)(2,1)S(1)} %get-tuple-element.395, bf16[256,768]{1,0:T(8,128)(2,1)S(1)} %copy-done.20, bf16[256,768]{1,0:T(8,128)(2,1)S(1)} %copy-done.18), kind=kOutput, calls=%fused_computation.86 | convolution fusion | flops 1616379904 | bytes 9175040 | tf_op jit(solution)/shard_map/dot_general | solution.py:589
  290.2 4.7 %fusion.50 = f32[768,2048]{1,0:T(8,128)} fusion(bf16[256,2048]{1,0:T(8,128)(2,1)S(1)} %get-tuple-element.396, bf16[256,2048]{1,0:T(8,128)(2,1)S(1)} %get-tuple-element.394, bf16[256,768]{1,0:T(8,128)(2,1)S(1)} %copy-done.20, bf16[256,768]{1,0:T(8,128)(2,1)S(1)} %copy-done.18), kind=kOutput, calls=%fused_computation.90 | convolution fusion | flops 1616379904 | bytes 9175040 | tf_op jit(solution)/shard_map/dot_general | solution.py:590
  299.9 2.8 add_add_fusion.2
  302.8 109.3 %tail_all.1 = (f32[48,2048]{1,0:T(8,128)}, f32[48,2048]{1,0:T(8,128)}, f32[128,768]{1,0:T(8,128)}, f32[2008,768]{1,0:T(8,128)}) custom-call(f32[2,2,2,2,48,2048]{5,4,3,2,1,0:T(8,128)} %bitcast.130, f32[2,2,2,2,48,2048]{5,4,3,2,1,0:T(8,128)} %bitcast.131, f32[2,2,2,2,128,768]{5,4,3,2,1,0:T(8,128)} %bitcast.150, f32[16,64,768]{2,1,0:T(8,128)} %bitcast.138, ...), custom_call_target="tpu_custom_call" | custom-call | flops 9474932736 | bytes 41943040 | tf_op jit(solution)/shard_map/tail_all/pallas_call | solution.py:479
  412.2 1.4 while.27
  414.9 5.9 %copy.50 = f32[2008,768]{1,0:T(8,128)} copy(f32[2008,768]{1,0:T(8,128)} %get-tuple-element.638) | data formatting | bytes 12337152
  (171 shorter events, 26.8 us)
Async XLA Ops:
  7.2 70.9 %all-gather.5.cloned.1.call-start = ((), (), s32[]{:S(2)}) async-start(), calls=%async_computation.3 | async-start | bytes 10027008 | tf_op jit(solution)/shard_map/all_gather | solution.py:525
  33.6 32.5 %all-to-all-start.2 = ((bf16[16,64,768]{2,1,0:T(8,128)(2,1)}), bf16[16,64,768]{2,1,0:T(8,128)(2,1)S(1)}, u32[]{:S(2)}, u32[]{:S(2)}) async-start(bf16[16,64,768]{2,1,0:T(8,128)(2,1)} %bitcast.140), calls=%async_computation.2 | async-start | bytes 3145728 | tf_op jit(solution)/shard_map/all_to_all | solution.py:554
  67.4 10.7 %copy-start.5 = (bf16[512,768]{1,0:T(8,128)(2,1)}, bf16[512,768]{1,0:T(8,128)(2,1)S(1)}, u32[]{:S(2)}) copy-start(bf16[512,768]{1,0:T(8,128)(2,1)S(1)} %get-tuple-element.284) | copy-start | bytes 2359300
  67.5 10.7 %copy-start.13 = (s32[16,512]{1,0:T(8,128)}, s32[16,512]{1,0:T(8,128)S(1)}, u32[]{:S(2)}) copy-start(s32[16,512]{1,0:T(8,128)S(1)} %get-tuple-element.648) | copy-start | bytes 98308
  67.5 10.7 %copy-start.15 = (s32[16,512]{1,0:T(8,128)}, s32[16,512]{1,0:T(8,128)S(1)}, u32[]{:S(2)}) copy-start(s32[16,512]{1,0:T(8,128)S(1)} %get-tuple-element.649) | copy-start | bytes 98308
  67.5 10.7 %copy-start.25 = (pred[16,512]{1,0:T(8,128)(4,1)}, pred[16,512]{1,0:T(8,128)(4,1)S(1)}, u32[]{:S(2)}) copy-start(pred[16,512]{1,0:T(8,128)(4,1)S(1)} %get-tuple-element.655) | copy-start | bytes 24580
  67.5 10.7 %copy-start.34 = (s32[512]{0:T(512)}, s32[512]{0:T(512)S(1)}, u32[]{:S(2)}) copy-start(s32[512]{0:T(512)S(1)} %get-tuple-element.656) | copy-start | bytes 6148
  67.5 10.7 %copy-start.36 = (s32[512]{0:T(512)}, s32[512]{0:T(512)S(1)}, u32[]{:S(2)}) copy-start(s32[512]{0:T(512)S(1)} %get-tuple-element.657) | copy-start | bytes 6148
  68.4 9.7 %copy-start.48 = (f32[256]{0:T(256)}, f32[256]{0:T(256)S(1)}, u32[]{:S(2)}) copy-start(f32[256]{0:T(256)S(1)} %get-tuple-element.428) | copy-start | bytes 3076
  68.4 9.7 %copy-start.50 = (f32[256]{0:T(256)}, f32[256]{0:T(256)S(1)}, u32[]{:S(2)}) copy-start(f32[256]{0:T(256)S(1)} %get-tuple-element.414) | copy-start | bytes 3076
  69.4 30.5 %copy-start.17 = (bf16[256,768]{1,0:T(8,128)(2,1)}, bf16[256,768]{1,0:T(8,128)(2,1)S(1)}, u32[]{:S(2)}) copy-start(bf16[256,768]{1,0:T(8,128)(2,1)S(1)} %get-tuple-element.403) | copy-start | bytes 1179652
  84.3 15.7 %copy-start.3 = (bf16[16,48,2048]{2,1,0:T(8,128)(2,1)}, bf16[16,48,2048]{2,1,0:T(8,128)(2,1)S(1)}, u32[]{:S(2)}) copy-start(bf16[16,48,2048]{2,1,0:T(8,128)(2,1)S(1)} %get-tuple-element.392) | copy-start | bytes 9437188
  94.3 5.6 %copy-start.60 = (bf16[256,2048]{1,0:T(8,128)(2,1)}, bf16[256,2048]{1,0:T(8,128)(2,1)S(1)}, u32[]{:S(2)}) copy-start(bf16[256,2048]{1,0:T(8,128)(2,1)S(1)} %convolution_convert_fusion.3) | copy-start | bytes 3145732
  276.2 4.5 %copy-start.59 = (bf16[256,2048]{1,0:T(8,128)(2,1)S(1)}, bf16[256,2048]{1,0:T(8,128)(2,1)}, u32[]{:S(2)}) copy-start(bf16[256,2048]{1,0:T(8,128)(2,1)} %copy-done.58) | copy-start | bytes 3145732
  276.2 4.5 %copy-start.65 = (bf16[256,2048]{1,0:T(8,128)(2,1)S(1)}, bf16[256,2048]{1,0:T(8,128)(2,1)}, u32[]{:S(2)}) copy-start(bf16[256,2048]{1,0:T(8,128)(2,1)} %get-tuple-element.424) | copy-start | bytes 3145732
  290.2 4.7 %copy-start.7 = (bf16[512,768]{1,0:T(8,128)(2,1)S(1)}, bf16[512,768]{1,0:T(8,128)(2,1)}, u32[]{:S(2)}) copy-start(bf16[512,768]{1,0:T(8,128)(2,1)} %copy-done.5) | copy-start | bytes 2359300
  302.7 109.4 %copy-start.14 = (s32[16,512]{1,0:T(8,128)S(1)}, s32[16,512]{1,0:T(8,128)}, u32[]{:S(2)}) copy-start(s32[16,512]{1,0:T(8,128)} %copy-done.13) | copy-start | bytes 98308
  302.8 109.4 %copy-start.16 = (s32[16,512]{1,0:T(8,128)S(1)}, s32[16,512]{1,0:T(8,128)}, u32[]{:S(2)}) copy-start(s32[16,512]{1,0:T(8,128)} %copy-done.15) | copy-start | bytes 98308
  302.8 109.4 %copy-start.26 = (pred[16,512]{1,0:T(8,128)(4,1)S(1)}, pred[16,512]{1,0:T(8,128)(4,1)}, u32[]{:S(2)}) copy-start(pred[16,512]{1,0:T(8,128)(4,1)} %copy-done.25) | copy-start | bytes 24580
  302.8 109.4 %copy-start.35 = (s32[512]{0:T(512)S(1)}, s32[512]{0:T(512)}, u32[]{:S(2)}) copy-start(s32[512]{0:T(512)} %copy-done.34) | copy-start | bytes 6148
  302.8 109.4 %copy-start.37 = (s32[512]{0:T(512)S(1)}, s32[512]{0:T(512)}, u32[]{:S(2)}) copy-start(s32[512]{0:T(512)} %copy-done.36) | copy-start | bytes 6148
  414.9 5.9 %copy-start.33 = (f32[48,2048]{1,0:T(8,128)S(1)}, f32[48,2048]{1,0:T(8,128)}, u32[]{:S(2)}) copy-start(f32[48,2048]{1,0:T(8,128)} %get-tuple-element.639) | copy-start | bytes 1179652
  414.9 6.7 %copy-start.32 = (f32[48,2048]{1,0:T(8,128)S(1)}, f32[48,2048]{1,0:T(8,128)}, u32[]{:S(2)}) copy-start(f32[48,2048]{1,0:T(8,128)} %get-tuple-element.640) | copy-start | bytes 1179652
  414.9 7.4 %copy-start.31 = (f32[128,768]{1,0:T(8,128)S(1)}, f32[128,768]{1,0:T(8,128)}, u32[]{:S(2)}) copy-start(f32[128,768]{1,0:T(8,128)} %get-tuple-element.641) | copy-start | bytes 1179652
  (37 other events, 81.0 us)
Sparse Core Ops, SparseCore 0:
  10.4 67.6 all-gather.4

commit v5 on v4

--- a/solution.py
+++ b/solution.py
@@ -489,6 +489,166 @@
     )(grad_gate, grad_up, grad_down, send, row_idx, dtable)
 
 
+def front_kernel(table_rows, pack_hbm, table_ref, gate_hbm, up_hbm, down_hbm,
+                 pack_out, table_out, gate_out, up_out, down_out, x_out, slots_out, rows_out, rank_out,
+                 send, got, before_ref, local_sem, id_send, id_recv, w_send, w_recv, c_send, c_recv, row_send, row_recv):
+    me = lax.axis_index('fsdp')
+    total = 16
+    core = lax.rem(me, 2)
+    pos = [lax.rem(me // 2, 2), lax.rem(me // 4, 2), me // 8]
+    core_peer = me + 1 - 2 * core
+    shards = (gate_hbm, up_hbm, down_hbm)
+    outs = (gate_out, up_out, down_out)
+    tokens = pack_out.shape[2]
+    padded, dim = table_out.shape
+
+    barrier = pltpu.get_barrier_semaphore()
+    for step in range(1, total):
+        pl.semaphore_signal(barrier, inc=1, device_id=(lax.rem(me + step, total),), device_id_type=MESH_ID)
+    loads = [pltpu.make_async_copy(shards[part], outs[part].at[pos[2], pos[1], pos[0], core], local_sem.at[part]) for part in range(3)]
+    loads.append(pltpu.make_async_copy(pack_hbm, pack_out.at[me], local_sem.at[3]))
+    for load in loads:
+        load.start()
+
+    def remote(src, dst, send_sem, recv_sem, to):
+        return pltpu.make_async_remote_copy(src, dst, send_sem, recv_sem, device_id=(to,), device_id_type=MESH_ID)
+
+    def wide(phase):
+        made = []
+        for part in range(3):
+            order = axes(part)
+            iz, iy, ix = cube_index({axis: pos[axis] for axis in order[phase - 1:]})
+            here = outs[part].at[iz, iy, ix, core]
+            axis = order[phase - 1]
+            made.append(remote(shards[part] if phase == 1 else here, here, w_send.at[phase, part], w_recv.at[phase, part],
+                               me + (1 - 2 * pos[axis]) * (2 << axis)))
+        return made
+
+    def across(stage):
+        made = []
+        for part in range(3):
+            order = axes(part)
+            fixed = {axis: pos[axis] for axis in order[stage:]}
+            if stage:
+                fixed[order[stage - 1]] = 1 - pos[order[stage - 1]]
+            iz, iy, ix = cube_index(fixed)
+            here = outs[part].at[iz, iy, ix, core]
+            made.append(remote(here if stage else shards[part], here, c_send.at[stage, part], c_recv.at[stage, part], core_peer))
+        return made
+
+    def id_copies():
+        return [remote(pack_hbm, pack_out.at[me], id_send.at[step], id_recv.at[step], lax.rem(me + step, total)) for step in range(1, total)]
+
+    def row_copy(step):
+        to = lax.rem(me + step, total)
+        return remote(send.at[to], got.at[me], row_send.at[step], row_recv.at[step], to)
+
+    def start(made):
+        for copy in made:
+            copy.start()
+
+    def finish(made):
+        for copy in made:
+            copy.wait()
+
+    pl.semaphore_wait(barrier, total - 1)
+    start(id_copies())
+    start(wide(1))
+    start(across(0))
+    table_out[0:table_rows, :] = table_ref[...]
+    table_out[table_rows:padded, :] = jnp.zeros((padded - table_rows, dim), table_out.dtype)
+    earlier = lax.broadcasted_iota(jnp.int32, (tokens, tokens), 0) < lax.broadcasted_iota(jnp.int32, (tokens, tokens), 1)
+    before_ref[...] = jnp.where(earlier, 1.0, 0.0).astype(jnp.bfloat16)
+    rank_out[...] = jnp.zeros_like(rank_out)
+    for load in loads:
+        load.wait()
+    finish(id_copies())
+
+    lanes_iota = lax.broadcasted_iota(jnp.int32, (SLOTS, padded), 1)
+    slot_iota = lax.broadcasted_iota(jnp.int32, (SLOTS, tokens), 0)
+    dev_iota = lax.broadcasted_iota(jnp.int32, (total, tokens), 0)
+
+    def build(step):
+        to = lax.rem(me + step, total)
+        ids = pack_out[to, 0:1, :]
+        owner = jnp.zeros_like(ids)
+        for k in range(1, total):
+            owner = owner + jnp.where(ids >= k * table_rows, 1, 0)
+        hot = jnp.where(dev_iota == owner, 1.0, 0.0)
+        before = jnp.dot(hot.astype(jnp.bfloat16), before_ref[...], preferred_element_type=jnp.float32)
+        rank = jnp.sum(hot * before, axis=0, keepdims=True)
+        rank_out[...] = jnp.maximum(rank_out[...], rank)
+        rank = rank.astype(jnp.int32)
+        owned = jnp.where(owner == me, rank, -1)
+        picked = jnp.where(slot_iota == owned, 1.0, 0.0)
+        code = ids - me * table_rows + 1
+        column = jnp.sum(picked * code.astype(jnp.float32), axis=1, keepdims=True).astype(jnp.int32) - 1
+        high = lax.shift_right_arithmetic(code, 6)
+        digits = jnp.where(owner == me, jnp.concatenate([high, code - high * 64], axis=0), 0)
+        digits = jnp.concatenate([digits, jnp.zeros((6, tokens), jnp.int32)], axis=0).astype(jnp.float32).astype(jnp.bfloat16)
+        spread = lax.dot_general(digits, picked.astype(jnp.bfloat16), COLS_DIMS, preferred_element_type=jnp.float32)
+        rows_out[pl.ds(to, 1), :] = (spread[0:1] * 64.0 + spread[1:2]).astype(jnp.int32) - 1
+        choose = jnp.where(lanes_iota == column, 1.0, 0.0).astype(jnp.bfloat16)
+        send[to] = jnp.dot(choose, table_out[...], preferred_element_type=jnp.float32).astype(jnp.bfloat16)
+        return owner, rank
+
+    owner, rank = build(0)
+    slots_out[...] = jnp.where(rank < SLOTS, owner * SLOTS + rank, -1)
+    own_rows = pltpu.make_async_copy(send.at[me], got.at[me], local_sem.at[4])
+
+    def build_step(step, carry):
+        build(step)
+        pl.when(step > 1)(lambda: row_copy(step - 1).start())
+        return carry
+
+    lax.fori_loop(1, 6, build_step, 0)
+    own_rows.start()
+    finish(wide(1))
+    start(wide(2))
+    start(across(1))
+    lax.fori_loop(6, total, build_step, 0)
+    row_copy(total - 1).start()
+    finish(wide(2))
+    start(wide(3))
+    start(across(2))
+    own_rows.wait()
+    finish([row_copy(step) for step in range(1, total)])
+    place = lax.broadcasted_iota(jnp.int32, (total * SLOTS, tokens), 0) == slots_out[...]
+    x_out[...] = lax.dot_general(jnp.where(place, 1.0, 0.0).astype(jnp.bfloat16), got[...].reshape(total * SLOTS, dim), ROWS_DIMS,
+                                 preferred_element_type=jnp.float32).astype(jnp.bfloat16)
+    finish(across(0))
+    finish(across(1))
+    finish(wide(3))
+    start(across(3))
+    finish(across(2))
+    finish(across(3))
+
+
+def front(packed, table_shard, gate_shard, up_shard, down_shard):
+    bf16 = jnp.bfloat16
+    rows, dim = table_shard.shape
+    padded = -(-rows // VOCAB_TILE) * VOCAB_TILE
+    tokens = packed.shape[1]
+    vmem = pl.BlockSpec(memory_space=pltpu.VMEM)
+    anywhere = pl.BlockSpec(memory_space=pl.ANY)
+    sems = pltpu.SemaphoreType.DMA
+    shards = (gate_shard, up_shard, down_shard)
+    return pl.pallas_call(
+        functools.partial(front_kernel, rows),
+        in_specs=[anywhere, vmem, anywhere, anywhere, anywhere],
+        out_specs=[vmem] * 9,
+        out_shape=[jax.ShapeDtypeStruct((16,) + packed.shape, jnp.int32), jax.ShapeDtypeStruct((padded, dim), bf16)]
+        + [jax.ShapeDtypeStruct((2, 2, 2, 2) + shard.shape, bf16) for shard in shards]
+        + [jax.ShapeDtypeStruct((tokens, dim), bf16), jax.ShapeDtypeStruct((1, tokens), jnp.int32),
+           jax.ShapeDtypeStruct((16, SLOTS), jnp.int32), jax.ShapeDtypeStruct((1, tokens), jnp.float32)],
+        scratch_shapes=[pltpu.VMEM((16, SLOTS, dim), bf16), pltpu.VMEM((16, SLOTS, dim), bf16), pltpu.VMEM((tokens, tokens), bf16),
+                        sems((5,)), sems((16,)), sems((16,)), sems((4, 3)), sems((4, 3)), sems((4, 3)), sems((4, 3)), sems((16,)), sems((16,))],
+        compiler_params=pltpu.CompilerParams(vmem_limit_bytes=60 * 1024 * 1024, collective_id=3, has_side_effects=True),
+        cost_estimate=pl.CostEstimate(flops=4 * 16 * SLOTS * padded * dim, bytes_accessed=20 * 1024 * 1024, transcendentals=0),
+        name="front_all",
+    )(packed, table_shard, gate_shard, up_shard, down_shard)
+
+
 def split3(values):
     high = lax.reduce_precision(values, 8, 7)
     rest = values - high
@@ -517,54 +677,52 @@
         me = lax.axis_index('fsdp')
 
         packed = jnp.stack([token_ids.reshape(tok_dev), labels.reshape(tok_dev)])
-        packed_all = lax.all_gather(packed, 'fsdp', axis=0, tiled=False)
-        ids_all = packed_all[:, 0]
-
         gate_rows, ffn = gate_shard.shape
         down_rows = down_shard.shape[0]
-        w_all = lax.all_gather(jnp.concatenate([gate_shard, up_shard, down_shard.reshape(gate_rows, ffn)], axis=0), 'fsdp', axis=0, tiled=False)
-        w_gate = w_all[:, :gate_rows].reshape(groups * gate_rows, ffn)
-        w_up = w_all[:, gate_rows:2 * gate_rows].reshape(groups * gate_rows, ffn)
-        w_down = w_all[:, 2 * gate_rows:].reshape(groups, down_rows, dim).reshape(groups * down_rows, dim)
-
-        owner = ids_all // rows
-        local = ids_all - owner * rows
-        owner_hot = owner[:, :, None] == jnp.arange(groups, dtype=jnp.int32)
-        tri = jnp.tril(jnp.ones((tok_dev, tok_dev), jnp.bfloat16), -1)
-        before = jnp.einsum('tu,suo->sto', tri, owner_hot.astype(jnp.bfloat16), preferred_element_type=jnp.float32)
-        rank = jnp.sum(jnp.where(owner_hot, before, 0.0), axis=-1).astype(jnp.int32)
-        rounds = jnp.max(rank) // SLOTS + 1
-        my_owner = lax.dynamic_index_in_dim(owner, me, 0, keepdims=False)
-        my_rank = lax.dynamic_index_in_dim(rank, me, 0, keepdims=False)
-        owned = owner == me
+        (packed_all, table_padded, w_gate, w_up, w_down, emb_rows, slots, row_idx, top_rank) = front(
+            packed, table_shard, gate_shard, up_shard, down_shard)
+        w_gate = w_gate.reshape(groups * gate_rows, ffn)
+        w_up = w_up.reshape(groups * gate_rows, ffn)
+        w_down = w_down.reshape(groups * down_rows, dim)
+        rounds = jnp.max(top_rank).astype(jnp.int32) // SLOTS + 1
         slot_ids = jnp.arange(SLOTS, dtype=jnp.int32)
 
-        def owned_rows(round_idx):
-            hit = owned[:, None, :] & (rank[:, None, :] == slot_ids[None, :, None] + round_idx * SLOTS)
+        def ranks(round_idx):
+            ids_all, round_idx = lax.optimization_barrier((packed_all[:, 0], round_idx))
+            owner = ids_all // rows
+            owner_hot = owner[:, :, None] == jnp.arange(groups, dtype=jnp.int32)
+            tri = jnp.tril(jnp.ones((tok_dev, tok_dev), jnp.bfloat16), -1)
+            before = jnp.einsum('tu,suo->sto', tri, owner_hot.astype(jnp.bfloat16), preferred_element_type=jnp.float32)
+            rank = jnp.sum(jnp.where(owner_hot, before, 0.0), axis=-1).astype(jnp.int32)
+            return owner, ids_all - owner * rows, rank - round_idx * SLOTS
+
+        def owned_rows(owner, local, rank):
+            hit = (owner == me)[:, None, :] & (rank[:, None, :] == slot_ids[None, :, None])
             return (jnp.sum(jnp.where(hit, local[:, None, :] + 1, 0), axis=-1) - 1).reshape(groups * SLOTS)
 
-        def my_slots(round_idx):
-            off = my_rank - round_idx * SLOTS
-            return jnp.where((off >= 0) & (off < SLOTS), my_owner * SLOTS + off, -1)
+        def my_slots(owner, rank):
+            mine = lax.dynamic_index_in_dim(owner, me, 0, keepdims=False)
+            off = lax.dynamic_index_in_dim(rank, me, 0, keepdims=False)
+            return jnp.where((off >= 0) & (off < SLOTS), mine * SLOTS + off, -1)
+
+        def slot_place(slot_row):
+            return (jnp.arange(groups * SLOTS, dtype=jnp.int32)[:, None] == slot_row[None, :]).astype(jnp.bfloat16)
 
         def fetch_round(round_idx):
-            row_idx = owned_rows(round_idx)
-            select = (row_idx[:, None] == jnp.arange(rows, dtype=jnp.int32)[None, :]).astype(jnp.bfloat16)
+            owner, local, rank = ranks(round_idx)
+            select = (owned_rows(owner, local, rank)[:, None] == jnp.arange(rows, dtype=jnp.int32)[None, :]).astype(jnp.bfloat16)
             send = jnp.dot(select, table_shard, preferred_element_type=jnp.float32).astype(jnp.bfloat16)
             got = lax.all_to_all(send.reshape(groups, SLOTS, dim), 'fsdp', 0, 0).reshape(groups * SLOTS, dim)
-            place = (my_slots(round_idx)[:, None] == jnp.arange(groups * SLOTS, dtype=jnp.int32)[None, :]).astype(jnp.bfloat16)
-            return jnp.dot(place, got, preferred_element_type=jnp.float32).astype(jnp.bfloat16)
-
-        def slot_place(round_idx):
-            return (jnp.arange(groups * SLOTS, dtype=jnp.int32)[:, None] == my_slots(round_idx)[None, :]).astype(jnp.bfloat16)
+            place = slot_place(my_slots(owner, rank))
+            return lax.dot_general(place, got, ROWS_DIMS, preferred_element_type=jnp.float32).astype(jnp.bfloat16)
 
         def return_round(round_idx, grad_rows):
-            send = pick_rows(slot_place(round_idx), grad_rows)
+            owner, local, rank = ranks(round_idx)
+            send = pick_rows(slot_place(my_slots(owner, rank)), grad_rows)
             got = lax.all_to_all(send.reshape(groups, SLOTS, dim), 'fsdp', 0, 0).reshape(groups * SLOTS, dim)
-            select = (jnp.arange(rows, dtype=jnp.int32)[:, None] == owned_rows(round_idx)[None, :]).astype(jnp.bfloat16)
+            select = (jnp.arange(rows, dtype=jnp.int32)[:, None] == owned_rows(owner, local, rank)[None, :]).astype(jnp.bfloat16)
             return pick_rows(select, got)
 
-        emb_rows = fetch_round(jnp.int32(0))
         emb_rows = lax.fori_loop(1, rounds, lambda r, acc: acc + fetch_round(r), emb_rows)
 
         normed, saved = [], []
@@ -575,8 +733,6 @@
 
         chunks = tok_dev // UNIT
         lab_rows = jnp.transpose(packed_all[:, 1].reshape(groups, chunks, UNIT), (1, 0, 2)).reshape(2 * chunks, groups * UNIT // 2)
-        padded = -(-rows // VOCAB_TILE) * VOCAB_TILE
-        table_padded = jnp.pad(table_shard, ((0, padded - rows), (0, 0)))
         dz, dtable, loss_rows = head(jnp.concatenate(normed, axis=0), table_padded, lab_rows, rows)
         loss_total = jnp.sum(loss_rows)
         grad_normed = [dz[m * tok_micro:(m + 1) * tok_micro] for m in range(micro_count)]
@@ -589,9 +745,9 @@
         grad_gate = lax.dot_general(normed_in, grad_gate_pre, ROWS_DIMS, preferred_element_type=jnp.float32)
         grad_up = lax.dot_general(normed_in, grad_up_proj, ROWS_DIMS, preferred_element_type=jnp.float32)
         cube = (2, 2, 2, 2)
-        send = pick_rows(slot_place(0), grad_rows).reshape(groups, SLOTS, dim)
+        send = pick_rows(slot_place(slots[0]), grad_rows).reshape(groups, SLOTS, dim)
         out_gate, out_up, out_down, dtable = tail(grad_gate.reshape(cube + (gate_rows, ffn)), grad_up.reshape(cube + (gate_rows, ffn)),
-                                                  grad_down.reshape(cube + (down_rows, dim)), send, owned_rows(0).reshape(1, groups * SLOTS), dtable, rows)
+                                                  grad_down.reshape(cube + (down_rows, dim)), send, row_idx.reshape(1, groups * SLOTS), dtable, rows)
         dtable = lax.fori_loop(1, rounds, lambda r, acc: acc + return_round(r, grad_rows), dtable)
         return (loss_total / total_tokens, dtable, out_gate, out_up, out_down)
 

time: 439 us -> 423 us (0.964)
  Pallas kernels: 273 us -> 343 us
  waiting for transfers between devices: 29.7 us -> 0 us
  between operations: 19.6 us -> 3.94 us
  blocking collectives: 15 us -> 0 us
  local copies, waits for them, and re-layouts: 31.4 us -> 18.5 us
  matrix products: 46.2 us -> 38.5 us
    pallas_call x0 -> x1, Pallas kernels: none -> 69.1 us  [front(): pl.pallas_call(functools.partial(front_kernel, rows), in_specs=[anywhere,...]
    all_to_all x1 -> x0, waiting for transfers between devices: 20.9 us -> none  [fetch_round(): lax.all_to_all(send.reshape(groups, SLOTS, dim), 'fsdp', 0, 0)]
    all_gather x1 -> x0, blocking collectives: 15 us -> none  [device_step(): packed_all = lax.all_gather(packed, 'fsdp', axis=0, tiled=False)]
    all_gather x1 -> x0, waiting for transfers between devices: 8.75 us -> none  [device_step(): lax.all_gather(jnp.concatenate([gate_shard, up_shard, down_shard.reshape(...]
    dot_general x3 -> x0, matrix products: 8.31 us -> none  [the longest x1 6.77 us: fetch_round(): jnp.dot(select, table_shard, preferred_element_type=jnp.float32)]
    another operation x1 -> x0, local copies, waits for them, and re-layouts: 7.03 us -> none  [device_step(): w_all[:, 2 * gate_rows:].reshape(groups, down_rows, dim)]
    slice x1 -> x0, local copies, waits for them, and re-layouts: 6.08 us -> none  [device_step(): w_all[:, 2 * gate_rows:].reshape(groups, down_rows, dim)]
    unnamed x122 -> x99, local copies, waits for them, and re-layouts: 11.6 us -> 13.9 us
  transfers between devices with their start and end apart: 2 -> 0, of which waited for: 2 -> 0; matrix products, arithmetic and copies ran while one was open for 4% -> 0% of each run, Pallas kernels for 0% -> 0%
where the time goes in v5:
time: 423 us; the launch traced here: 416 us
  Pallas kernels  343 us (81%)
  matrix products  38.5 us (9%)
  local copies, waits for them, and re-layouts  18.5 us (4%)
  other arithmetic  10.3 us (2%)
    pallas_call x1, Pallas kernels, head(): pl.pallas_call(functools.partial(head_kernel, vocab_rows, chunks), in_spe...  165 us
    pallas_call x1, Pallas kernels, tail(): pl.pallas_call(functools.partial(tail_kernel, table_rows), in_specs=[anyw...  109 us
    pallas_call x1, Pallas kernels, front(): pl.pallas_call(functools.partial(front_kernel, rows), in_specs=[anywhere,...  69.1 us
    unnamed x99, local copies, waits for them, and re-layouts  13.9 us

profile of v5, /device:TPU:0, one launch (start us, length us, event | category | flops | bytes accessed | tf_op | source)
XLA Modules:
  0.0 416.4 jit_solution(14745879966135979018)
XLA Ops:
  2.8 69.1 %front_all.1 = (s32[16,2,512]{2,1,0:T(2,128)}, bf16[2048,768]{1,0:T(8,128)(2,1)}, bf16[2,2,2,2,48,2048]{5,4,3,2,1,0:T(8,128)(2,1)}, bf16[2,2,2,2,48,2048]{5,4,3,...) custom-call(s32[2,512]{1,0:T(2,128)} %pad_add_fusion.pack_hbm, ...), custom_call_target="tpu_custom_call" | custom-call | flops 6442450944 | bytes 20971520 | tf_op jit(solution)/shard_map/front_all/pallas_call | solution.py:636
  71.9 1.3 reduce_max.9
  73.9 1.4 reshape.195.row_ref
  79.5 3.2 convolution_convert_fusion.3
  83.8 1.2 copy-done.14
  85.0 2.2 fusion.54
  87.5 1.1 fusion.101
  89.3 2.2 fusion.50
  91.5 1.1 fusion.95
  94.4 165.1 %head_all.1 = (f32[512,768]{1,0:T(8,128)}, f32[2048,768]{1,0:T(8,128)}, f32[3,512]{1,0:T(4,128)}) custom-call(bf16[8,64,768]{2,1,0:T(8,128)(2,1)} %bitcast.132, bf16[2048,768]{1,0:T(8,128)(2,1)} %get-tuple-element.322.table_ref, s32[16,512]{1,0:T(8,128)} %reshape.190.lab_ref), custom_call_target="tpu_custom_call" | custom-call | flops 77309411328 | bytes 6291456 | tf_op jit(solution)/shard_map/head_all/pallas_call | solution.py:306
  259.6 1.5 reduce_sum.137
  261.7 1.9 fusion.100
  264.1 1.4 copy-done.45
  265.5 3.2 fusion.63
  268.7 1.5 fusion.69
  274.6 1.2 fusion.113
  278.5 1.5 fusion.82
  280.1 2.8 add_add_fusion.2
  282.9 4.5 %fusion.78 = f32[2048,768]{1,0:T(8,128)} fusion(bf16[256,2048]{1,0:T(8,128)(2,1)S(1)} %copy-done.50, bf16[256,2048]{1,0:T(8,128)(2,1)S(1)} %copy-done.52, bf16[256,768]{1,0:T(8,128)(2,1)S(1)} %get-tuple-element.457, bf16[256,768]{1,0:T(8,128)(2,1)S(1)} %get-tuple-element.456), kind=kOutput, calls=%fused_computation.135 | convolution fusion | flops 1616379904 | bytes 9175040 | tf_op jit(solution)/shard_map/dot_general | solution.py:744
  287.4 4.5 %fusion.74 = f32[768,2048]{1,0:T(8,128)} fusion(bf16[256,2048]{1,0:T(8,128)(2,1)S(1)} %get-tuple-element.454, bf16[256,2048]{1,0:T(8,128)(2,1)S(1)} %get-tuple-element.452, bf16[256,768]{1,0:T(8,128)(2,1)S(1)} %copy-done.13, bf16[256,768]{1,0:T(8,128)(2,1)S(1)} %copy-done.11), kind=kOutput, calls=%fused_computation.131 | convolution fusion | flops 1616379904 | bytes 9175040 | tf_op jit(solution)/shard_map/dot_general | solution.py:746
  291.9 4.4 %fusion.70 = f32[768,2048]{1,0:T(8,128)} fusion(bf16[256,2048]{1,0:T(8,128)(2,1)S(1)} %get-tuple-element.455, bf16[256,2048]{1,0:T(8,128)(2,1)S(1)} %get-tuple-element.453, bf16[256,768]{1,0:T(8,128)(2,1)S(1)} %copy-done.13, bf16[256,768]{1,0:T(8,128)(2,1)S(1)} %copy-done.11), kind=kOutput, calls=%fused_computation.127 | convolution fusion | flops 1616379904 | bytes 9175040 | tf_op jit(solution)/shard_map/dot_general | solution.py:745
  296.3 109.2 %tail_all.1 = (f32[48,2048]{1,0:T(8,128)}, f32[48,2048]{1,0:T(8,128)}, f32[128,768]{1,0:T(8,128)}, f32[2008,768]{1,0:T(8,128)}) custom-call(f32[2,2,2,2,48,2048]{5,4,3,2,1,0:T(8,128)} %bitcast.124, f32[2,2,2,2,48,2048]{5,4,3,2,1,0:T(8,128)} %bitcast.123, f32[2,2,2,2,128,768]{5,4,3,2,1,0:T(8,128)} %bitcast.141, f32[16,64,768]{2,1,0:T(8,128)} %bitcast.131, ...), custom_call_target="tpu_custom_call" | custom-call | flops 9474932736 | bytes 41943040 | tf_op jit(solution)/shard_map/tail_all/pallas_call | solution.py:479
  405.5 1.3 while.29
  406.9 5.9 %copy.37 = f32[2008,768]{1,0:T(8,128)} copy(f32[2008,768]{1,0:T(8,128)} %get-tuple-element.672) | data formatting | bytes 12337152
  (124 shorter events, 19.9 us)
Async XLA Ops:
  77.6 5.1 %copy-start.16 = (s32[16,2,512]{2,0,1:T(8,128)}, s32[16,2,512]{2,0,1:T(8,128)S(1)}, u32[]{:S(2)}) copy-start(s32[16,2,512]{2,0,1:T(8,128)S(1)} %get-tuple-element.680) | copy-start | bytes 196612
  77.6 13.9 %copy-start.3 = (bf16[512,768]{1,0:T(8,128)(2,1)}, bf16[512,768]{1,0:T(8,128)(2,1)S(1)}, u32[]{:S(2)}) copy-start(bf16[512,768]{1,0:T(8,128)(2,1)S(1)} %get-tuple-element.318) | copy-start | bytes 2359300
  78.4 4.3 %copy-start.35 = (f32[256]{0:T(256)}, f32[256]{0:T(256)S(1)}, u32[]{:S(2)}) copy-start(f32[256]{0:T(256)S(1)} %get-tuple-element.468) | copy-start | bytes 3076
  78.4 4.3 %copy-start.37 = (f32[256]{0:T(256)}, f32[256]{0:T(256)S(1)}, u32[]{:S(2)}) copy-start(f32[256]{0:T(256)S(1)} %get-tuple-element.482) | copy-start | bytes 3076
  79.4 4.3 %copy-start.12 = (bf16[256,768]{1,0:T(8,128)(2,1)}, bf16[256,768]{1,0:T(8,128)(2,1)S(1)}, u32[]{:S(2)}) copy-start(bf16[256,768]{1,0:T(8,128)(2,1)S(1)} %get-tuple-element.462) | copy-start | bytes 1179652
  79.4 9.8 %copy-start.10 = (bf16[256,768]{1,0:T(8,128)(2,1)}, bf16[256,768]{1,0:T(8,128)(2,1)S(1)}, u32[]{:S(2)}) copy-start(bf16[256,768]{1,0:T(8,128)(2,1)S(1)} %get-tuple-element.461) | copy-start | bytes 1179652
  79.4 3.3 copy-start.42
  82.7 6.5 %copy-start.48 = (bf16[256,2048]{1,0:T(8,128)(2,1)}, bf16[256,2048]{1,0:T(8,128)(2,1)S(1)}, u32[]{:S(2)}) copy-start(bf16[256,2048]{1,0:T(8,128)(2,1)S(1)} %convolution_convert_fusion.3) | copy-start | bytes 3145732
  88.6 4.5 %copy-start.5 = (bf16[256,768]{1,0:T(8,128)(2,1)}, bf16[256,768]{1,0:T(8,128)(2,1)S(1)}, u32[]{:S(2)}) copy-start(bf16[256,768]{1,0:T(8,128)(2,1)S(1)} %get-tuple-element.480) | copy-start | bytes 1179652
  89.3 3.9 copy-start.27
  259.5 4.1 copy-start.2
  259.5 4.1 copy-start.6
  259.5 4.1 copy-start.8
  259.5 4.1 copy-start.26
  259.5 4.1 copy-start.28
  259.5 4.1 copy-start.30
  259.5 4.1 copy-start.33
  259.6 4.1 copy-start.34
  282.9 4.5 %copy-start.11 = (bf16[256,768]{1,0:T(8,128)(2,1)S(1)}, bf16[256,768]{1,0:T(8,128)(2,1)}, u32[]{:S(2)}) copy-start(bf16[256,768]{1,0:T(8,128)(2,1)} %copy-done.10) | copy-start | bytes 1179652
  282.9 4.5 %copy-start.13 = (bf16[256,768]{1,0:T(8,128)(2,1)S(1)}, bf16[256,768]{1,0:T(8,128)(2,1)}, u32[]{:S(2)}) copy-start(bf16[256,768]{1,0:T(8,128)(2,1)} %copy-done.12) | copy-start | bytes 1179652
  296.3 109.2 %copy-start.17 = (s32[16,2,512]{2,0,1:T(8,128)S(1)}, s32[16,2,512]{2,0,1:T(8,128)}, u32[]{:S(2)}) copy-start(s32[16,2,512]{2,0,1:T(8,128)} %copy-done.16) | copy-start | bytes 196612
  406.8 5.9 %copy-start.24 = (f32[48,2048]{1,0:T(8,128)S(1)}, f32[48,2048]{1,0:T(8,128)}, u32[]{:S(2)}) copy-start(f32[48,2048]{1,0:T(8,128)} %get-tuple-element.673) | copy-start | bytes 1179652
  406.9 6.7 %copy-start.23 = (f32[48,2048]{1,0:T(8,128)S(1)}, f32[48,2048]{1,0:T(8,128)}, u32[]{:S(2)}) copy-start(f32[48,2048]{1,0:T(8,128)} %get-tuple-element.674) | copy-start | bytes 1179652
  406.9 7.4 %copy-start.22 = (f32[128,768]{1,0:T(8,128)S(1)}, f32[128,768]{1,0:T(8,128)}, u32[]{:S(2)}) copy-start(f32[128,768]{1,0:T(8,128)} %get-tuple-element.675) | copy-start | bytes 1179652
  (23 other events, 40.6 us)

commit v6 on v5

--- a/solution.py
+++ b/solution.py
@@ -343,23 +343,22 @@
     return choice.get(2, slice(None)), choice.get(1, slice(None)), choice.get(0, slice(None))
 
 
-def tail_kernel(table_rows, gate_hbm, up_hbm, down_hbm, send_hbm, row_ref, dtable_hbm, gate_out, up_out, down_out, dtable_out,
-                acc_g, acc_u, acc_d, core_g, core_u, core_d, one_g, one_u, one_d, two_g, two_u, two_d, three_g, three_u, three_d,
+def tail_kernel(table_rows, u_ref, acts_ref, mid_ref, gate_ref, up_ref, send_hbm, row_ref, dtable_hbm, gate_out, up_out, down_out, dtable_out,
+                all_g, all_u, all_d, core_g, core_u, core_d, one_g, one_u, one_d, two_g, two_u, two_d, three_g, three_u, three_d,
                 rows_got, split, local_sem, send_sem, recv_sem, row_send, row_recv):
     me = lax.axis_index('fsdp')
     total = 16
     core = lax.rem(me, 2)
     pos = [lax.rem(me // 2, 2), lax.rem(me // 4, 2), me // 8]
     core_peer = me + 1 - 2 * core
-    whole = (gate_hbm, up_hbm, down_hbm)
-    accs = (acc_g, acc_u, acc_d)
+    whole = (all_g, all_u, all_d)
     gots = ((core_g, core_u, core_d), (one_g, one_u, one_d), (two_g, two_u, two_d), (three_g, three_u, three_d))
     outs = (gate_out, up_out, down_out)
 
     barrier = pltpu.get_barrier_semaphore()
     for step in range(1, total):
         pl.semaphore_signal(barrier, inc=1, device_id=(lax.rem(me + step, total),), device_id_type=MESH_ID)
-    loads = [pltpu.make_async_copy(whole[part].at[:, :, :, core], accs[part], local_sem.at[part]) for part in range(3)]
+    loads = []
     loads.append(pltpu.make_async_copy(dtable_hbm.at[pl.ds(0, table_rows)], dtable_out, local_sem.at[3]))
     loads.append(pltpu.make_async_copy(send_hbm.at[me], rows_got.at[me], local_sem.at[4]))
     for load in loads:
@@ -368,25 +367,25 @@
 
     def piece(part, q):
         if part == 2:
-            size = acc_d.shape[3] // PIECES
+            size = all_d.shape[4] // PIECES
             return pl.ds(q * size, size), slice(None)
-        size = acc_g.shape[4] // PIECES
+        size = all_g.shape[5] // PIECES
         return slice(None), pl.ds(q * size, size)
 
-    def copies(phase, q):
+    def copies(phase, q, parts=(0, 1, 2)):
         made = []
-        for part in range(3):
+        for part in parts:
             rows, lanes = piece(part, q)
             order = axes(part)
             if phase == 0:
-                src = whole[part].at[:, :, :, 1 - core, rows, lanes]
+                src = whole[part].at[1 - core, :, :, :, rows, lanes]
                 dst = gots[0][part].at[:, :, :, rows, lanes]
                 to = core_peer
             else:
                 fixed = {axis: pos[axis] for axis in order[:phase - 1]}
                 fixed[order[phase - 1]] = 1 - pos[order[phase - 1]]
                 iz, iy, ix = cube_index(fixed)
-                src = accs[part].at[iz, iy, ix, rows, lanes]
+                src = whole[part].at[core, iz, iy, ix, rows, lanes]
                 lead = (slice(None),) * (3 - phase)
                 dst = gots[phase][part].at[lead + (rows, lanes)]
                 axis = order[phase - 1]
@@ -407,18 +406,33 @@
             iz, iy, ix = cube_index({axis: pos[axis] for axis in axes(part)[:phase]})
             got = gots[phase][part][(slice(None),) * (3 - phase) + (rows, lanes)]
             if phase == 3:
-                outs[part][rows, lanes] = accs[part][iz, iy, ix, rows, lanes] + got
+                outs[part][rows, lanes] = whole[part][core, iz, iy, ix, rows, lanes] + got
             else:
-                accs[part][iz, iy, ix, rows, lanes] += got
+                whole[part][core, iz, iy, ix, rows, lanes] += got
 
     row_copies = []
     for step in range(1, total):
         to = lax.rem(me + step, total)
         row_copies.append(pltpu.make_async_remote_copy(send_hbm.at[to], rows_got.at[me], row_send.at[step], row_recv.at[step],
                                                        device_id=(to,), device_id_type=MESH_ID))
+    start(row_copies)
+    down_rows = all_d.shape[4]
+    for chip in range(8):
+        block = lax.dot_general(acts_ref[:, 2 * chip * down_rows:2 * (chip + 1) * down_rows], mid_ref[...], ROWS_DIMS,
+                                preferred_element_type=jnp.float32)
+        for c in range(2):
+            all_d[c, chip // 4, chip // 2 % 2, chip % 2] = block[c * down_rows:(c + 1) * down_rows]
     for q in range(PIECES):
-        start(copies(0, q))
-    start(row_copies)
+        start(copies(0, q, (2,)))
+    unit, lanes = all_g.shape[4], all_g.shape[5] // PIECES
+    for q in range(PIECES):
+        here = slice(q * lanes, (q + 1) * lanes)
+        for grads, array in ((gate_ref, all_g), (up_ref, all_u)):
+            for h in range(2):
+                block = lax.dot_general(u_ref[:, 8 * unit * h:8 * unit * (h + 1)], grads[:, here], ROWS_DIMS, preferred_element_type=jnp.float32)
+                for k in range(8):
+                    array[k % 2, h, k // 4, k // 2 % 2, :, here] = block[k * unit:(k + 1) * unit]
+        start(copies(0, q, (0, 1)))
     for load in loads:
         load.wait()
     for q in range(PIECES):
@@ -467,26 +481,27 @@
             finish_add(3, q - 2)
 
 
-def tail(grad_gate, grad_up, grad_down, send, row_idx, dtable, table_rows):
+def tail(normed_in, acts, grad_mid, grad_gate_pre, grad_up_proj, send, row_idx, dtable, table_rows):
     f32 = jnp.float32
     vmem = pl.BlockSpec(memory_space=pltpu.VMEM)
     anywhere = pl.BlockSpec(memory_space=pl.ANY)
     sems = pltpu.SemaphoreType.DMA
-    blocks = [tuple(array.shape[4:]) for array in (grad_gate, grad_up, grad_down)]
-    scratch = [pltpu.VMEM(lead + block, f32) for lead in ((2, 2, 2), (2, 2, 2), (2, 2), (2,), ()) for block in blocks]
+    ffn = acts.shape[1]
+    blocks = [(normed_in.shape[1] // 16, ffn), (normed_in.shape[1] // 16, ffn), (ffn // 16, normed_in.shape[1])]
+    scratch = [pltpu.VMEM(lead + block, f32) for lead in ((2, 2, 2, 2), (2, 2, 2), (2, 2), (2,), ()) for block in blocks]
     slots = send.shape[0] * send.shape[1]
     dim = send.shape[2]
     return pl.pallas_call(
         functools.partial(tail_kernel, table_rows),
-        in_specs=[anywhere, anywhere, anywhere, anywhere, vmem, anywhere],
+        in_specs=[vmem, vmem, vmem, vmem, vmem, anywhere, vmem, anywhere],
         out_specs=[vmem] * 4,
         out_shape=[jax.ShapeDtypeStruct(block, f32) for block in blocks] + [jax.ShapeDtypeStruct((table_rows, dim), f32)],
         scratch_shapes=scratch + [pltpu.VMEM(send.shape, f32), pltpu.VMEM((3 * slots, dim), jnp.bfloat16),
                                   sems((5,)), sems((4, 3, PIECES)), sems((4, 3, PIECES)), sems((16,)), sems((16,))],
-        compiler_params=pltpu.CompilerParams(vmem_limit_bytes=60 * 1024 * 1024, collective_id=2, has_side_effects=True),
+        compiler_params=pltpu.CompilerParams(vmem_limit_bytes=67043328, collective_id=2, has_side_effects=True),
         cost_estimate=pl.CostEstimate(flops=6 * slots * table_rows * dim, bytes_accessed=40 * 1024 * 1024, transcendentals=0),
         name="tail_all",
-    )(grad_gate, grad_up, grad_down, send, row_idx, dtable)
+    )(normed_in, acts, grad_mid, grad_gate_pre, grad_up_proj, send, row_idx, dtable)
 
 
 def front_kernel(table_rows, pack_hbm, table_ref, gate_hbm, up_hbm, down_hbm,
@@ -564,12 +579,11 @@
         load.wait()
     finish(id_copies())
 
-    lanes_iota = lax.broadcasted_iota(jnp.int32, (SLOTS, padded), 1)
+    lanes_iota = lax.broadcasted_iota(jnp.int32, (4 * SLOTS, padded), 1)
     slot_iota = lax.broadcasted_iota(jnp.int32, (SLOTS, tokens), 0)
     dev_iota = lax.broadcasted_iota(jnp.int32, (total, tokens), 0)
 
-    def build(step):
-        to = lax.rem(me + step, total)
+    def rank_of(to):
         ids = pack_out[to, 0:1, :]
         owner = jnp.zeros_like(ids)
         for k in range(1, total):
@@ -578,36 +592,41 @@
         before = jnp.dot(hot.astype(jnp.bfloat16), before_ref[...], preferred_element_type=jnp.float32)
         rank = jnp.sum(hot * before, axis=0, keepdims=True)
         rank_out[...] = jnp.maximum(rank_out[...], rank)
-        rank = rank.astype(jnp.int32)
-        owned = jnp.where(owner == me, rank, -1)
-        picked = jnp.where(slot_iota == owned, 1.0, 0.0)
-        code = ids - me * table_rows + 1
-        column = jnp.sum(picked * code.astype(jnp.float32), axis=1, keepdims=True).astype(jnp.int32) - 1
-        high = lax.shift_right_arithmetic(code, 6)
-        digits = jnp.where(owner == me, jnp.concatenate([high, code - high * 64], axis=0), 0)
-        digits = jnp.concatenate([digits, jnp.zeros((6, tokens), jnp.int32)], axis=0).astype(jnp.float32).astype(jnp.bfloat16)
-        spread = lax.dot_general(digits, picked.astype(jnp.bfloat16), COLS_DIMS, preferred_element_type=jnp.float32)
-        rows_out[pl.ds(to, 1), :] = (spread[0:1] * 64.0 + spread[1:2]).astype(jnp.int32) - 1
-        choose = jnp.where(lanes_iota == column, 1.0, 0.0).astype(jnp.bfloat16)
-        send[to] = jnp.dot(choose, table_out[...], preferred_element_type=jnp.float32).astype(jnp.bfloat16)
-        return owner, rank
-
-    owner, rank = build(0)
-    slots_out[...] = jnp.where(rank < SLOTS, owner * SLOTS + rank, -1)
+        return ids, owner, rank.astype(jnp.int32)
+
+    def build(group):
+        columns = []
+        for step in range(4 * group, 4 * group + 4):
+            to = lax.rem(me + step, total)
+            ids, owner, rank = rank_of(to)
+            if step == 0:
+                slots_out[...] = jnp.where(rank < SLOTS, owner * SLOTS + rank, -1)
+            picked = jnp.where(slot_iota == jnp.where(owner == me, rank, -1), 1.0, 0.0)
+            code = ids - me * table_rows + 1
+            columns.append(jnp.sum(picked * code.astype(jnp.float32), axis=1, keepdims=True).astype(jnp.int32) - 1)
+            high = lax.shift_right_arithmetic(code, 6)
+            digits = jnp.where(owner == me, jnp.concatenate([high, code - high * 64], axis=0), 0)
+            digits = jnp.concatenate([digits, jnp.zeros((6, tokens), jnp.int32)], axis=0).astype(jnp.float32).astype(jnp.bfloat16)
+            spread = lax.dot_general(digits, picked.astype(jnp.bfloat16), COLS_DIMS, preferred_element_type=jnp.float32)
+            rows_out[pl.ds(to, 1), :] = (spread[0:1] * 64.0 + spread[1:2]).astype(jnp.int32) - 1
+        choose = jnp.where(lanes_iota == jnp.concatenate(columns, axis=0), 1.0, 0.0).astype(jnp.bfloat16)
+        rows = jnp.dot(choose, table_out[...], preferred_element_type=jnp.float32).astype(jnp.bfloat16)
+        for j in range(4):
+            send[lax.rem(me + 4 * group + j, total)] = rows[j * SLOTS:(j + 1) * SLOTS]
+
     own_rows = pltpu.make_async_copy(send.at[me], got.at[me], local_sem.at[4])
-
-    def build_step(step, carry):
-        build(step)
-        pl.when(step > 1)(lambda: row_copy(step - 1).start())
-        return carry
-
-    lax.fori_loop(1, 6, build_step, 0)
-    own_rows.start()
+    build(0)
     finish(wide(1))
     start(wide(2))
     start(across(1))
-    lax.fori_loop(6, total, build_step, 0)
-    row_copy(total - 1).start()
+    start([row_copy(step) for step in range(1, 4)])
+    build(1)
+    own_rows.start()
+    start([row_copy(step) for step in range(4, 8)])
+    build(2)
+    start([row_copy(step) for step in range(8, 12)])
+    build(3)
+    start([row_copy(step) for step in range(12, 16)])
     finish(wide(2))
     start(wide(3))
     start(across(2))
@@ -741,13 +760,9 @@
         grad_rows, grad_mid, grad_gate_pre, grad_up_proj = [jnp.concatenate(parts, axis=0) for parts in zip(*backs)]
         normed_in = jnp.concatenate([kept[1] for kept in saved], axis=0)
         acts = jnp.concatenate([kept[5] for kept in saved], axis=0)
-        grad_down = lax.dot_general(acts, grad_mid, ROWS_DIMS, preferred_element_type=jnp.float32)
-        grad_gate = lax.dot_general(normed_in, grad_gate_pre, ROWS_DIMS, preferred_element_type=jnp.float32)
-        grad_up = lax.dot_general(normed_in, grad_up_proj, ROWS_DIMS, preferred_element_type=jnp.float32)
-        cube = (2, 2, 2, 2)
         send = pick_rows(slot_place(slots[0]), grad_rows).reshape(groups, SLOTS, dim)
-        out_gate, out_up, out_down, dtable = tail(grad_gate.reshape(cube + (gate_rows, ffn)), grad_up.reshape(cube + (gate_rows, ffn)),
-                                                  grad_down.reshape(cube + (down_rows, dim)), send, row_idx.reshape(1, groups * SLOTS), dtable, rows)
+        out_gate, out_up, out_down, dtable = tail(normed_in, acts, grad_mid, grad_gate_pre, grad_up_proj, send,
+                                                  row_idx.reshape(1, groups * SLOTS), dtable, rows)
         dtable = lax.fori_loop(1, rounds, lambda r, acc: acc + return_round(r, grad_rows), dtable)
         return (loss_total / total_tokens, dtable, out_gate, out_up, out_down)
 

time: 423 us -> 415 us (0.981)
  matrix products: 38.5 us -> 22.7 us
  other arithmetic: 10.3 us -> 16.6 us
    dot_general x3 -> x0, matrix products: 13.4 us -> none  [the longest x1 4.5 us: device_step(): lax.dot_general(acts, grad_mid, ROWS_DIMS, preferred_element_type=jnp.flo...]
    concatenate x0 -> x5, other arithmetic: none -> 6.39 us  [the longest x3 3.9 us: device_step(): jnp.concatenate(parts, axis=0)]
    unnamed x99 -> x87, local copies, waits for them, and re-layouts: 13.9 us -> 14.3 us
where the time goes in v6:
time: 415 us; the launch traced here: 409 us
  Pallas kernels  345 us (83%)
  matrix products  22.7 us (5%)
  local copies, waits for them, and re-layouts  18.9 us (5%)
  other arithmetic  16.6 us (4%)
    pallas_call x1, Pallas kernels, head(): pl.pallas_call(functools.partial(head_kernel, vocab_rows, chunks), in_spe...  163 us
    pallas_call x1, Pallas kernels, tail(): pl.pallas_call(functools.partial(tail_kernel, table_rows), in_specs=[vmem...  112 us
    pallas_call x1, Pallas kernels, front(): pl.pallas_call(functools.partial(front_kernel, rows), in_specs=[anywhere,...  70.1 us
    unnamed x87, local copies, waits for them, and re-layouts  14.3 us

profile of v6, /device:TPU:0, one launch (start us, length us, event | category | flops | bytes accessed | tf_op | source)
XLA Modules:
  0.0 408.7 jit_solution(12778803169850659155)
XLA Ops:
  2.8 70.1 %front_all.1 = (s32[16,2,512]{2,1,0:T(2,128)}, bf16[2048,768]{1,0:T(8,128)(2,1)}, bf16[2,2,2,2,48,2048]{5,4,3,2,1,0:T(8,128)(2,1)}, bf16[2,2,2,2,48,2048]{5,4,3,...) custom-call(s32[2,512]{1,0:T(2,128)} %pad_add_fusion.pack_hbm, ...), custom_call_target="tpu_custom_call" | custom-call | flops 6442450944 | bytes 20971520 | tf_op jit(solution)/shard_map/front_all/pallas_call | solution.py:655
  72.9 1.3 reduce_max.9
  74.9 1.4 reshape.183.row_ref
  84.1 1.2 copy-done.10
  85.3 2.2 fusion.54
  87.7 1.1 fusion.89
  89.5 2.2 fusion.50
  91.7 1.1 fusion.83
  92.8 1.6 pad_maximum_fusion.acts_ref
  96.4 162.9 %head_all.1 = (f32[512,768]{1,0:T(8,128)}, f32[2048,768]{1,0:T(8,128)}, f32[3,512]{1,0:T(4,128)}) custom-call(bf16[8,64,768]{2,1,0:T(8,128)(2,1)} %bitcast.127, bf16[2048,768]{1,0:T(8,128)(2,1)} %get-tuple-element.322.table_ref, s32[16,512]{1,0:T(8,128)} %reshape.181.lab_ref), custom_call_target="tpu_custom_call" | custom-call | flops 77309411328 | bytes 6291456 | tf_op jit(solution)/shard_map/head_all/pallas_call | solution.py:306
  259.4 1.5 reduce_sum.137
  261.5 1.9 fusion.88
  263.9 1.4 copy-done.39
  265.3 3.2 fusion.63
  268.5 1.5 fusion.69
  275.1 1.2 fusion.101
  276.3 1.5 pad_maximum_fusion.2.up_ref
  278.1 1.5 pad_maximum_fusion.1.gate_ref
  280.6 1.0 fusion.71
  281.7 1.2 fusion.70
  282.9 2.8 add_add_fusion.2
  285.7 111.8 %tail_all.1 = (f32[48,2048]{1,0:T(8,128)}, f32[48,2048]{1,0:T(8,128)}, f32[128,768]{1,0:T(8,128)}, f32[2008,768]{1,0:T(8,128)}) custom-call(bf16[512,768]{1,0:T(8,128)(2,1)} %pad_maximum_fusion.5.u_ref, bf16[512,2048]{1,0:T(8,128)(2,1)} %pad_maximum_fusion.acts_ref, bf16[512,768]{1,0:T(8,128)(2,1)} %pad_maximum_fusion.6.mid_ref, ...), custom_call_target="tpu_custom_call" | custom-call | flops 9474932736 | bytes 41943040 | tf_op jit(solution)/shard_map/tail_all/pallas_call | solution.py:494
  397.6 1.4 while.29
  399.0 5.9 %copy.37 = f32[2008,768]{1,0:T(8,128)} copy(f32[2008,768]{1,0:T(8,128)} %get-tuple-element.672) | data formatting | bytes 12337152
  (114 shorter events, 21.9 us)
Async XLA Ops:
  78.2 2.8 copy-start.12
  78.2 13.4 %copy-start.3 = (bf16[512,768]{1,0:T(8,128)(2,1)}, bf16[512,768]{1,0:T(8,128)(2,1)S(1)}, u32[]{:S(2)}) copy-start(bf16[512,768]{1,0:T(8,128)(2,1)S(1)} %get-tuple-element.318) | copy-start | bytes 2359300
  79.0 4.0 copy-start.29
  79.0 4.0 copy-start.31
  83.0 6.4 %copy-start.42 = (bf16[256,2048]{1,0:T(8,128)(2,1)}, bf16[256,2048]{1,0:T(8,128)(2,1)S(1)}, u32[]{:S(2)}) copy-start(bf16[256,2048]{1,0:T(8,128)(2,1)S(1)} %convolution_convert_fusion.3) | copy-start | bytes 3145732
  83.0 2.3 copy-start.10
  85.3 2.4 copy-start.38
  88.8 6.1 %copy-start.5 = (bf16[256,768]{1,0:T(8,128)(2,1)}, bf16[256,768]{1,0:T(8,128)(2,1)S(1)}, u32[]{:S(2)}) copy-start(bf16[256,768]{1,0:T(8,128)(2,1)S(1)} %get-tuple-element.480) | copy-start | bytes 1179652
  89.5 5.5 %copy-start.21 = (f32[256]{0:T(256)}, f32[256]{0:T(256)S(1)}, u32[]{:S(2)}) copy-start(f32[256]{0:T(256)S(1)} %get-tuple-element.472) | copy-start | bytes 3076
  259.3 4.1 %copy-start.2 = (f32[512,768]{1,0:T(8,128)S(1)}, f32[512,768]{1,0:T(8,128)}, u32[]{:S(2)}) copy-start(f32[512,768]{1,0:T(8,128)} %get-tuple-element.324) | copy-start | bytes 4718596
  259.3 4.1 %copy-start.6 = (bf16[256,768]{1,0:T(8,128)(2,1)S(1)}, bf16[256,768]{1,0:T(8,128)(2,1)}, u32[]{:S(2)}) copy-start(bf16[256,768]{1,0:T(8,128)(2,1)} %copy-done.5) | copy-start | bytes 1179652
  259.3 4.1 %copy-start.8 = (bf16[256,768]{1,0:T(8,128)(2,1)S(1)}, bf16[256,768]{1,0:T(8,128)(2,1)}, u32[]{:S(2)}) copy-start(bf16[256,768]{1,0:T(8,128)(2,1)} %copy-done.7) | copy-start | bytes 1179652
  259.3 4.1 %copy-start.20 = (f32[768]{0:T(1024)S(1)}, f32[768]{0:T(1024)}, u32[]{:S(2)}) copy-start(f32[768]{0:T(1024)} %param.19) | copy-start | bytes 9220
  259.4 4.1 %copy-start.22 = (f32[256]{0:T(256)S(1)}, f32[256]{0:T(256)}, u32[]{:S(2)}) copy-start(f32[256]{0:T(256)} %copy-done.21) | copy-start | bytes 3076
  259.4 4.1 %copy-start.24 = (f32[256]{0:T(256)S(1)}, f32[256]{0:T(256)}, u32[]{:S(2)}) copy-start(f32[256]{0:T(256)} %copy-done.23) | copy-start | bytes 3076
  259.4 4.1 %copy-start.27 = (f32[256]{0:T(256)S(1)}, f32[256]{0:T(256)}, u32[]{:S(2)}) copy-start(f32[256]{0:T(256)} %get-tuple-element.471) | copy-start | bytes 3076
  259.4 4.1 %copy-start.28 = (f32[256]{0:T(256)S(1)}, f32[256]{0:T(256)}, u32[]{:S(2)}) copy-start(f32[256]{0:T(256)} %get-tuple-element.469) | copy-start | bytes 3076
  265.3 3.2 copy-start.41
  265.3 3.2 copy-start.43
  268.5 2.5 copy-start.37
  280.4 2.5 copy-start
  399.0 5.9 %copy-start.18 = (f32[48,2048]{1,0:T(8,128)S(1)}, f32[48,2048]{1,0:T(8,128)}, u32[]{:S(2)}) copy-start(f32[48,2048]{1,0:T(8,128)} %get-tuple-element.673) | copy-start | bytes 1179652
  399.0 6.7 %copy-start.17 = (f32[48,2048]{1,0:T(8,128)S(1)}, f32[48,2048]{1,0:T(8,128)}, u32[]{:S(2)}) copy-start(f32[48,2048]{1,0:T(8,128)} %get-tuple-element.674) | copy-start | bytes 1179652
  399.0 7.4 %copy-start.16 = (f32[128,768]{1,0:T(8,128)S(1)}, f32[128,768]{1,0:T(8,128)}, u32[]{:S(2)}) copy-start(f32[128,768]{1,0:T(8,128)} %get-tuple-element.675) | copy-start | bytes 1179652
  (17 other events, 27.0 us)

commit v7 on v6

--- a/solution.py
+++ b/solution.py
@@ -57,13 +57,13 @@
 CUBE_BITS = 3
 PARTS = 3
 VOCAB_TILE = 256
-STAT_ROWS = 4
+STAT_ROWS = 2
 MESH_ID = pl.DeviceIdType.MESH
 PAD_LOGIT = -1e30
 
 
 def head_kernel(vocab_rows, chunks, z_hbm, table_ref, lab_ref, dz_ref, dtable_ref, loss_ref,
-                zbuf, lbuf, gbuf, dzbuf, got_core, got_one, got_two, got_three, stats, labs, norm,
+                zbuf, lbuf, gbuf, dzbuf, got_core, got_one, got_two, got_three, stats, labs, norm, loss_acc,
                 local_sem, ag_send, ag_recv, rs_send, rs_recv, st_send, st_recv, lab_send, lab_recv):
     me = lax.axis_index('fsdp')
     total = 16
@@ -86,7 +86,7 @@
     own = pltpu.make_async_copy(z_hbm, zbuf.at[:, pos[2], pos[1], pos[0], core], local_sem)
     own.start()
     dtable_ref[...] = jnp.zeros_like(dtable_ref)
-    loss_ref[...] = jnp.zeros_like(loss_ref)
+    loss_acc[...] = jnp.zeros_like(loss_acc)
     labs[me] = jnp.zeros((1, half), jnp.float32)
     own.wait()
     pl.semaphore_wait(barrier, total - 1)
@@ -193,18 +193,17 @@
             hits.append(jnp.sum(jnp.where(row_ids == lab - tile * VOCAB_TILE, logits, 0.0), axis=0, keepdims=True))
         top = functools.reduce(jnp.maximum, tops)
         exp_sum = sum(s * jnp.exp(t - top) for s, t in zip(sums, tops))
-        stats[chunk, me, part:part + 1, :] = top
-        stats[chunk, me, 2 + part:3 + part, :] = exp_sum
+        stats[chunk, me, part:part + 1, :] = top + jnp.log(exp_sum)
         labs[me] += sum(hits)
 
     def combine(chunk):
         for part in range(2):
             tops = stats[chunk, :, part, :]
             top = jnp.max(tops, axis=0, keepdims=True)
-            exp_sum = jnp.sum(stats[chunk, :, 2 + part, :] * jnp.exp(tops - top), axis=0, keepdims=True)
+            exp_sum = jnp.sum(jnp.exp(tops - top), axis=0, keepdims=True)
             norm[part:part + 1, :] = top
             norm[2 + part:3 + part, :] = 1.0 / exp_sum
-            loss_ref[part:part + 1, :] += top + jnp.log(exp_sum)
+            loss_acc[...] += top + jnp.log(exp_sum)
 
     def table_half(chunk, which):
         slot = lax.rem(chunk, 2)
@@ -290,7 +289,7 @@
 
     lax.fori_loop(0, chunks + 4, body, 0)
     finish(lab_copies())
-    loss_ref[2:3, :] = -jnp.sum(labs[...], axis=0)
+    loss_ref[...] = jnp.broadcast_to(jnp.sum(loss_acc[...] - jnp.sum(labs[...], axis=0), axis=1, keepdims=True), loss_ref.shape)
 
 
 def head(z_local, table_padded, lab_rows, vocab_rows):
@@ -309,7 +308,7 @@
         out_specs=[vmem, vmem, vmem],
         out_shape=[jax.ShapeDtypeStruct((tokens, dim), f32),
                    jax.ShapeDtypeStruct((padded, dim), f32),
-                   jax.ShapeDtypeStruct((3, 8 * UNIT), f32)],
+                   jax.ShapeDtypeStruct((1, 128), f32)],
         scratch_shapes=[pltpu.VMEM((chunks, 2, 2, 2, 2, UNIT, dim), bf16),
                         pltpu.VMEM((2, padded, chunk_tokens), f32),
                         pltpu.VMEM((padded, chunk_tokens), bf16),
@@ -321,6 +320,7 @@
                         pltpu.VMEM((chunks, 16, STAT_ROWS, 8 * UNIT), f32),
                         pltpu.VMEM((16, 1, 8 * UNIT), f32),
                         pltpu.VMEM((8, 8 * UNIT), f32),
+                        pltpu.VMEM((1, 8 * UNIT), f32),
                         sems(()),
                         sems((chunks, 10)), sems((chunks, 10)),
                         sems((chunks, 10)), sems((chunks, 10)),
@@ -506,7 +506,7 @@
 
 def front_kernel(table_rows, pack_hbm, table_ref, gate_hbm, up_hbm, down_hbm,
                  pack_out, table_out, gate_out, up_out, down_out, x_out, slots_out, rows_out, rank_out,
-                 send, got, before_ref, local_sem, id_send, id_recv, w_send, w_recv, c_send, c_recv, row_send, row_recv):
+                 send, got, before_ref, rank_top, local_sem, id_send, id_recv, w_send, w_recv, c_send, c_recv, row_send, row_recv):
     me = lax.axis_index('fsdp')
     total = 16
     core = lax.rem(me, 2)
@@ -574,7 +574,7 @@
     table_out[table_rows:padded, :] = jnp.zeros((padded - table_rows, dim), table_out.dtype)
     earlier = lax.broadcasted_iota(jnp.int32, (tokens, tokens), 0) < lax.broadcasted_iota(jnp.int32, (tokens, tokens), 1)
     before_ref[...] = jnp.where(earlier, 1.0, 0.0).astype(jnp.bfloat16)
-    rank_out[...] = jnp.zeros_like(rank_out)
+    rank_top[...] = jnp.zeros_like(rank_top)
     for load in loads:
         load.wait()
     finish(id_copies())
@@ -591,7 +591,7 @@
         hot = jnp.where(dev_iota == owner, 1.0, 0.0)
         before = jnp.dot(hot.astype(jnp.bfloat16), before_ref[...], preferred_element_type=jnp.float32)
         rank = jnp.sum(hot * before, axis=0, keepdims=True)
-        rank_out[...] = jnp.maximum(rank_out[...], rank)
+        rank_top[...] = jnp.maximum(rank_top[...], rank)
         return ids, owner, rank.astype(jnp.int32)
 
     def build(group):
@@ -626,6 +626,7 @@
     build(2)
     start([row_copy(step) for step in range(8, 12)])
     build(3)
+    rank_out[...] = jnp.broadcast_to(jnp.max(rank_top[...], axis=1, keepdims=True), rank_out.shape).astype(jnp.int32)
     start([row_copy(step) for step in range(12, 16)])
     finish(wide(2))
     start(wide(3))
@@ -659,8 +660,8 @@
         out_shape=[jax.ShapeDtypeStruct((16,) + packed.shape, jnp.int32), jax.ShapeDtypeStruct((padded, dim), bf16)]
         + [jax.ShapeDtypeStruct((2, 2, 2, 2) + shard.shape, bf16) for shard in shards]
         + [jax.ShapeDtypeStruct((tokens, dim), bf16), jax.ShapeDtypeStruct((1, tokens), jnp.int32),
-           jax.ShapeDtypeStruct((16, SLOTS), jnp.int32), jax.ShapeDtypeStruct((1, tokens), jnp.float32)],
-        scratch_shapes=[pltpu.VMEM((16, SLOTS, dim), bf16), pltpu.VMEM((16, SLOTS, dim), bf16), pltpu.VMEM((tokens, tokens), bf16),
+           jax.ShapeDtypeStruct((16, SLOTS), jnp.int32), jax.ShapeDtypeStruct((1, 128), jnp.int32)],
+        scratch_shapes=[pltpu.VMEM((16, SLOTS, dim), bf16), pltpu.VMEM((16, SLOTS, dim), bf16), pltpu.VMEM((tokens, tokens), bf16), pltpu.VMEM((1, tokens), jnp.float32),
                         sems((5,)), sems((16,)), sems((16,)), sems((4, 3)), sems((4, 3)), sems((4, 3)), sems((4, 3)), sems((16,)), sems((16,))],
         compiler_params=pltpu.CompilerParams(vmem_limit_bytes=60 * 1024 * 1024, collective_id=3, has_side_effects=True),
         cost_estimate=pl.CostEstimate(flops=4 * 16 * SLOTS * padded * dim, bytes_accessed=20 * 1024 * 1024, transcendentals=0),
@@ -703,7 +704,7 @@
         w_gate = w_gate.reshape(groups * gate_rows, ffn)
         w_up = w_up.reshape(groups * gate_rows, ffn)
         w_down = w_down.reshape(groups * down_rows, dim)
-        rounds = jnp.max(top_rank).astype(jnp.int32) // SLOTS + 1
+        rounds = top_rank[0, 0] // SLOTS + 1
         slot_ids = jnp.arange(SLOTS, dtype=jnp.int32)
 
         def ranks(round_idx):
@@ -744,22 +745,13 @@
 
         emb_rows = lax.fori_loop(1, rounds, lambda r, acc: acc + fetch_round(r), emb_rows)
 
-        normed, saved = [], []
-        for m in range(micro_count):
-            out, kept = mlp_forward(emb_rows[m * tok_micro:(m + 1) * tok_micro], gain_in, gain_out, w_gate, w_up, w_down)
-            normed.append(out)
-            saved.append(kept)
-
+        normed_out, saved = mlp_forward(emb_rows, gain_in, gain_out, w_gate, w_up, w_down)
         chunks = tok_dev // UNIT
         lab_rows = jnp.transpose(packed_all[:, 1].reshape(groups, chunks, UNIT), (1, 0, 2)).reshape(2 * chunks, groups * UNIT // 2)
-        dz, dtable, loss_rows = head(jnp.concatenate(normed, axis=0), table_padded, lab_rows, rows)
-        loss_total = jnp.sum(loss_rows)
-        grad_normed = [dz[m * tok_micro:(m + 1) * tok_micro] for m in range(micro_count)]
-
-        backs = [mlp_backward(saved[m], grad_normed[m], gain_in, gain_out, w_gate, w_up, w_down) for m in range(micro_count)]
-        grad_rows, grad_mid, grad_gate_pre, grad_up_proj = [jnp.concatenate(parts, axis=0) for parts in zip(*backs)]
-        normed_in = jnp.concatenate([kept[1] for kept in saved], axis=0)
-        acts = jnp.concatenate([kept[5] for kept in saved], axis=0)
+        dz, dtable, loss_rows = head(normed_out, table_padded, lab_rows, rows)
+        loss_total = loss_rows[0, 0]
+        grad_rows, grad_mid, grad_gate_pre, grad_up_proj = mlp_backward(saved, dz, gain_in, gain_out, w_gate, w_up, w_down)
+        normed_in, acts = saved[1], saved[5]
         send = pick_rows(slot_place(slots[0]), grad_rows).reshape(groups, SLOTS, dim)
         out_gate, out_up, out_down, dtable = tail(normed_in, acts, grad_mid, grad_gate_pre, grad_up_proj, send,
                                                   row_idx.reshape(1, groups * SLOTS), dtable, rows)

time: 415 us -> 404 us (0.973)
  other arithmetic: 16.6 us -> 7.13 us
    concatenate x6 -> x0, other arithmetic: 7.34 us -> none  [the longest x3 3.9 us: device_step(): jnp.concatenate(parts, axis=0)]
    unnamed x87 -> x73, local copies, waits for them, and re-layouts: 14.3 us -> 12.9 us
where the time goes in v7:
time: 404 us; the launch traced here: 397 us
  Pallas kernels  342 us (85%)
  matrix products  23.4 us (6%)
  local copies, waits for them, and re-layouts  17.5 us (4%)
  other arithmetic  7.13 us (2%)
  between operations  5.98 us (1%)
    pallas_call x1, Pallas kernels, head(): pl.pallas_call(functools.partial(head_kernel, vocab_rows, chunks), in_spe...  159 us
    pallas_call x1, Pallas kernels, tail(): pl.pallas_call(functools.partial(tail_kernel, table_rows), in_specs=[vmem...  112 us
    pallas_call x1, Pallas kernels, front(): pl.pallas_call(functools.partial(front_kernel, rows), in_specs=[anywhere,...  70.1 us
    unnamed x73, local copies, waits for them, and re-layouts  12.9 us

profile of v7, /device:TPU:0, one launch (start us, length us, event | category | flops | bytes accessed | tf_op | source)
XLA Modules:
  0.0 397.3 jit_solution(10502332964345272875)
XLA Ops:
  0.6 0.8 stack_reshape.6
  1.4 0.8 stack_reshape.7
  2.8 70.1 %front_all.1 = (s32[16,2,512]{2,1,0:T(2,128)}, bf16[2048,768]{1,0:T(8,128)(2,1)}, bf16[2,2,2,2,48,2048]{5,4,3,2,1,0:T(8,128)(2,1)}, bf16[2,2,2,2,48,2048]{5,4,3,...) custom-call(s32[2,512]{1,0:T(2,128)} %pad_add_fusion.pack_hbm, ...), custom_call_target="tpu_custom_call" | custom-call | flops 6442450944 | bytes 20971520 | tf_op jit(solution)/shard_map/front_all/pallas_call | solution.py:656
  75.4 1.4 reshape.149.row_ref
  76.8 0.9 slice_reduce_fusion
  77.7 0.9 copy.16
  80.7 4.0 %convolution_convert_fusion.1 = bf16[512,2048]{1,0:T(8,128)(2,1)S(1)} fusion(bf16[512,768]{1,0:T(8,128)(2,1)S(1)} %fusion.72.u_ref, bf16[768,2048]{1,0:T(8,128)(2,1)} %bitcast.130), kind=kOutput, calls=%fused_computation.109 | convolution fusion | flops 1611661312 | bytes 6029312 | tf_op jit(solution)/shard_map/dot_general | solution.py:28
  84.8 3.6 fusion.50
  88.4 1.9 fusion.64
  91.2 1.1 fusion.66
  92.3 159.3 %head_all.1 = (f32[512,768]{1,0:T(8,128)}, f32[2048,768]{1,0:T(8,128)}, f32[1,128]{1,0:T(1,128)}) custom-call(bf16[8,64,768]{2,1,0:T(8,128)(2,1)} %bitcast.115, bf16[2048,768]{1,0:T(8,128)(2,1)} %get-tuple-element.322.table_ref, s32[16,512]{1,0:T(8,128)} %reshape.147.lab_ref), custom_call_target="tpu_custom_call" | custom-call | flops 77309411328 | bytes 6291456 | tf_op jit(solution)/shard_map/head_all/pallas_call | solution.py:305
  252.5 1.9 fusion.69
  254.9 1.4 copy-done.32
  256.3 5.2 %fusion.59 = (bf16[512,2048]{1,0:T(8,128)(2,1)S(1)}, bf16[512,2048]{1,0:T(8,128)(2,1)S(1)}) fusion(bf16[512,2048]{1,0:T(8,128)(2,1)} %copy-done.34, bf16[512,2048]{1,0:T(8,128)(2,1)} %get-tuple-element.457, bf16[512,768]{1,0:T(8,128)(2,1)S(1)} %fusion.81.mid_ref, bf16[2048,768]{1,0:T(8,128)(2,1)S(1)} %bitcast.133), kind=kOutput, calls=%fused_computation.101 | convolution fusion | flops 1626341376 | bytes 12320768 | tf_op jit(solution)/shard_map/dot_general | solution.py:45
  261.6 1.8 fusion.83
  263.6 1.5 copy-done.29
  265.2 2.0 fusion.77
  267.2 1.1 reduce-precision_convert_fusion.3
  269.0 1.0 fusion.61
  270.1 1.0 fusion.60
  271.1 2.8 add_add_fusion.2
  273.9 112.2 %tail_all.1 = (f32[48,2048]{1,0:T(8,128)}, f32[48,2048]{1,0:T(8,128)}, f32[128,768]{1,0:T(8,128)}, f32[2008,768]{1,0:T(8,128)}) custom-call(bf16[512,768]{1,0:T(8,128)(2,1)} %copy-done.9, bf16[512,2048]{1,0:T(8,128)(2,1)} %copy-done.36, bf16[512,768]{1,0:T(8,128)(2,1)} %copy-done.13, bf16[512,2048]{1,0:T(8,128)(2,1)} %copy-done.35, ...), custom_call_target="tpu_custom_call" | custom-call | flops 9474932736 | bytes 41943040 | tf_op jit(solution)/shard_map/tail_all/pallas_call | solution.py:494
  386.2 1.4 while.29
  387.6 5.9 %copy.37 = f32[2008,768]{1,0:T(8,128)} copy(f32[2008,768]{1,0:T(8,128)} %get-tuple-element.650) | data formatting | bytes 12337152
  (82 shorter events, 7.2 us)
Async XLA Ops:
  78.8 5.9 %copy-start.8 = (s32[16,2,512]{2,0,1:T(8,128)}, s32[16,2,512]{2,0,1:T(8,128)S(1)}, u32[]{:S(2)}) copy-start(s32[16,2,512]{2,0,1:T(8,128)S(1)} %get-tuple-element.658) | copy-start | bytes 196612
  78.8 9.6 %copy-start.5 = (bf16[512,768]{1,0:T(8,128)(2,1)}, bf16[512,768]{1,0:T(8,128)(2,1)S(1)}, u32[]{:S(2)}) copy-start(bf16[512,768]{1,0:T(8,128)(2,1)S(1)} %get-tuple-element.318) | copy-start | bytes 2359300
  79.6 5.1 %copy-start.21 = (f32[512]{0:T(512)}, f32[512]{0:T(512)S(1)}, u32[]{:S(2)}) copy-start(f32[512]{0:T(512)S(1)} %get-tuple-element.453) | copy-start | bytes 6148
  80.6 4.1 %copy-start.9 = (bf16[512,768]{1,0:T(8,128)(2,1)}, bf16[512,768]{1,0:T(8,128)(2,1)S(1)}, u32[]{:S(2)}) copy-start(bf16[512,768]{1,0:T(8,128)(2,1)S(1)} %fusion.72.u_ref) | copy-start | bytes 2359300
  80.7 4.1 %copy-start.28 = (bf16[2,2,2,2,48,2048]{5,4,3,2,1,0:T(8,128)(2,1)S(1)}, bf16[2,2,2,2,48,2048]{5,4,3,2,1,0:T(8,128)(2,1)}, u32[]{:S(2)}) copy-start(bf16[2,2,2,2,48,2048]{5,4,3,2,1,0:T(8,128)(2,1)} %get-tuple-element.320) | copy-start | bytes 9437188
  84.7 3.6 copy-start.34
  84.8 3.6 copy-start.31
  88.4 2.8 copy-start.17
  251.7 2.7 copy-start.2
  251.7 2.7 copy-start.4
  251.7 2.7 copy-start.18
  251.7 2.7 copy-start.20
  251.7 2.7 copy-start.23
  256.3 5.2 %copy-start.13 = (bf16[512,768]{1,0:T(8,128)(2,1)}, bf16[512,768]{1,0:T(8,128)(2,1)S(1)}, u32[]{:S(2)}) copy-start(bf16[512,768]{1,0:T(8,128)(2,1)S(1)} %fusion.81.mid_ref) | copy-start | bytes 2359300
  256.3 5.2 %copy-start.30 = (bf16[2,2,2,2,48,2048]{5,4,3,2,1,0:T(8,128)(2,1)S(1)}, bf16[2,2,2,2,48,2048]{5,4,3,2,1,0:T(8,128)(2,1)}, u32[]{:S(2)}) copy-start(bf16[2,2,2,2,48,2048]{5,4,3,2,1,0:T(8,128)(2,1)} %get-tuple-element.319) | copy-start | bytes 9437188
  261.5 2.1 copy-start.33
  261.5 2.1 copy-start.6
  261.5 2.1 copy-start.26
  261.6 3.6 copy-start.29
  265.2 2.0 copy-start.24
  268.3 2.8 copy-start
  387.5 5.9 %copy-start.16 = (f32[48,2048]{1,0:T(8,128)S(1)}, f32[48,2048]{1,0:T(8,128)}, u32[]{:S(2)}) copy-start(f32[48,2048]{1,0:T(8,128)} %get-tuple-element.651) | copy-start | bytes 1179652
  387.5 6.7 %copy-start.15 = (f32[48,2048]{1,0:T(8,128)S(1)}, f32[48,2048]{1,0:T(8,128)}, u32[]{:S(2)}) copy-start(f32[48,2048]{1,0:T(8,128)} %get-tuple-element.652) | copy-start | bytes 1179652
  387.5 7.4 %copy-start.14 = (f32[128,768]{1,0:T(8,128)S(1)}, f32[128,768]{1,0:T(8,128)}, u32[]{:S(2)}) copy-start(f32[128,768]{1,0:T(8,128)} %get-tuple-element.653) | copy-start | bytes 1179652
  (10 other events, 15.4 us)

commit v8 on v7

--- a/solution.py
+++ b/solution.py
@@ -8,6 +8,7 @@
 
 NORM_EPS = 1e-6
 SLOTS = 64
+BACK_SLOTS = 56
 
 
 def rms_scale(values, gain_vec):
@@ -442,18 +443,20 @@
         copy.wait()
     slots, dim = rows_got.shape[0] * rows_got.shape[1], rows_got.shape[2]
 
+    pair = 2 * rows_got.shape[1]
+
     def split_rows(s, carry):
-        vals = rows_got[s]
-        at = pl.multiple_of(s * SLOTS, SLOTS)
+        vals = rows_got[pl.ds(2 * s, 2)].reshape(pair, dim)
+        at = pl.multiple_of(s * pair, pair)
         high = vals.astype(jnp.bfloat16)
         rest = vals - high.astype(jnp.float32)
         mid = rest.astype(jnp.bfloat16)
-        split[pl.ds(at, SLOTS), :] = high
-        split[pl.ds(slots + at, SLOTS), :] = mid
-        split[pl.ds(2 * slots + at, SLOTS), :] = (rest - mid.astype(jnp.float32)).astype(jnp.bfloat16)
+        split[pl.ds(at, pair), :] = high
+        split[pl.ds(slots + at, pair), :] = mid
+        split[pl.ds(2 * slots + at, pair), :] = (rest - mid.astype(jnp.float32)).astype(jnp.bfloat16)
         return carry
 
-    lax.fori_loop(0, total, split_rows, 0)
+    lax.fori_loop(0, total // 2, split_rows, 0)
 
     def add_rows(first, count):
         ids = lax.broadcasted_iota(jnp.int32, (count, slots), 0) + first
@@ -678,11 +681,7 @@
 
 
 def pick_rows(select, values):
-    total = None
-    for part in split3(values):
-        term = jnp.dot(select, part, preferred_element_type=jnp.float32)
-        total = term if total is None else total + term
-    return total
+    return jnp.dot(select, jnp.concatenate(split3(values), axis=0), preferred_element_type=jnp.float32)
 
 
 def solution(mesh):
@@ -705,43 +704,43 @@
         w_up = w_up.reshape(groups * gate_rows, ffn)
         w_down = w_down.reshape(groups * down_rows, dim)
         rounds = top_rank[0, 0] // SLOTS + 1
-        slot_ids = jnp.arange(SLOTS, dtype=jnp.int32)
-
-        def ranks(round_idx):
+        back_rounds = top_rank[0, 0] // BACK_SLOTS + 1
+
+        def ranks(round_idx, count):
             ids_all, round_idx = lax.optimization_barrier((packed_all[:, 0], round_idx))
             owner = ids_all // rows
             owner_hot = owner[:, :, None] == jnp.arange(groups, dtype=jnp.int32)
             tri = jnp.tril(jnp.ones((tok_dev, tok_dev), jnp.bfloat16), -1)
             before = jnp.einsum('tu,suo->sto', tri, owner_hot.astype(jnp.bfloat16), preferred_element_type=jnp.float32)
             rank = jnp.sum(jnp.where(owner_hot, before, 0.0), axis=-1).astype(jnp.int32)
-            return owner, ids_all - owner * rows, rank - round_idx * SLOTS
-
-        def owned_rows(owner, local, rank):
-            hit = (owner == me)[:, None, :] & (rank[:, None, :] == slot_ids[None, :, None])
-            return (jnp.sum(jnp.where(hit, local[:, None, :] + 1, 0), axis=-1) - 1).reshape(groups * SLOTS)
-
-        def my_slots(owner, rank):
+            return owner, ids_all - owner * rows, rank - round_idx * count
+
+        def owned_rows(owner, local, rank, count):
+            hit = (owner == me)[:, None, :] & (rank[:, None, :] == jnp.arange(count, dtype=jnp.int32)[None, :, None])
+            return (jnp.sum(jnp.where(hit, local[:, None, :] + 1, 0), axis=-1) - 1).reshape(groups * count)
+
+        def my_slots(owner, rank, count):
             mine = lax.dynamic_index_in_dim(owner, me, 0, keepdims=False)
             off = lax.dynamic_index_in_dim(rank, me, 0, keepdims=False)
-            return jnp.where((off >= 0) & (off < SLOTS), mine * SLOTS + off, -1)
-
-        def slot_place(slot_row):
-            return (jnp.arange(groups * SLOTS, dtype=jnp.int32)[:, None] == slot_row[None, :]).astype(jnp.bfloat16)
+            return jnp.where((off >= 0) & (off < count), mine * count + off, -1)
+
+        def slot_place(slot_row, count):
+            return (jnp.arange(groups * count, dtype=jnp.int32)[:, None] == slot_row[None, :]).astype(jnp.bfloat16)
 
         def fetch_round(round_idx):
-            owner, local, rank = ranks(round_idx)
-            select = (owned_rows(owner, local, rank)[:, None] == jnp.arange(rows, dtype=jnp.int32)[None, :]).astype(jnp.bfloat16)
+            owner, local, rank = ranks(round_idx, SLOTS)
+            select = (owned_rows(owner, local, rank, SLOTS)[:, None] == jnp.arange(rows, dtype=jnp.int32)[None, :]).astype(jnp.bfloat16)
             send = jnp.dot(select, table_shard, preferred_element_type=jnp.float32).astype(jnp.bfloat16)
             got = lax.all_to_all(send.reshape(groups, SLOTS, dim), 'fsdp', 0, 0).reshape(groups * SLOTS, dim)
-            place = slot_place(my_slots(owner, rank))
+            place = slot_place(my_slots(owner, rank, SLOTS), SLOTS)
             return lax.dot_general(place, got, ROWS_DIMS, preferred_element_type=jnp.float32).astype(jnp.bfloat16)
 
         def return_round(round_idx, grad_rows):
-            owner, local, rank = ranks(round_idx)
-            send = pick_rows(slot_place(my_slots(owner, rank)), grad_rows)
-            got = lax.all_to_all(send.reshape(groups, SLOTS, dim), 'fsdp', 0, 0).reshape(groups * SLOTS, dim)
-            select = (jnp.arange(rows, dtype=jnp.int32)[:, None] == owned_rows(owner, local, rank)[None, :]).astype(jnp.bfloat16)
-            return pick_rows(select, got)
+            owner, local, rank = ranks(round_idx, BACK_SLOTS)
+            send = pick_rows(slot_place(jnp.tile(my_slots(owner, rank, BACK_SLOTS), 3), BACK_SLOTS), grad_rows)
+            got = lax.all_to_all(send.reshape(groups, BACK_SLOTS, dim), 'fsdp', 0, 0).reshape(groups * BACK_SLOTS, dim)
+            row_of = jnp.tile(owned_rows(owner, local, rank, BACK_SLOTS), 3)
+            return pick_rows((jnp.arange(rows, dtype=jnp.int32)[:, None] == row_of[None, :]).astype(jnp.bfloat16), got)
 
         emb_rows = lax.fori_loop(1, rounds, lambda r, acc: acc + fetch_round(r), emb_rows)
 
@@ -752,10 +751,12 @@
         loss_total = loss_rows[0, 0]
         grad_rows, grad_mid, grad_gate_pre, grad_up_proj = mlp_backward(saved, dz, gain_in, gain_out, w_gate, w_up, w_down)
         normed_in, acts = saved[1], saved[5]
-        send = pick_rows(slot_place(slots[0]), grad_rows).reshape(groups, SLOTS, dim)
+        first_rank = slots[0] % SLOTS
+        back_slots = jnp.where((slots[0] >= 0) & (first_rank < BACK_SLOTS), slots[0] // SLOTS * BACK_SLOTS + first_rank, -1)
+        send = pick_rows(slot_place(jnp.tile(back_slots, 3), BACK_SLOTS), grad_rows).reshape(groups, BACK_SLOTS, dim)
         out_gate, out_up, out_down, dtable = tail(normed_in, acts, grad_mid, grad_gate_pre, grad_up_proj, send,
-                                                  row_idx.reshape(1, groups * SLOTS), dtable, rows)
-        dtable = lax.fori_loop(1, rounds, lambda r, acc: acc + return_round(r, grad_rows), dtable)
+                                                  row_idx[:, :BACK_SLOTS].reshape(1, groups * BACK_SLOTS), dtable, rows)
+        dtable = lax.fori_loop(1, back_rounds, lambda r, acc: acc + return_round(r, grad_rows), dtable)
         return (loss_total / total_tokens, dtable, out_gate, out_up, out_down)
 
     row_spec = P('fsdp', None)

time: 404 us -> 397 us (0.983)
  Pallas kernels: 342 us -> 336 us
    pallas_call x1, Pallas kernels: 112 us -> 106 us  [tail(): pl.pallas_call(functools.partial(tail_kernel, table_rows), in_specs=[vmem...]
    unnamed x73 -> x72, local copies, waits for them, and re-layouts: 12.9 us -> 12.1 us
where the time goes in v8:
time: 397 us; the launch traced here: 391 us
  Pallas kernels  336 us (85%)
  matrix products  22.4 us (6%)
  local copies, waits for them, and re-layouts  16 us (4%)
  other arithmetic  8.89 us (2%)
  between operations  6.45 us (2%)
    pallas_call x1, Pallas kernels, head(): pl.pallas_call(functools.partial(head_kernel, vocab_rows, chunks), in_spe...  159 us
    pallas_call x1, Pallas kernels, tail(): pl.pallas_call(functools.partial(tail_kernel, table_rows), in_specs=[vmem...  106 us
    pallas_call x1, Pallas kernels, front(): pl.pallas_call(functools.partial(front_kernel, rows), in_specs=[anywhere,...  70.1 us
    unnamed x72, local copies, waits for them, and re-layouts  12.1 us

profile of v8, /device:TPU:0, one launch (start us, length us, event | category | flops | bytes accessed | tf_op | source)
XLA Modules:
  0.0 391.2 jit_solution(2947756579020785354)
XLA Ops:
  0.6 0.8 stack_reshape.6
  1.4 0.8 stack_reshape.7
  2.8 70.1 %front_all.1 = (s32[16,2,512]{2,1,0:T(2,128)}, bf16[2048,768]{1,0:T(8,128)(2,1)}, bf16[2,2,2,2,48,2048]{5,4,3,2,1,0:T(8,128)(2,1)}, bf16[2,2,2,2,48,2048]{5,4,3,...) custom-call(s32[2,512]{1,0:T(2,128)} %pad_add_fusion.pack_hbm, ...), custom_call_target="tpu_custom_call" | custom-call | flops 6442450944 | bytes 20971520 | tf_op jit(solution)/shard_map/front_all/pallas_call | solution.py:659
  75.4 0.9 copy.16
  77.6 4.0 %convolution_convert_fusion.1 = bf16[512,2048]{1,0:T(8,128)(2,1)S(1)} fusion(bf16[512,768]{1,0:T(8,128)(2,1)S(1)} %fusion.68.u_ref, bf16[768,2048]{1,0:T(8,128)(2,1)} %bitcast.109), kind=kOutput, calls=%fused_computation.105 | convolution fusion | flops 1611661312 | bytes 6029312 | tf_op jit(solution)/shard_map/dot_general | solution.py:29
  81.7 3.6 fusion.48
  85.3 1.9 fusion.60
  88.1 1.1 fusion.62
  90.2 159.3 %head_all.1 = (f32[512,768]{1,0:T(8,128)}, f32[2048,768]{1,0:T(8,128)}, f32[1,128]{1,0:T(1,128)}) custom-call(bf16[8,64,768]{2,1,0:T(8,128)(2,1)} %bitcast.95, bf16[2048,768]{1,0:T(8,128)(2,1)} %get-tuple-element.289.table_ref, s32[16,512]{1,0:T(8,128)} %reshape.148.lab_ref), custom_call_target="tpu_custom_call" | custom-call | flops 77309411328 | bytes 6291456 | tf_op jit(solution)/shard_map/head_all/pallas_call | solution.py:306
  249.5 2.0 fusion.65
  252.2 1.6 copy-done.30
  253.8 5.0 %fusion.57 = (bf16[512,2048]{1,0:T(8,128)(2,1)S(1)}, bf16[512,2048]{1,0:T(8,128)(2,1)S(1)}) fusion(bf16[512,2048]{1,0:T(8,128)(2,1)} %copy-done.33, bf16[512,2048]{1,0:T(8,128)(2,1)} %get-tuple-element.374, bf16[512,768]{1,0:T(8,128)(2,1)S(1)} %fusion.74.mid_ref, bf16[2048,768]{1,0:T(8,128)(2,1)S(1)} %bitcast.112), kind=kOutput, calls=%fused_computation.98 | convolution fusion | flops 1626341376 | bytes 12320768 | tf_op jit(solution)/shard_map/dot_general | solution.py:46
  258.9 1.8 fusion.76
  261.0 1.5 copy-done.27
  262.5 2.0 fusion.73
  264.6 1.1 reduce-precision_convert_fusion.3
  266.0 1.6 pad_maximum_fusion
  267.6 4.0 %fusion.47 = f32[896,768]{1,0:T(8,128)} fusion(s32[1536]{0:T(1024)S(1)} %eq.235, bf16[512,768]{1,0:T(8,128)(2,1)S(1)} %get-tuple-element.368, bf16[512,768]{1,0:T(8,128)(2,1)S(1)} %get-tuple-element.367, bf16[512,768]{1,0:T(8,128)(2,1)S(1)} %get-tuple-element.356), kind=kOutput, calls=%fused_computation.86 | convolution fusion | flops 2122383360 | bytes 5117952 | tf_op jit(solution)/shard_map/dot_general | solution.py:684
  272.3 106.5 %tail_all.1 = (f32[48,2048]{1,0:T(8,128)}, f32[48,2048]{1,0:T(8,128)}, f32[128,768]{1,0:T(8,128)}, f32[2008,768]{1,0:T(8,128)}) custom-call(bf16[512,768]{1,0:T(8,128)(2,1)} %copy-done.8, bf16[512,2048]{1,0:T(8,128)(2,1)} %copy-done.35, bf16[512,768]{1,0:T(8,128)(2,1)} %copy-done.9, bf16[512,2048]{1,0:T(8,128)(2,1)} %copy-done.34, ...), custom_call_target="tpu_custom_call" | custom-call | flops 8290566144 | bytes 41943040 | tf_op jit(solution)/shard_map/tail_all/pallas_call | solution.py:497
  380.1 1.4 while.27
  381.5 5.9 %copy.37 = f32[2008,768]{1,0:T(8,128)} copy(f32[2008,768]{1,0:T(8,128)} %get-tuple-element.549) | data formatting | bytes 12337152
  387.4 0.7 copy.38
  388.2 0.7 copy.39
  388.9 0.7 copy.40
  (84 shorter events, 5.6 us)
Async XLA Ops:
  76.5 5.2 %copy-start.7 = (s32[16,2,512]{2,0,1:T(8,128)}, s32[16,2,512]{2,0,1:T(8,128)S(1)}, u32[]{:S(2)}) copy-start(s32[16,2,512]{2,0,1:T(8,128)S(1)} %get-tuple-element.557) | copy-start | bytes 196612
  76.5 8.8 %copy-start.3 = (bf16[512,768]{1,0:T(8,128)(2,1)}, bf16[512,768]{1,0:T(8,128)(2,1)S(1)}, u32[]{:S(2)}) copy-start(bf16[512,768]{1,0:T(8,128)(2,1)S(1)} %get-tuple-element.285) | copy-start | bytes 2359300
  77.3 4.3 %copy-start.18 = (f32[512]{0:T(512)}, f32[512]{0:T(512)S(1)}, u32[]{:S(2)}) copy-start(f32[512]{0:T(512)S(1)} %get-tuple-element.370) | copy-start | bytes 6148
  77.6 4.1 %copy-start.8 = (bf16[512,768]{1,0:T(8,128)(2,1)}, bf16[512,768]{1,0:T(8,128)(2,1)S(1)}, u32[]{:S(2)}) copy-start(bf16[512,768]{1,0:T(8,128)(2,1)S(1)} %fusion.68.u_ref) | copy-start | bytes 2359300
  77.6 4.1 %copy-start.26 = (bf16[2,2,2,2,48,2048]{5,4,3,2,1,0:T(8,128)(2,1)S(1)}, bf16[2,2,2,2,48,2048]{5,4,3,2,1,0:T(8,128)(2,1)}, u32[]{:S(2)}) copy-start(bf16[2,2,2,2,48,2048]{5,4,3,2,1,0:T(8,128)(2,1)} %get-tuple-element.287) | copy-start | bytes 9437188
  81.7 3.6 copy-start.33
  81.7 3.6 copy-start.29
  85.3 2.8 copy-start.14
  85.3 4.0 %copy-start.13 = (s32[16,2,512]{2,1,0:T(2,128)S(1)}, s32[16,2,512]{2,1,0:T(2,128)}, u32[]{:S(2)}) copy-start(s32[16,2,512]{2,1,0:T(2,128)} %get-tuple-element.324) | copy-start | bytes 196612
  249.5 2.1 copy-start
  249.5 2.3 copy-start.2
  249.5 2.3 copy-start.15
  249.5 2.3 copy-start.17
  249.5 2.3 copy-start.20
  251.6 2.2 copy-start.30
  252.2 6.6 %copy-start.9 = (bf16[512,768]{1,0:T(8,128)(2,1)}, bf16[512,768]{1,0:T(8,128)(2,1)S(1)}, u32[]{:S(2)}) copy-start(bf16[512,768]{1,0:T(8,128)(2,1)S(1)} %fusion.74.mid_ref) | copy-start | bytes 2359300
  253.8 5.1 %copy-start.28 = (bf16[2,2,2,2,48,2048]{5,4,3,2,1,0:T(8,128)(2,1)S(1)}, bf16[2,2,2,2,48,2048]{5,4,3,2,1,0:T(8,128)(2,1)}, u32[]{:S(2)}) copy-start(bf16[2,2,2,2,48,2048]{5,4,3,2,1,0:T(8,128)(2,1)} %get-tuple-element.286) | copy-start | bytes 9437188
  258.9 2.1 copy-start.32
  258.9 2.1 copy-start.4
  258.9 3.6 copy-start.27
  267.6 4.0 %copy-start.22 = (s32[16,64]{1,0:T(8,128)S(1)}, s32[16,64]{1,0:T(8,128)}, u32[]{:S(2)}) copy-start(s32[16,64]{1,0:T(8,128)} %get-tuple-element.293) | copy-start | bytes 12292
  381.5 5.9 %copy-start.12 = (f32[48,2048]{1,0:T(8,128)S(1)}, f32[48,2048]{1,0:T(8,128)}, u32[]{:S(2)}) copy-start(f32[48,2048]{1,0:T(8,128)} %get-tuple-element.550) | copy-start | bytes 1179652
  381.5 6.7 %copy-start.11 = (f32[48,2048]{1,0:T(8,128)S(1)}, f32[48,2048]{1,0:T(8,128)}, u32[]{:S(2)}) copy-start(f32[48,2048]{1,0:T(8,128)} %get-tuple-element.551) | copy-start | bytes 1179652
  381.5 7.4 %copy-start.10 = (f32[128,768]{1,0:T(8,128)S(1)}, f32[128,768]{1,0:T(8,128)}, u32[]{:S(2)}) copy-start(f32[128,768]{1,0:T(8,128)} %get-tuple-element.552) | copy-start | bytes 1179652
  (10 other events, 16.2 us)

commit v9 on v8

--- a/solution.py
+++ b/solution.py
@@ -333,7 +333,7 @@
     )(z_local.reshape(chunks, UNIT, dim), table_padded, lab_rows)
 
 
-PIECES = 4
+PIECES = 8
 
 
 def axes(part):
@@ -344,9 +344,9 @@
     return choice.get(2, slice(None)), choice.get(1, slice(None)), choice.get(0, slice(None))
 
 
-def tail_kernel(table_rows, u_ref, acts_ref, mid_ref, gate_ref, up_ref, send_hbm, row_ref, dtable_hbm, gate_out, up_out, down_out, dtable_out,
+def tail_kernel(table_rows, u_ref, acts_ref, mid_ref, gate_ref, up_ref, send_hbm, row_ref, dtable_hbm, gate_out, up_out, down_out, dtable_hbm_out,
                 all_g, all_u, all_d, core_g, core_u, core_d, one_g, one_u, one_d, two_g, two_u, two_d, three_g, three_u, three_d,
-                rows_got, split, local_sem, send_sem, recv_sem, row_send, row_recv):
+                rows_got, split, dtable_out, local_sem, send_sem, recv_sem, row_send, row_recv):
     me = lax.axis_index('fsdp')
     total = 16
     core = lax.rem(me, 2)
@@ -473,7 +473,10 @@
     if table_rows % VOCAB_TILE:
         add_rows(full * VOCAB_TILE, table_rows % VOCAB_TILE)
 
+    save = pltpu.make_async_copy(dtable_out, dtable_hbm_out, local_sem.at[0])
     for q in range(PIECES + 2):
+        if q == 1:
+            save.start()
         if q < PIECES:
             finish_add(1, q)
             start(copies(2, q))
@@ -482,6 +485,7 @@
             start(copies(3, q - 1))
         if q >= 2:
             finish_add(3, q - 2)
+    save.wait()
 
 
 def tail(normed_in, acts, grad_mid, grad_gate_pre, grad_up_proj, send, row_idx, dtable, table_rows):
@@ -497,9 +501,9 @@
     return pl.pallas_call(
         functools.partial(tail_kernel, table_rows),
         in_specs=[vmem, vmem, vmem, vmem, vmem, anywhere, vmem, anywhere],
-        out_specs=[vmem] * 4,
+        out_specs=[vmem, vmem, vmem, anywhere],
         out_shape=[jax.ShapeDtypeStruct(block, f32) for block in blocks] + [jax.ShapeDtypeStruct((table_rows, dim), f32)],
-        scratch_shapes=scratch + [pltpu.VMEM(send.shape, f32), pltpu.VMEM((3 * slots, dim), jnp.bfloat16),
+        scratch_shapes=scratch + [pltpu.VMEM(send.shape, f32), pltpu.VMEM((3 * slots, dim), jnp.bfloat16), pltpu.VMEM((table_rows, dim), f32),
                                   sems((5,)), sems((4, 3, PIECES)), sems((4, 3, PIECES)), sems((16,)), sems((16,))],
         compiler_params=pltpu.CompilerParams(vmem_limit_bytes=67043328, collective_id=2, has_side_effects=True),
         cost_estimate=pl.CostEstimate(flops=6 * slots * table_rows * dim, bytes_accessed=40 * 1024 * 1024, transcendentals=0),
@@ -508,8 +512,8 @@
 
 
 def front_kernel(table_rows, pack_hbm, table_ref, gate_hbm, up_hbm, down_hbm,
-                 pack_out, table_out, gate_out, up_out, down_out, x_out, slots_out, rows_out, rank_out,
-                 send, got, before_ref, rank_top, local_sem, id_send, id_recv, w_send, w_recv, c_send, c_recv, row_send, row_recv):
+                 pack_out, table_hbm_out, gate_hbm_out, up_hbm_out, down_hbm_out, x_out, slots_out, rows_out, rank_out,
+                 table_out, gate_out, up_out, down_out, send, got, before_ref, rank_top, local_sem, save_sem, id_send, id_recv, w_send, w_recv, c_send, c_recv, row_send, row_recv):
     me = lax.axis_index('fsdp')
     total = 16
     core = lax.rem(me, 2)
@@ -634,17 +638,32 @@
     finish(wide(2))
     start(wide(3))
     start(across(2))
+    saves = [pltpu.make_async_copy(table_out, table_hbm_out, save_sem.at[9])]
+    saves[0].start()
+    results = (gate_hbm_out, up_hbm_out, down_hbm_out)
+
+    def save(mine, which, sem):
+        for part in range(3):
+            axis = axes(part)[2]
+            index = cube_index({axis: pos[axis] if mine else 1 - pos[axis]}) + (which,)
+            saves.append(pltpu.make_async_copy(outs[part].at[index], results[part].at[index], save_sem.at[sem * 3 + part]))
+            saves[-1].start()
+
+    for stage in range(3):
+        finish(across(stage))
+    save(True, slice(None), 0)
     own_rows.wait()
     finish([row_copy(step) for step in range(1, total)])
     place = lax.broadcasted_iota(jnp.int32, (total * SLOTS, tokens), 0) == slots_out[...]
     x_out[...] = lax.dot_general(jnp.where(place, 1.0, 0.0).astype(jnp.bfloat16), got[...].reshape(total * SLOTS, dim), ROWS_DIMS,
                                  preferred_element_type=jnp.float32).astype(jnp.bfloat16)
-    finish(across(0))
-    finish(across(1))
     finish(wide(3))
     start(across(3))
-    finish(across(2))
+    save(False, core, 1)
     finish(across(3))
+    save(False, 1 - core, 2)
+    for copy in saves:
+        copy.wait()
 
 
 def front(packed, table_shard, gate_shard, up_shard, down_shard):
@@ -659,13 +678,14 @@
     return pl.pallas_call(
         functools.partial(front_kernel, rows),
         in_specs=[anywhere, vmem, anywhere, anywhere, anywhere],
-        out_specs=[vmem] * 9,
+        out_specs=[vmem] + [anywhere] * 4 + [vmem] * 4,
         out_shape=[jax.ShapeDtypeStruct((16,) + packed.shape, jnp.int32), jax.ShapeDtypeStruct((padded, dim), bf16)]
         + [jax.ShapeDtypeStruct((2, 2, 2, 2) + shard.shape, bf16) for shard in shards]
         + [jax.ShapeDtypeStruct((tokens, dim), bf16), jax.ShapeDtypeStruct((1, tokens), jnp.int32),
            jax.ShapeDtypeStruct((16, SLOTS), jnp.int32), jax.ShapeDtypeStruct((1, 128), jnp.int32)],
-        scratch_shapes=[pltpu.VMEM((16, SLOTS, dim), bf16), pltpu.VMEM((16, SLOTS, dim), bf16), pltpu.VMEM((tokens, tokens), bf16), pltpu.VMEM((1, tokens), jnp.float32),
-                        sems((5,)), sems((16,)), sems((16,)), sems((4, 3)), sems((4, 3)), sems((4, 3)), sems((4, 3)), sems((16,)), sems((16,))],
+        scratch_shapes=[pltpu.VMEM((padded, dim), bf16)] + [pltpu.VMEM((2, 2, 2, 2) + shard.shape, bf16) for shard in shards]
+        + [pltpu.VMEM((16, SLOTS, dim), bf16), pltpu.VMEM((16, SLOTS, dim), bf16), pltpu.VMEM((tokens, tokens), bf16), pltpu.VMEM((1, tokens), jnp.float32),
+           sems((5,)), sems((10,)), sems((16,)), sems((16,)), sems((4, 3)), sems((4, 3)), sems((4, 3)), sems((4, 3)), sems((16,)), sems((16,))],
         compiler_params=pltpu.CompilerParams(vmem_limit_bytes=60 * 1024 * 1024, collective_id=3, has_side_effects=True),
         cost_estimate=pl.CostEstimate(flops=4 * 16 * SLOTS * padded * dim, bytes_accessed=20 * 1024 * 1024, transcendentals=0),
         name="front_all",

time: 397 us -> 396 us (level)
  no operation moved by 1% of the time
where the time goes in v9:
time: 396 us; the launch traced here: 390 us
  Pallas kernels  335 us (85%)
  matrix products  22.4 us (6%)
  local copies, waits for them, and re-layouts  16.6 us (4%)
  other arithmetic  8.89 us (2%)
  between operations  6.39 us (2%)
    pallas_call x1, Pallas kernels, head(): pl.pallas_call(functools.partial(head_kernel, vocab_rows, chunks), in_spe...  159 us
    pallas_call x1, Pallas kernels, tail(): pl.pallas_call(functools.partial(tail_kernel, table_rows), in_specs=[vmem...  108 us
    pallas_call x1, Pallas kernels, front(): pl.pallas_call(functools.partial(front_kernel, rows), in_specs=[anywhere,...  67.7 us
    unnamed x72, local copies, waits for them, and re-layouts  12.7 us

profile of v9, /device:TPU:0, one launch (start us, length us, event | category | flops | bytes accessed | tf_op | source)
XLA Modules:
  0.0 389.7 jit_solution(6038389097591120924)
XLA Ops:
  0.6 0.8 stack_reshape.6
  1.4 0.8 stack_reshape.7
  2.8 67.7 %front_all.1 = (s32[16,2,512]{2,1,0:T(2,128)}, bf16[2048,768]{1,0:T(8,128)(2,1)}, bf16[2,2,2,2,48,2048]{5,4,3,2,1,0:T(8,128)(2,1)}, bf16[2,2,2,2,48,2048]{5,4,3,...) custom-call(s32[2,512]{1,0:T(2,128)} %pad_add_fusion.pack_hbm, ...), custom_call_target="tpu_custom_call" | custom-call | flops 6442450944 | bytes 20971520 | tf_op jit(solution)/shard_map/front_all/pallas_call | solution.py:678
  73.0 0.9 copy.16
  75.2 4.0 %convolution_convert_fusion.1 = bf16[512,2048]{1,0:T(8,128)(2,1)S(1)} fusion(bf16[512,768]{1,0:T(8,128)(2,1)S(1)} %fusion.68.u_ref, bf16[768,2048]{1,0:T(8,128)(2,1)} %bitcast.109), kind=kOutput, calls=%fused_computation.105 | convolution fusion | flops 1611661312 | bytes 6029312 | tf_op jit(solution)/shard_map/dot_general | solution.py:29
  79.3 3.6 fusion.48
  82.9 1.9 fusion.60
  85.7 1.1 fusion.62
  87.0 0.7 reshape.148.lab_ref
  87.7 159.3 %head_all.1 = (f32[512,768]{1,0:T(8,128)}, f32[2048,768]{1,0:T(8,128)}, f32[1,128]{1,0:T(1,128)}) custom-call(bf16[8,64,768]{2,1,0:T(8,128)(2,1)} %bitcast.95, bf16[2048,768]{1,0:T(8,128)(2,1)} %get-tuple-element.289.table_ref, s32[16,512]{1,0:T(8,128)} %reshape.148.lab_ref), custom_call_target="tpu_custom_call" | custom-call | flops 77309411328 | bytes 6291456 | tf_op jit(solution)/shard_map/head_all/pallas_call | solution.py:306
  247.1 2.0 fusion.65
  249.8 1.6 copy-done.30
  251.4 5.0 %fusion.57 = (bf16[512,2048]{1,0:T(8,128)(2,1)S(1)}, bf16[512,2048]{1,0:T(8,128)(2,1)S(1)}) fusion(bf16[512,2048]{1,0:T(8,128)(2,1)} %copy-done.33, bf16[512,2048]{1,0:T(8,128)(2,1)} %get-tuple-element.374, bf16[512,768]{1,0:T(8,128)(2,1)S(1)} %fusion.74.mid_ref, bf16[2048,768]{1,0:T(8,128)(2,1)S(1)} %bitcast.112), kind=kOutput, calls=%fused_computation.98 | convolution fusion | flops 1626341376 | bytes 12320768 | tf_op jit(solution)/shard_map/dot_general | solution.py:46
  256.5 1.8 fusion.76
  258.6 1.5 copy-done.27
  260.1 2.0 fusion.73
  262.1 1.1 reduce-precision_convert_fusion.3
  263.6 1.6 pad_maximum_fusion
  265.2 4.0 %fusion.47 = f32[896,768]{1,0:T(8,128)} fusion(s32[1536]{0:T(1024)S(1)} %eq.235, bf16[512,768]{1,0:T(8,128)(2,1)S(1)} %get-tuple-element.368, bf16[512,768]{1,0:T(8,128)(2,1)S(1)} %get-tuple-element.367, bf16[512,768]{1,0:T(8,128)(2,1)S(1)} %get-tuple-element.356), kind=kOutput, calls=%fused_computation.86 | convolution fusion | flops 2122383360 | bytes 5117952 | tf_op jit(solution)/shard_map/dot_general | solution.py:704
  269.9 108.2 %tail_all.1 = (f32[48,2048]{1,0:T(8,128)}, f32[48,2048]{1,0:T(8,128)}, f32[128,768]{1,0:T(8,128)}, f32[2008,768]{1,0:T(8,128)}) custom-call(bf16[512,768]{1,0:T(8,128)(2,1)} %copy-done.8, bf16[512,2048]{1,0:T(8,128)(2,1)} %copy-done.35, bf16[512,768]{1,0:T(8,128)(2,1)} %copy-done.9, bf16[512,2048]{1,0:T(8,128)(2,1)} %copy-done.34, ...), custom_call_target="tpu_custom_call" | custom-call | flops 8290566144 | bytes 41943040 | tf_op jit(solution)/shard_map/tail_all/pallas_call | solution.py:501
  380.1 5.9 %copy.37 = f32[2008,768]{1,0:T(8,128)} copy(f32[2008,768]{1,0:T(8,128)} %get-tuple-element.549) | data formatting | bytes 12337152
  386.0 0.7 copy.38
  386.7 0.7 copy.39
  387.5 0.7 copy.40
  (84 shorter events, 5.5 us)
Async XLA Ops:
  74.1 5.2 %copy-start.7 = (s32[16,2,512]{2,0,1:T(8,128)}, s32[16,2,512]{2,0,1:T(8,128)S(1)}, u32[]{:S(2)}) copy-start(s32[16,2,512]{2,0,1:T(8,128)S(1)} %get-tuple-element.557) | copy-start | bytes 196612
  74.1 8.8 %copy-start.3 = (bf16[512,768]{1,0:T(8,128)(2,1)}, bf16[512,768]{1,0:T(8,128)(2,1)S(1)}, u32[]{:S(2)}) copy-start(bf16[512,768]{1,0:T(8,128)(2,1)S(1)} %get-tuple-element.285) | copy-start | bytes 2359300
  74.9 4.3 %copy-start.18 = (f32[512]{0:T(512)}, f32[512]{0:T(512)S(1)}, u32[]{:S(2)}) copy-start(f32[512]{0:T(512)S(1)} %get-tuple-element.370) | copy-start | bytes 6148
  75.2 4.1 %copy-start.8 = (bf16[512,768]{1,0:T(8,128)(2,1)}, bf16[512,768]{1,0:T(8,128)(2,1)S(1)}, u32[]{:S(2)}) copy-start(bf16[512,768]{1,0:T(8,128)(2,1)S(1)} %fusion.68.u_ref) | copy-start | bytes 2359300
  75.2 4.1 %copy-start.26 = (bf16[2,2,2,2,48,2048]{5,4,3,2,1,0:T(8,128)(2,1)S(1)}, bf16[2,2,2,2,48,2048]{5,4,3,2,1,0:T(8,128)(2,1)}, u32[]{:S(2)}) copy-start(bf16[2,2,2,2,48,2048]{5,4,3,2,1,0:T(8,128)(2,1)} %get-tuple-element.287) | copy-start | bytes 9437188
  79.2 3.6 copy-start.33
  79.3 3.6 copy-start.29
  82.9 2.8 copy-start.14
  82.9 4.0 %copy-start.13 = (s32[16,2,512]{2,1,0:T(2,128)S(1)}, s32[16,2,512]{2,1,0:T(2,128)}, u32[]{:S(2)}) copy-start(s32[16,2,512]{2,1,0:T(2,128)} %get-tuple-element.324) | copy-start | bytes 196612
  247.1 2.1 copy-start
  247.1 2.3 copy-start.2
  247.1 2.3 copy-start.15
  247.1 2.3 copy-start.17
  247.1 2.3 copy-start.20
  249.2 2.2 copy-start.30
  249.8 6.6 %copy-start.9 = (bf16[512,768]{1,0:T(8,128)(2,1)}, bf16[512,768]{1,0:T(8,128)(2,1)S(1)}, u32[]{:S(2)}) copy-start(bf16[512,768]{1,0:T(8,128)(2,1)S(1)} %fusion.74.mid_ref) | copy-start | bytes 2359300
  251.4 5.1 %copy-start.28 = (bf16[2,2,2,2,48,2048]{5,4,3,2,1,0:T(8,128)(2,1)S(1)}, bf16[2,2,2,2,48,2048]{5,4,3,2,1,0:T(8,128)(2,1)}, u32[]{:S(2)}) copy-start(bf16[2,2,2,2,48,2048]{5,4,3,2,1,0:T(8,128)(2,1)} %get-tuple-element.286) | copy-start | bytes 9437188
  256.5 2.1 copy-start.32
  256.5 2.1 copy-start.4
  256.5 3.6 copy-start.27
  265.2 4.0 %copy-start.22 = (s32[16,64]{1,0:T(8,128)S(1)}, s32[16,64]{1,0:T(8,128)}, u32[]{:S(2)}) copy-start(s32[16,64]{1,0:T(8,128)} %get-tuple-element.293) | copy-start | bytes 12292
  380.0 5.9 %copy-start.12 = (f32[48,2048]{1,0:T(8,128)S(1)}, f32[48,2048]{1,0:T(8,128)}, u32[]{:S(2)}) copy-start(f32[48,2048]{1,0:T(8,128)} %get-tuple-element.550) | copy-start | bytes 1179652
  380.1 6.7 %copy-start.11 = (f32[48,2048]{1,0:T(8,128)S(1)}, f32[48,2048]{1,0:T(8,128)}, u32[]{:S(2)}) copy-start(f32[48,2048]{1,0:T(8,128)} %get-tuple-element.551) | copy-start | bytes 1179652
  380.1 7.4 %copy-start.10 = (f32[128,768]{1,0:T(8,128)S(1)}, f32[128,768]{1,0:T(8,128)}, u32[]{:S(2)}) copy-start(f32[128,768]{1,0:T(8,128)} %get-tuple-element.552) | copy-start | bytes 1179652
  (10 other events, 15.5 us)

commit v10 on v9

--- a/solution.py
+++ b/solution.py
@@ -333,7 +333,7 @@
     )(z_local.reshape(chunks, UNIT, dim), table_padded, lab_rows)
 
 
-PIECES = 8
+PIECES = 4
 
 
 def axes(part):

time: 396 us -> 393 us (level)
  no operation moved by 1% of the time
where the time goes in v10:
time: 393 us; the launch traced here: 387 us
  Pallas kernels  332 us (84%)
  matrix products  22.4 us (6%)
  local copies, waits for them, and re-layouts  16 us (4%)
  other arithmetic  8.89 us (2%)
  between operations  6.45 us (2%)
    pallas_call x1, Pallas kernels, head(): pl.pallas_call(functools.partial(head_kernel, vocab_rows, chunks), in_spe...  159 us
    pallas_call x1, Pallas kernels, tail(): pl.pallas_call(functools.partial(tail_kernel, table_rows), in_specs=[vmem...  105 us
    pallas_call x1, Pallas kernels, front(): pl.pallas_call(functools.partial(front_kernel, rows), in_specs=[anywhere,...  67.7 us
    unnamed x72, local copies, waits for them, and re-layouts  12.1 us

profile of v10, /device:TPU:0, one launch (start us, length us, event | category | flops | bytes accessed | tf_op | source)
XLA Modules:
  0.0 386.9 jit_solution(16546918430023569611)
XLA Ops:
  0.6 0.8 stack_reshape.6
  1.4 0.8 stack_reshape.7
  2.8 67.7 %front_all.1 = (s32[16,2,512]{2,1,0:T(2,128)}, bf16[2048,768]{1,0:T(8,128)(2,1)}, bf16[2,2,2,2,48,2048]{5,4,3,2,1,0:T(8,128)(2,1)}, bf16[2,2,2,2,48,2048]{5,4,3,...) custom-call(s32[2,512]{1,0:T(2,128)} %pad_add_fusion.pack_hbm, ...), custom_call_target="tpu_custom_call" | custom-call | flops 6442450944 | bytes 20971520 | tf_op jit(solution)/shard_map/front_all/pallas_call | solution.py:678
  73.0 0.9 copy.16
  75.2 4.0 %convolution_convert_fusion.1 = bf16[512,2048]{1,0:T(8,128)(2,1)S(1)} fusion(bf16[512,768]{1,0:T(8,128)(2,1)S(1)} %fusion.68.u_ref, bf16[768,2048]{1,0:T(8,128)(2,1)} %bitcast.109), kind=kOutput, calls=%fused_computation.105 | convolution fusion | flops 1611661312 | bytes 6029312 | tf_op jit(solution)/shard_map/dot_general | solution.py:29
  79.3 3.6 fusion.48
  82.9 1.9 fusion.60
  85.7 1.1 fusion.62
  87.7 159.3 %head_all.1 = (f32[512,768]{1,0:T(8,128)}, f32[2048,768]{1,0:T(8,128)}, f32[1,128]{1,0:T(1,128)}) custom-call(bf16[8,64,768]{2,1,0:T(8,128)(2,1)} %bitcast.95, bf16[2048,768]{1,0:T(8,128)(2,1)} %get-tuple-element.289.table_ref, s32[16,512]{1,0:T(8,128)} %reshape.148.lab_ref), custom_call_target="tpu_custom_call" | custom-call | flops 77309411328 | bytes 6291456 | tf_op jit(solution)/shard_map/head_all/pallas_call | solution.py:306
  247.1 2.0 fusion.65
  249.8 1.6 copy-done.30
  251.4 5.0 %fusion.57 = (bf16[512,2048]{1,0:T(8,128)(2,1)S(1)}, bf16[512,2048]{1,0:T(8,128)(2,1)S(1)}) fusion(bf16[512,2048]{1,0:T(8,128)(2,1)} %copy-done.33, bf16[512,2048]{1,0:T(8,128)(2,1)} %get-tuple-element.374, bf16[512,768]{1,0:T(8,128)(2,1)S(1)} %fusion.74.mid_ref, bf16[2048,768]{1,0:T(8,128)(2,1)S(1)} %bitcast.112), kind=kOutput, calls=%fused_computation.98 | convolution fusion | flops 1626341376 | bytes 12320768 | tf_op jit(solution)/shard_map/dot_general | solution.py:46
  256.5 1.8 fusion.76
  258.6 1.5 copy-done.27
  260.1 2.0 fusion.73
  262.1 1.1 reduce-precision_convert_fusion.3
  263.6 1.6 pad_maximum_fusion
  265.2 4.0 %fusion.47 = f32[896,768]{1,0:T(8,128)} fusion(s32[1536]{0:T(1024)S(1)} %eq.235, bf16[512,768]{1,0:T(8,128)(2,1)S(1)} %get-tuple-element.368, bf16[512,768]{1,0:T(8,128)(2,1)S(1)} %get-tuple-element.367, bf16[512,768]{1,0:T(8,128)(2,1)S(1)} %get-tuple-element.356), kind=kOutput, calls=%fused_computation.86 | convolution fusion | flops 2122383360 | bytes 5117952 | tf_op jit(solution)/shard_map/dot_general | solution.py:704
  269.9 104.5 %tail_all.1 = (f32[48,2048]{1,0:T(8,128)}, f32[48,2048]{1,0:T(8,128)}, f32[128,768]{1,0:T(8,128)}, f32[2008,768]{1,0:T(8,128)}) custom-call(bf16[512,768]{1,0:T(8,128)(2,1)} %copy-done.8, bf16[512,2048]{1,0:T(8,128)(2,1)} %copy-done.35, bf16[512,768]{1,0:T(8,128)(2,1)} %copy-done.9, bf16[512,2048]{1,0:T(8,128)(2,1)} %copy-done.34, ...), custom_call_target="tpu_custom_call" | custom-call | flops 8290566144 | bytes 41943040 | tf_op jit(solution)/shard_map/tail_all/pallas_call | solution.py:501
  375.7 1.4 while.27
  377.2 5.9 %copy.37 = f32[2008,768]{1,0:T(8,128)} copy(f32[2008,768]{1,0:T(8,128)} %get-tuple-element.549) | data formatting | bytes 12337152
  383.1 0.7 copy.38
  383.8 0.7 copy.39
  384.6 0.7 copy.40
  (84 shorter events, 5.6 us)
Async XLA Ops:
  74.1 5.2 %copy-start.7 = (s32[16,2,512]{2,0,1:T(8,128)}, s32[16,2,512]{2,0,1:T(8,128)S(1)}, u32[]{:S(2)}) copy-start(s32[16,2,512]{2,0,1:T(8,128)S(1)} %get-tuple-element.557) | copy-start | bytes 196612
  74.1 8.8 %copy-start.3 = (bf16[512,768]{1,0:T(8,128)(2,1)}, bf16[512,768]{1,0:T(8,128)(2,1)S(1)}, u32[]{:S(2)}) copy-start(bf16[512,768]{1,0:T(8,128)(2,1)S(1)} %get-tuple-element.285) | copy-start | bytes 2359300
  74.9 4.3 %copy-start.18 = (f32[512]{0:T(512)}, f32[512]{0:T(512)S(1)}, u32[]{:S(2)}) copy-start(f32[512]{0:T(512)S(1)} %get-tuple-element.370) | copy-start | bytes 6148
  75.2 4.1 %copy-start.8 = (bf16[512,768]{1,0:T(8,128)(2,1)}, bf16[512,768]{1,0:T(8,128)(2,1)S(1)}, u32[]{:S(2)}) copy-start(bf16[512,768]{1,0:T(8,128)(2,1)S(1)} %fusion.68.u_ref) | copy-start | bytes 2359300
  75.2 4.1 %copy-start.26 = (bf16[2,2,2,2,48,2048]{5,4,3,2,1,0:T(8,128)(2,1)S(1)}, bf16[2,2,2,2,48,2048]{5,4,3,2,1,0:T(8,128)(2,1)}, u32[]{:S(2)}) copy-start(bf16[2,2,2,2,48,2048]{5,4,3,2,1,0:T(8,128)(2,1)} %get-tuple-element.287) | copy-start | bytes 9437188
  79.2 3.6 copy-start.33
  79.3 3.6 copy-start.29
  82.9 2.8 copy-start.14
  82.9 4.0 %copy-start.13 = (s32[16,2,512]{2,1,0:T(2,128)S(1)}, s32[16,2,512]{2,1,0:T(2,128)}, u32[]{:S(2)}) copy-start(s32[16,2,512]{2,1,0:T(2,128)} %get-tuple-element.324) | copy-start | bytes 196612
  247.1 2.1 copy-start
  247.1 2.3 copy-start.2
  247.1 2.3 copy-start.15
  247.1 2.3 copy-start.17
  247.1 2.3 copy-start.20
  249.2 2.2 copy-start.30
  249.8 6.6 %copy-start.9 = (bf16[512,768]{1,0:T(8,128)(2,1)}, bf16[512,768]{1,0:T(8,128)(2,1)S(1)}, u32[]{:S(2)}) copy-start(bf16[512,768]{1,0:T(8,128)(2,1)S(1)} %fusion.74.mid_ref) | copy-start | bytes 2359300
  251.4 5.1 %copy-start.28 = (bf16[2,2,2,2,48,2048]{5,4,3,2,1,0:T(8,128)(2,1)S(1)}, bf16[2,2,2,2,48,2048]{5,4,3,2,1,0:T(8,128)(2,1)}, u32[]{:S(2)}) copy-start(bf16[2,2,2,2,48,2048]{5,4,3,2,1,0:T(8,128)(2,1)} %get-tuple-element.286) | copy-start | bytes 9437188
  256.5 2.1 copy-start.32
  256.5 2.1 copy-start.4
  256.5 3.6 copy-start.27
  265.2 4.0 %copy-start.22 = (s32[16,64]{1,0:T(8,128)S(1)}, s32[16,64]{1,0:T(8,128)}, u32[]{:S(2)}) copy-start(s32[16,64]{1,0:T(8,128)} %get-tuple-element.293) | copy-start | bytes 12292
  377.1 5.9 %copy-start.12 = (f32[48,2048]{1,0:T(8,128)S(1)}, f32[48,2048]{1,0:T(8,128)}, u32[]{:S(2)}) copy-start(f32[48,2048]{1,0:T(8,128)} %get-tuple-element.550) | copy-start | bytes 1179652
  377.1 6.7 %copy-start.11 = (f32[48,2048]{1,0:T(8,128)S(1)}, f32[48,2048]{1,0:T(8,128)}, u32[]{:S(2)}) copy-start(f32[48,2048]{1,0:T(8,128)} %get-tuple-element.551) | copy-start | bytes 1179652
  377.1 7.4 %copy-start.10 = (f32[128,768]{1,0:T(8,128)S(1)}, f32[128,768]{1,0:T(8,128)}, u32[]{:S(2)}) copy-start(f32[128,768]{1,0:T(8,128)} %get-tuple-element.552) | copy-start | bytes 1179652
  (10 other events, 16.2 us)
